TPU v7x, 32 devices: a whole 2x2x4 slice. The times are simulated.
32 devices in a mesh: query: 2 (over y), ctx: 16 (over z, x, core).
Axes of the slice: x: 2, y: 2, z: 4, core: 2. Of those that a mesh axis runs over, the one named last changes fastest.
Arguments:
- query_states: bfloat16 [64, 3072], P('query'), may hold values from -370 to 370
- key_states: bfloat16 [16384, 3072], P('ctx', 'query'), may hold values from -10.5 to 10.5
- value_states: bfloat16 [16384, 3072], P('ctx', 'query'), may hold values from -6 to 6
- level_ids: int32 [16384], P('ctx'), may hold values from 0 to 4, as said below
- level_bias: float32 [5, 24], replicated, may hold values from -1.5 to 1.5
- live_counts: int32 [16], P('ctx'), may hold values from 256 to 1024, as said below
- out_grad: bfloat16 [64, 3072], P('query'), may hold values from -6 to 6
Outputs:
- attn_out: bfloat16 [64, 3072], P(('query', 'ctx'))
- query_grad: bfloat16 [64, 3072], P(('query', 'ctx'))
- key_grad: bfloat16 [16384, 3072], P('ctx', 'query')
- value_grad: bfloat16 [16384, 3072], P('ctx', 'query')
Inputs may be any that keep to these rules, and one draw needn't show every extreme that they name: Owner c's slots c * 1024 to c * 1024 + live_counts[c] - 1 are live, its other slots are empty; at least one owner has all 1024 slots live. `level_ids`: constant over each aligned run of 16 slots.
All inputs are finite; a program needn't handle non-finite values.
Results may differ from a plain program's by a relative error of at most 0.012.
Values may be sent and summed in bfloat16 or wider, within the bound.
No kernel may reach another device: no remote copies, remote signals or barrier semaphores. Data moves between devices by JAX's collectives and lax.ppermute only.
A program may use at most 64 MiB of HBM per device.

v0:
```python
import math

import jax
import jax.numpy as jnp
from jax import lax
from jax.sharding import PartitionSpec as P


def combined_all(x, axis, combine):
    everything = jax.tree.map(lambda part: lax.all_gather(part, axis), x)
    initial = jax.tree.map(lambda part: part[0], everything)

    def hop(k, so_far):
        return combine(so_far, jax.tree.map(lambda part: part[k], everything))

    return lax.fori_loop(1, lax.axis_size(axis), hop, initial)


def rescale(outputs, factor):
    row_count = outputs.shape[0]
    head_count = factor.shape[0]
    return (outputs.reshape(row_count, head_count, -1) * factor.T[:, :, None]).reshape(
        row_count, -1
    )


def combine_parts(first, second):
    first_max, first_sum, first_out = first
    second_max, second_sum, second_out = second
    joint_max = jnp.maximum(first_max, second_max)
    first_factor = jnp.exp(first_max - joint_max)
    second_factor = jnp.exp(second_max - joint_max)
    joint_sum = first_sum * first_factor + second_sum * second_factor
    joint_out = rescale(first_out, first_factor) + rescale(second_out, second_factor)
    return (joint_max, joint_sum, joint_out)


def local(query_states, key_states, value_states, level_ids, level_bias, live_counts, out_grad):
    query_ways = lax.axis_size("query")
    owner_ways = lax.axis_size("ctx")
    level_count, head_total = level_bias.shape
    moved_queries, moved_grads = (
        lax.all_to_all(query_states, "query", split_axis=1, concat_axis=0, tiled=True),
        lax.all_to_all(out_grad, "query", split_axis=1, concat_axis=0, tiled=True),
    )
    rows_total = moved_queries.shape[0]
    part_rows = rows_total // query_ways // owner_ways

    def regroup(array):
        return jnp.transpose(
            array.reshape(query_ways, owner_ways, part_rows, -1), (1, 0, 2, 3)
        ).reshape(rows_total, -1)

    queries_in = regroup(moved_queries)
    grads_in = regroup(moved_grads)
    key_full, value_full = (key_states, value_states)
    head_count = head_total // query_ways
    bias_table = lax.dynamic_slice_in_dim(
        level_bias, lax.axis_index("query") * head_count, head_count, 1
    )
    query_count, feature_count = queries_in.shape
    slot_count = key_full.shape[0]
    head_size = feature_count // head_count
    softmax_scale = 1.0 / math.sqrt(head_size)
    queries = queries_in.reshape(query_count, head_count, head_size)
    key_heads = key_full.reshape(slot_count, head_count, head_size)
    value_heads = value_full.reshape(slot_count, head_count, head_size)
    grad_heads = grads_in.reshape(query_count, head_count, head_size)
    live_slots = lax.broadcasted_iota(jnp.int32, (slot_count,), 0) < live_counts[0]
    level_onehot = (
        level_ids[:, None] == lax.broadcasted_iota(jnp.int32, (1, level_count), 1)
    ).astype(jnp.float32)
    level_term = jnp.dot(
        level_onehot,
        bias_table,
        precision=lax.Precision.HIGHEST,
        preferred_element_type=jnp.float32,
    )
    scores = (
        jnp.einsum("qhd,khd->hqk", queries, key_heads, preferred_element_type=jnp.float32)
        * softmax_scale
    )
    scores = jnp.where(live_slots[None, None, :], scores + level_term.T[:, None, :], -1e30)
    local_max = jnp.max(scores, axis=2)
    raw_weights = jnp.exp(scores - local_max[..., None])
    local_sum = jnp.sum(raw_weights, axis=2)
    partial_value = jnp.einsum(
        "hqk,khd->qhd",
        raw_weights.astype(jnp.bfloat16),
        value_heads,
        preferred_element_type=jnp.float32,
    ).reshape(query_count, feature_count)
    row_count = query_count // owner_ways
    row_start = lax.axis_index("ctx") * row_count
    total_max, total_sum, total_out = combined_all(
        (local_max, local_sum, partial_value), "ctx", combine_parts
    )
    attention = total_out.reshape(query_count, head_count, head_size) / total_sum.T[:, :, None]
    log_total = total_max + jnp.log(total_sum)
    deltas = jnp.sum(grad_heads * attention, axis=2).T
    attn_rows = lax.dynamic_slice_in_dim(
        attention.reshape(query_count, feature_count), row_start, row_count, 0
    ).astype(jnp.bfloat16)
    probabilities = jnp.exp(scores - log_total[..., None])
    dprobs = jnp.einsum("qhd,khd->hqk", grad_heads, value_heads, preferred_element_type=jnp.float32)
    dscores = (probabilities * (dprobs - deltas[..., None])).astype(jnp.bfloat16)
    prob_rounded = probabilities.astype(jnp.bfloat16)
    query_part = softmax_scale * jnp.einsum(
        "hqk,khd->qhd", dscores, key_heads, preferred_element_type=jnp.float32
    ).reshape(query_count, feature_count)
    query_rows = lax.psum_scatter(query_part, "ctx", scatter_dimension=0, tiled=True).astype(
        jnp.bfloat16
    )
    block_shape = (head_count, owner_ways, query_ways, part_rows, slot_count)
    row_shape = (owner_ways, query_ways, part_rows, head_count, head_size)
    key_blocks = softmax_scale * jnp.einsum(
        "hcbrk,cbrhd->bkhd",
        dscores.reshape(block_shape),
        queries.reshape(row_shape),
        preferred_element_type=jnp.float32,
    )
    value_blocks = jnp.einsum(
        "hcbrk,cbrhd->bkhd",
        prob_rounded.reshape(block_shape),
        grad_heads.reshape(row_shape),
        preferred_element_type=jnp.float32,
    )
    key_cols = jnp.sum(key_blocks.astype(jnp.bfloat16).astype(jnp.float32), axis=0).reshape(
        slot_count, feature_count
    )
    value_cols = jnp.sum(value_blocks.astype(jnp.bfloat16).astype(jnp.float32), axis=0).reshape(
        slot_count, feature_count
    )
    attn_final, query_final = (
        lax.all_to_all(attn_rows, "query", split_axis=0, concat_axis=1, tiled=True),
        lax.all_to_all(query_rows, "query", split_axis=0, concat_axis=1, tiled=True),
    )
    return (attn_final, query_final, key_cols.astype(jnp.bfloat16), value_cols.astype(jnp.bfloat16))


def solution(mesh):
    placed = (
        P("query", None),
        P("ctx", "query"),
        P("ctx", "query"),
        P("ctx"),
        P(),
        P("ctx"),
        P("query", None),
    )
    return jax.shard_map(
        local,
        mesh=mesh,
        in_specs=placed,
        out_specs=(
            P(("query", "ctx"), None),
            P(("query", "ctx"), None),
            P("ctx", "query"),
            P("ctx", "query"),
        ),
        check_vma=False,
    )
```

profile of v0, /device:TPU:0, one launch (start us, length us, event | category | flops | bytes accessed | tf_op | source)
XLA Modules:
  0.0 373.6 jit_solution(4573565596319728397)
XLA Ops:
  7.2 1.6 copy.169
  8.8 4.3 %all-to-all-start = ((bf16[32,2,1536]{2,0,1:T(8,128)(2,1)}), bf16[32,2,1536]{2,0,1:T(8,128)(2,1)S(1)}, u32[]{:S(2)}, u32[]{:S(2)}) async-start(bf16[32,2,1536]{2,0,1:T(8,128)(2,1)} %bitcast.102), calls=%async_computation | async-start | bytes 393216 | tf_op jit(solution)/shard_map/all_to_all | solution.py:43
  13.1 4.8 %copy.98 = bf16[1024,1536]{0,1:T(8,128)(2,1)} copy(bf16[1024,1536]{1,0:T(8,128)(2,1)} %param.10) | data formatting | bytes 6291456 | tf_op args[1]
  18.5 2.9 copy.101
  23.7 3.0 fusion.29
  29.1 1.9 all_gather_reshape.3
  31.7 3.5 all-to-all-start.2
  37.3 3.1 all-to-all-done.2
  41.6 22.6 %all-gather.2 = f32[16,12,64]{2,1,0:T(8,128)S(1)} all-gather(f32[1,12,64]{2,1,0:T(8,128)S(1)} %bitcast.144), channel_id=2, replica_groups=mesh['query'=2,'ctx'=16] {'ctx'}, dimensions={0}, use_global_device_ids=true | all-gather | bytes 52224 | tf_op jit(solution)/shard_map/all_gather | solution.py:10
  66.1 18.9 %all-gather.3 = f32[16,12,64]{2,1,0:T(8,128)S(1)} all-gather(f32[1,12,64]{2,1,0:T(8,128)S(1)} %bitcast.148), channel_id=3, replica_groups=mesh['query'=2,'ctx'=16] {'ctx'}, dimensions={0}, use_global_device_ids=true | all-gather | bytes 52224 | tf_op jit(solution)/shard_map/all_gather | solution.py:10
  87.2 9.3 %all-gather.6.cloned.1.call-done = f32[16,64,1536]{2,1,0:T(8,128)} async-done(((f32[1,64,1536]{2,1,0:T(8,128)}), f32[16,64,1536]{2,1,0:T(8,128)}) %all-gather.6.cloned.1.call-update) | async-done | bytes 6291472 | tf_op jit(solution)/shard_map/all_gather | solution.py:10
  97.6 153.3 %while.19 = (s32[]{:T(128)}, f32[12,64]{0,1:T(8,128)}, f32[12,64]{0,1:T(8,128)}, f32[64,1536]{1,0:T(8,128)S(1)}, f32[16,12,64]{2,1,0:T(8,128)}, /*index=5*/f32[1...) while((s32[]{:T(128)}, f32[12,64]{0,1:T(8,128)}, f32[12,64]{0,1:T(8,128)}, ...), condition=%wide.region_3.4_spmd, body=%wide.region_2.3_spmd.sunk | while | flops 300293 | bytes 2823319 | solution.py:16
  102.4 1.4 fusion.39
  106.4 1.4 fusion.40
  112.6 1.4 fusion.39
  116.6 1.4 fusion.40
  122.8 1.4 fusion.39
  126.8 1.4 fusion.40
  133.1 1.4 fusion.39
  137.0 1.4 fusion.40
  143.3 1.4 fusion.39
  147.2 1.4 fusion.40
  153.5 1.4 fusion.39
  157.5 1.4 fusion.40
  163.7 1.4 fusion.39
  167.7 1.4 fusion.40
  173.9 1.4 fusion.39
  184.2 1.4 fusion.39
  194.4 1.4 fusion.39
  204.6 1.4 fusion.39
  214.8 1.4 fusion.39
  225.0 1.4 fusion.39
  235.3 1.4 fusion.39
  245.5 1.4 fusion.39
  251.8 2.1 multiply_reduce_fusion
  257.5 3.1 multiply_convert_fusion
  261.8 1.9 fusion.19
  263.7 3.7 reshape.96
  267.4 1.6 fusion.10
  270.0 3.2 all-to-all-start.1
  274.2 63.2 %all-reduce.2 = bf16[64,1536]{1,0:T(8,128)(2,1)S(1)} all-reduce(f32[64,1536]{1,0:T(8,128)S(1)} %bitcast.137), channel_id=4, replica_groups=mesh['query'=2,'ctx'=16] {'ctx'}, use_global_device_ids=true, to_apply=%region_5.6.clone | all-reduce | flops 98304 | bytes 589824
  337.5 6.5 %fusion.6 = bf16[12,1024,128]{2,1,0:T(8,128)(2,1)} fusion(bf16[12,16,2,2,1024]{4,3,2,1,0:T(2,128)(2,1)} %reshape.96, bf16[16,2,2,12,128]{4,3,1,2,0:T(8,128)(2,1)} %reshape.114), kind=kOutput, calls=%fused_computation.16 | convolution fusion | flops 209190912 | bytes 4915200 | tf_op jit(solution)/shard_map/hcbrk,cbrhd->bkhd/dot_general | solution.py:116
  345.3 3.2 all-to-all-start.3
  348.6 4.8 %fusion.7 = bf16[12,1024,128]{2,1,0:T(8,128)(2,1)} fusion(bf16[12,16,2,2,1024]{4,3,2,1,0:T(2,128)(2,1)S(1)} %reshape.97, bf16[16,2,2,12,128]{4,3,1,2,0:T(8,128)(2,1)S(1)} %copy-done.7), kind=kOutput, calls=%fused_computation.17 | convolution fusion | flops 206045184 | bytes 4915200 | tf_op jit(solution)/shard_map/hcbrk,cbrhd->bkhd/dot_general | solution.py:122
  353.3 3.2 copy.121
  356.5 2.9 copy.126
  359.4 3.2 copy.125
  362.6 2.9 copy.127
  (178 shorter events, 144.2 us)
Async XLA Ops:
  7.2 14.2 %copy-start = (f32[5,24]{1,0:T(8,128)S(1)}, f32[5,24]{1,0:T(8,128)}, u32[]{:S(2)}) copy-start(f32[5,24]{1,0:T(8,128)} %param.13) | copy-start | bytes 1444
  8.8 13.7 %all-to-all-start = ((bf16[32,2,1536]{2,0,1:T(8,128)(2,1)}), bf16[32,2,1536]{2,0,1:T(8,128)(2,1)S(1)}, u32[]{:S(2)}, u32[]{:S(2)}) async-start(bf16[32,2,1536]{2,0,1:T(8,128)(2,1)} %bitcast.102), calls=%async_computation | async-start | bytes 393216 | tf_op jit(solution)/shard_map/all_to_all | solution.py:43
  13.1 83.5 %all-gather.6.cloned.1.call-start = ((), (), s32[]{:S(2)}) async-start(), calls=%async_computation.4 | async-start | bytes 6684672 | tf_op jit(solution)/shard_map/all_gather | solution.py:10
  13.1 5.4 %copy-start.5 = (bf16[1024,1536]{1,0:T(8,128)(2,1)S(1)}, bf16[1024,1536]{1,0:T(8,128)(2,1)}, u32[]{:S(2)}) copy-start(bf16[1024,1536]{1,0:T(8,128)(2,1)} %param.11) | copy-start | bytes 9437188
  18.5 2.9 copy-start.11
  23.7 3.0 copy-start.2
  26.8 4.2 %copy-start.10 = (bf16[32,3072]{1,0:T(8,128)(2,1)S(1)}, bf16[32,3072]{1,0:T(8,128)(2,1)}, u32[]{:S(2)}) copy-start(bf16[32,3072]{1,0:T(8,128)(2,1)} %param.15) | copy-start | bytes 589828
  26.8 8.4 %copy-start.12 = (u32[32]{0:T(128)S(1)}, u32[32]{0:T(128)}, u32[]{:S(2)}) copy-start(u32[32]{0:T(128)} %constant.71) | copy-start | bytes 388
  31.7 8.7 %all-to-all-start.2 = ((bf16[32,2,1536]{2,0,1:T(8,128)(2,1)}), bf16[32,2,1536]{2,0,1:T(8,128)(2,1)S(1)}, u32[]{:S(2)}, u32[]{:S(2)}) async-start(bf16[32,2,1536]{2,0,1:T(8,128)(2,1)} %bitcast.140), calls=%async_computation.2 | async-start | bytes 393216 | tf_op jit(solution)/shard_map/all_to_all | solution.py:44
  64.1 0.7 copy-start.8
  85.0 0.6 copy-start.9
  257.5 4.3 %copy-start.1 = (bf16[1024,1536]{0,1:T(8,128)(2,1)S(1)}, bf16[1024,1536]{0,1:T(8,128)(2,1)}, u32[]{:S(2)}) copy-start(bf16[1024,1536]{0,1:T(8,128)(2,1)} %copy.98) | copy-start | bytes 9437188
  260.6 1.1 copy-start.3
  267.4 1.6 copy-start.6
  270.0 75.3 %all-to-all-start.1 = ((bf16[2,2,1536]{2,1,0:T(2,128)(2,1)}), bf16[2,2,1536]{2,1,0:T(2,128)(2,1)S(1)}, u32[]{:S(2)}, u32[]{:S(2)}) async-start(bf16[2,2,1536]{2,1,0:T(2,128)(2,1)} %all_to_all.55), calls=%async_computation.1 | async-start | bytes 24576 | tf_op jit(solution)/shard_map/all_to_all | solution.py:135
  337.5 7.2 %copy-start.4 = (bf16[12,64,1024]{2,1,0:T(8,128)(2,1)S(1)}, bf16[12,64,1024]{2,1,0:T(8,128)(2,1)}, u32[]{:S(2)}) copy-start(bf16[12,64,1024]{2,1,0:T(8,128)(2,1)} %fusion.10) | copy-start | bytes 4718596
  344.0 4.5 %copy-start.7 = (bf16[16,2,2,12,128]{4,3,1,2,0:T(8,128)(2,1)S(1)}, bf16[16,2,2,12,128]{4,3,1,2,0:T(8,128)(2,1)}, u32[]{:S(2)}) copy-start(bf16[16,2,2,12,128]{4,3,1,2,0:T(8,128)(2,1)} %reshape.115) | copy-start | bytes 589828
  345.3 20.3 %all-to-all-start.3 = ((bf16[2,2,1536]{2,1,0:T(2,128)(2,1)}), bf16[2,2,1536]{2,1,0:T(2,128)(2,1)S(1)}, u32[]{:S(2)}, u32[]{:S(2)}) async-start(bf16[2,2,1536]{2,1,0:T(2,128)(2,1)} %all_to_all.62), calls=%async_computation.3 | async-start | bytes 24576 | tf_op jit(solution)/shard_map/all_to_all | solution.py:136
Sparse Core Ops, SparseCore 0:
  31.1 65.4 all-gather.5
where the time goes:
time: 381 us; the launch traced here: 374 us
  local copies, waits for them, and re-layouts  134 us (35%)
  blocking collectives  105 us (28%)
  other arithmetic  70 us (18%)
  matrix products  21.8 us (6%)
  between operations  15.6 us (4%)
  starting transfers between devices  14.2 us (4%)
  waiting for transfers between devices  12.4 us (3%)
    unnamed x1, blocking collectives  63.2 us
    dynamic_slice x45, local copies, waits for them, and re-layouts, hop(): return combine(so_far, jax.tree.map(lambda part: part[k], everything))  51 us
    transpose x30, other arithmetic, rescale(): factor.T[:, :, None]  42.8 us
    all_gather x2, blocking collectives, combined_all(): everything = jax.tree.map(lambda part: lax.all_gather(part, axis), x)  41.5 us
    add x15, other arithmetic, combine_parts(): rescale(first_out, first_factor) + rescale(second_out, second_factor)  21.5 us
    while x15, local copies, waits for them, and re-layouts  20.4 us
    unnamed x34, local copies, waits for them, and re-layouts  17.9 us
    mul x30, local copies, waits for them, and re-layouts, rescale(): outputs.reshape(row_count, head_count, -1) * factor.T[:, :, None]  17.1 us
  transfers between devices with their start and end apart: 5, of which 2 were waited for; matrix products, arithmetic and copies ran while one was open for 11% of the time, Pallas kernels for 0%

commit v1 on v0

v1 whole, which is shorter than its diff:
```python
import functools
import math

import jax
import jax.numpy as jnp
from jax import lax
from jax.experimental import pallas as pl
from jax.experimental.pallas import tpu as pltpu
from jax.sharding import PartitionSpec as P

F32 = jnp.float32
BF16 = jnp.bfloat16
MIB = 1024 * 1024
VMEM = pl.BlockSpec(memory_space=pltpu.VMEM)


def call(body, out_shape, vmem_mib, flops, **kwargs):
    return pl.pallas_call(
        body,
        out_shape=out_shape,
        compiler_params=pltpu.CompilerParams(vmem_limit_bytes=vmem_mib * MIB),
        cost_estimate=pl.CostEstimate(flops=flops, bytes_accessed=MIB, transcendentals=0),
        **kwargs,
    )


def nt(a, b):
    return lax.dot_general(a, b, (((1,), (1,)), ((), ())), preferred_element_type=F32)


def nn(a, b):
    return lax.dot_general(a, b, (((1,), (0,)), ((), ())), preferred_element_type=F32)


class Plan:
    def __init__(self, query_states, key_states, level_bias):
        self.query_ways = lax.axis_size("query")
        self.owner_ways = lax.axis_size("ctx")
        self.slots, self.features = key_states.shape
        self.heads = level_bias.shape[1] // self.query_ways
        self.head_size = self.features // self.heads
        self.scale = 1.0 / math.sqrt(self.head_size)
        self.own_rows = query_states.shape[0]
        self.rows = self.own_rows * self.query_ways
        self.part_rows = self.own_rows // self.owner_ways
        self.last_rows = self.part_rows * self.query_ways
        self.group = 2 if self.heads % 2 == 0 and self.rows <= 128 else 1
        self.groups = self.heads // self.group
        self.lanes = self.group * self.rows
        self.rounds = self.owner_ways.bit_length() - 1
        assert 1 << self.rounds == self.owner_ways and self.groups <= 8
        counts = [self.rows]
        for _ in range(self.rounds):
            half = counts[-1] // 2
            counts.append(half if half >= 8 else counts[-1])
        self.counts = counts

    def split(self, k):
        return k < self.rounds and self.counts[k + 1] < self.counts[k]

    def bit(self, k):
        return (lax.axis_index("ctx") >> k) & 1

    def keep(self, k):
        return self.bit(k) * self.counts[k + 1] if self.split(k) else 0

    def give(self, k):
        return (1 - self.bit(k)) * self.counts[k + 1] if self.split(k) else 0

    def base(self, k):
        return sum((self.keep(j) for j in range(k)), 0)

    def last_offset(self):
        offset = 0
        for k in range(self.rounds):
            if not self.split(k):
                offset = offset + self.bit(k) * (self.rows >> (k + 1))
        return offset


def aligned(x, by):
    return pl.multiple_of(x, by) if by >= 8 and not isinstance(x, int) else x


def forward_body(plan, split_parts, *refs):
    if split_parts:
        q_ref, g_ref, moved_ref = refs[:3]
        refs = refs[3:]
    else:
        moved_ref = refs[0]
        refs = refs[1:]
    (k_ref, v_ref, term_ref, part_ref, send_ref, stat_ref, pair_ref, qb_ref, gb_ref) = refs[:9]
    source, scores, dprobs, columns = refs[9:]
    rows, size, group = plan.rows, plan.head_size, plan.group
    width = group * size
    place = lax.broadcasted_iota(jnp.int32, (rows, rows), 0)
    column = lax.broadcasted_iota(jnp.int32, (rows, rows), 1)
    inner = place % plan.last_rows
    outer = place // plan.last_rows
    owner = jnp.zeros_like(outer)
    for k in range(plan.rounds):
        owner = owner | (((outer >> (plan.rounds - 1 - k)) & 1) << k)
    wanted = (
        inner // plan.part_rows * plan.own_rows + owner * plan.part_rows + inner % plan.part_rows
    )
    permute = (column == wanted).astype(F32).astype(BF16)
    qb_ref[...] = jnp.zeros_like(qb_ref)
    gb_ref[...] = jnp.zeros_like(gb_ref)
    for which, own_ref, block_ref in ((0, 0, qb_ref), (1, 1, gb_ref)):
        if split_parts:
            mine = (q_ref, g_ref)[own_ref]
            start = pl.multiple_of(lax.axis_index("query") * plan.features, 128)
            source[: plan.own_rows] = mine[:, pl.ds(start, plan.features)]
            source[plan.own_rows :] = moved_ref[which]
        else:
            source[...] = moved_ref[which]
        for p in range(plan.groups):
            ordered = nn(permute, source[:, p * width : (p + 1) * width]).astype(BF16)
            for q in range(group):
                block_ref[p, q * rows : (q + 1) * rows, q * size : (q + 1) * size] = ordered[
                    :, q * size : (q + 1) * size
                ]
    columns[...] = jnp.zeros_like(columns)
    step = 16
    for p in range(plan.groups):
        keys = k_ref[:, p * width : (p + 1) * width]
        values = v_ref[:, p * width : (p + 1) * width]
        scores[...] = nt(qb_ref[p], keys)
        dprobs[...] = nt(gb_ref[p], values)
        for r in range(0, plan.lanes, step):
            h = p * group + r // rows
            s = scores[r : r + step] * plan.scale + term_ref[h : h + 1, :]
            top = jnp.max(s, axis=1, keepdims=True)
            e = jnp.exp(s - top)
            total = jnp.sum(e, axis=1, keepdims=True)
            d = dprobs[r : r + step]
            mean = jnp.sum(e * d, axis=1, keepdims=True) / total
            pair_ref[p, r : r + step, :] = e.astype(BF16)
            pair_ref[p, plan.lanes + r : plan.lanes + r + step, :] = (e * (d - mean)).astype(BF16)
            columns[r : r + step, p : p + 1] = top
            columns[r : r + step, 8 + p : 9 + p] = total
            columns[r : r + step, 16 + p : 17 + p] = mean
        with_values = nn(pair_ref[p, : plan.lanes, :], values)
        with_keys = nn(pair_ref[p], keys)
        for q in range(group):
            at = slice(q * rows, (q + 1) * rows)
            of = slice(q * size, (q + 1) * size)
            part_ref[0, p * group + q] = with_values[at, of]
            part_ref[1, p * group + q] = with_keys[at, of]
            part_ref[2, p * group + q] = with_keys[plan.lanes + q * rows : plan.lanes + (q + 1) * rows, of]
    count = plan.counts[1]
    gone = pl.ds(aligned(plan.give(0), count), count)
    for a in range(3):
        for h in range(plan.heads):
            send_ref[a, h] = part_ref[a, h, gone, :].astype(BF16)
    stat_ref[...] = columns[...].T[:24]


def merge_body(plan, k, part_ref, came_ref, stat_ref, stat_came_ref, *refs):
    last = k == plan.rounds - 1
    if last:
        stat_new_ref, own_ref, send_ref, table = refs
    else:
        part_new_ref, send_ref, stat_new_ref, table = refs
    top1, total1, mean1 = (stat_ref[8 * t : 8 * t + 8] for t in range(3))
    top2, total2, mean2 = (stat_came_ref[8 * t : 8 * t + 8] for t in range(3))
    top = jnp.maximum(top1, top2)
    f1 = jnp.exp(top1 - top)
    f2 = jnp.exp(top2 - top)
    total = f1 * total1 + f2 * total2
    live = total > 0.0
    inverse = 1.0 / jnp.where(live, total, 1.0)
    w1 = f1 * total1 * inverse
    w2 = f2 * total2 * inverse
    stat_new_ref[0:8] = top
    stat_new_ref[8:16] = total
    stat_new_ref[16:24] = mean1 * w1 + mean2 * w2
    gap = mean1 - mean2
    rest = 128 - 40
    table[...] = jnp.concatenate(
        [f1, f2, f1 * w2 * gap, -f2 * w1 * gap, inverse, jnp.zeros((rest, plan.lanes), F32)], axis=0
    ).T
    count = plan.counts[k + 1]
    kept = pl.ds(aligned(plan.keep(k), count), count)
    base = plan.base(k + 1)
    if last:
        offset = plan.last_offset()
    for h in range(plan.heads):
        p, q = h // plan.group, h % plan.group
        at = pl.ds(aligned(q * plan.rows + base, count), count)
        factors = table[at, :]
        col = lambda t: factors[:, 8 * t + p : 8 * t + p + 1]
        out1, key1, dif1 = (part_ref[a, h, kept, :] for a in range(3))
        out2, key2, dif2 = (came_ref[a, h].astype(F32) for a in range(3))
        c1, c2 = col(0), col(1)
        out = c1 * out1 + c2 * out2
        dif = c1 * dif1 + c2 * dif2 + col(2) * key1 + col(3) * key2
        if not last:
            part_new_ref[0, h] = out
            part_new_ref[1, h] = c1 * key1 + c2 * key2
            part_new_ref[2, h] = dif
            continue
        share = col(4)
        for a, x in ((0, out * share), (1, dif * (share * plan.scale))):
            if not isinstance(offset, int):
                x = pltpu.roll(x, (count - offset) % count, 0)
            of = slice(h * plan.head_size, (h + 1) * plan.head_size)
            if own_ref is not None:
                own_ref[a, :, of] = x[: plan.part_rows].astype(BF16)
                send_ref[a, :, of] = x[plan.part_rows : plan.last_rows].astype(BF16)
            else:
                send_ref[a, :, of] = x[: plan.last_rows].astype(BF16)
    if not last:
        after = plan.counts[k + 2]
        gone = pl.ds(aligned(plan.give(k + 1), after), after)
        for a in range(3):
            for h in range(plan.heads):
                send_ref[a, h] = part_new_ref[a, h, gone, :].astype(BF16)


def turn_body(pair_ref, turned_ref):
    for p in range(pair_ref.shape[0]):
        turned_ref[p] = pair_ref[p].T


def backward_body(plan, stat_ref, stat_all_ref, qb_ref, gb_ref, turned_ref, dk_ref, dv_ref, table, wk, wv):
    lanes = plan.lanes

    @pl.when(pl.program_id(0) == 0)
    def _():
        inverse = 1.0 / jnp.where(stat_all_ref[8:16] > 0.0, stat_all_ref[8:16], 1.0)
        f = jnp.exp(stat_ref[0:8] - stat_all_ref[0:8]) * inverse
        c = f * (stat_ref[16:24] - stat_all_ref[16:24])
        rest = jnp.zeros((128 - 24, lanes), F32)
        table[...] = jnp.concatenate([f, f * plan.scale, c * plan.scale, rest], axis=0).T
        for p in range(plan.groups):
            queries = qb_ref[p].astype(F32)
            wv[p] = (gb_ref[p].astype(F32) * table[:, p : p + 1]).astype(BF16)
            wk[p, :lanes] = (queries * table[:, 16 + p : 17 + p]).astype(BF16)
            wk[p, lanes:] = (queries * table[:, 8 + p : 9 + p]).astype(BF16)

    p = pl.program_id(0)
    dk_ref[...] = nn(turned_ref[0], wk[p]).astype(BF16)
    dv_ref[...] = nn(turned_ref[0, :, :lanes], wv[p]).astype(BF16)


def local(query_states, key_states, value_states, level_ids, level_bias, live_counts, out_grad):
    plan = Plan(query_states, key_states, level_bias)
    qi = lax.axis_index("query")
    size, slots, lanes, groups, heads = plan.head_size, plan.slots, plan.lanes, plan.groups, plan.heads
    width = plan.group * size
    pairwise = plan.query_ways == 2
    both = jnp.stack([query_states, out_grad])
    if pairwise:
        theirs = lax.dynamic_slice_in_dim(both, (1 - qi) * plan.features, plan.features, 2)
        moved = lax.ppermute(theirs, "query", [(0, 1), (1, 0)])
        row_inputs = (query_states, out_grad, moved)
    else:
        row_inputs = (lax.all_to_all(both, "query", split_axis=2, concat_axis=1, tiled=True),)
    table = lax.dynamic_slice_in_dim(level_bias, qi * heads, heads, 1)
    term = jnp.zeros((heads, slots), F32)
    for level in range(level_bias.shape[0]):
        term = jnp.where(level_ids[None, :] == level, table[level][:, None], term)
    slot = lax.broadcasted_iota(jnp.int32, (1, slots), 1)
    term = jnp.where(slot < live_counts[0], term, -1e30)

    stat_shape = jax.ShapeDtypeStruct((24, lanes), F32)
    block_shape = jax.ShapeDtypeStruct((groups, lanes, width), BF16)
    part_shape = lambda k: jax.ShapeDtypeStruct((3, heads, plan.counts[k], size), F32)
    send_shape = lambda k: jax.ShapeDtypeStruct((3, heads, plan.counts[k + 1], size), BF16)
    part, send, stat_own, pair, qb, gb = call(
        functools.partial(forward_body, plan, pairwise),
        (
            part_shape(0),
            send_shape(0),
            stat_shape,
            jax.ShapeDtypeStruct((groups, 2 * lanes, slots), BF16),
            block_shape,
            block_shape,
        ),
        24,
        4 * 10**9,
        in_specs=[VMEM] * (len(row_inputs) + 3),
        out_specs=[VMEM] * 6,
        scratch_shapes=[
            pltpu.VMEM((plan.rows, plan.features), BF16),
            pltpu.VMEM((lanes, slots), F32),
            pltpu.VMEM((lanes, slots), F32),
            pltpu.VMEM((lanes, 128), F32),
        ],
        name="forward",
    )(*row_inputs, key_states, value_states, term)

    turned = call(
        turn_body,
        jax.ShapeDtypeStruct((groups, slots, 2 * lanes), BF16),
        8,
        10**9,
        in_specs=[VMEM],
        out_specs=VMEM,
        name="turn",
    )(pair)

    stat = stat_own
    for k in range(plan.rounds):
        swap = [(i, i ^ (1 << k)) for i in range(plan.owner_ways)]
        came = lax.ppermute(send, "ctx", swap)
        stat_came = lax.ppermute(stat, "ctx", swap)
        last = k == plan.rounds - 1
        if not last:
            outs = (part_shape(k + 1), send_shape(k + 1), stat_shape)
        elif pairwise:
            rows_shape = jax.ShapeDtypeStruct((2, plan.part_rows, plan.features), BF16)
            outs = (stat_shape, rows_shape, rows_shape)
        else:
            outs = (stat_shape, jax.ShapeDtypeStruct((2, plan.last_rows, plan.features), BF16))
        body = functools.partial(merge_body, plan, k)
        if last and not pairwise:
            body = lambda a, b, c, d, s, o, t: merge_body(plan, plan.rounds - 1, a, b, c, d, s, None, o, t)
        result = call(
            body,
            outs,
            8,
            10**8,
            in_specs=[VMEM] * 4,
            out_specs=[VMEM] * len(outs),
            scratch_shapes=[pltpu.VMEM((lanes, 128), F32)],
            name=f"merge{k}",
        )(part, came, stat, stat_came)
        if not last:
            part, send, stat = result
    stat = result[0]
    if pairwise:
        own, away = result[1:]
        back = lax.ppermute(away, "query", [(0, 1), (1, 0)])

    key_grad, value_grad = call(
        functools.partial(backward_body, plan),
        (jax.ShapeDtypeStruct(key_states.shape, BF16), jax.ShapeDtypeStruct(value_states.shape, BF16)),
        16,
        4 * 10**9,
        grid=(groups,),
        in_specs=[
            pl.BlockSpec((24, lanes), lambda p: (0, 0)),
            pl.BlockSpec((24, lanes), lambda p: (0, 0)),
            pl.BlockSpec((groups, lanes, width), lambda p: (0, 0, 0)),
            pl.BlockSpec((groups, lanes, width), lambda p: (0, 0, 0)),
            pl.BlockSpec((1, slots, 2 * lanes), lambda p: (p, 0, 0)),
        ],
        out_specs=[pl.BlockSpec((slots, width), lambda p: (0, p))] * 2,
        scratch_shapes=[
            pltpu.VMEM((lanes, 128), F32),
            pltpu.VMEM((groups, 2 * lanes, width), BF16),
            pltpu.VMEM((groups, lanes, width), BF16),
        ],
        name="backward",
    )(stat_own, stat, qb, gb, turned)

    if pairwise:
        first = jnp.where(qi == 0, own, back)
        second = jnp.where(qi == 0, back, own)
        final = jnp.concatenate([first, second], axis=2)
    else:
        final = lax.all_to_all(result[1], "query", split_axis=1, concat_axis=2, tiled=True)
    return final[0], final[1], key_grad, value_grad


def solution(mesh):
    placed = (
        P("query", None),
        P("ctx", "query"),
        P("ctx", "query"),
        P("ctx"),
        P(),
        P("ctx"),
        P("query", None),
    )
    return jax.shard_map(
        local,
        mesh=mesh,
        in_specs=placed,
        out_specs=(
            P(("query", "ctx"), None),
            P(("query", "ctx"), None),
            P("ctx", "query"),
            P("ctx", "query"),
        ),
        check_vma=False,
    )
```

time: 381 us -> 53.3 us (0.14); the launches traced: 374 us -> 53 us
  local copies, waits for them, and re-layouts: 134 us -> 7.35 us
  blocking collectives: 105 us -> 0 us
  other arithmetic: 70 us -> 2.4 us
  matrix products: 21.8 us -> 0 us
  between operations: 15.6 us -> 1.39 us
  Pallas kernels: 0 us -> 12.7 us
  waiting for transfers between devices: 12.4 us -> 16.9 us
    unnamed x1 -> x0, blocking collectives: 63.2 us -> none
    dynamic_slice x45 -> x1, local copies, waits for them, and re-layouts: 51 us -> 0.08 us  [local(): table = lax.dynamic_slice_in_dim(level_bias, qi * heads, heads, 1)]
    transpose x30 -> x0, other arithmetic: 42.8 us -> none  [rescale(): factor.T[:, :, None]]
    all_gather x2 -> x0, blocking collectives: 41.5 us -> none  [combined_all(): everything = jax.tree.map(lambda part: lax.all_gather(part, axis), x)]
    add x16 -> x0, other arithmetic: 22.9 us -> none  [the longest x15 21.5 us: combine_parts(): rescale(first_out, first_factor) + rescale(second_out, second_factor)]
    while x17 -> x0, local copies, waits for them, and re-layouts: 21.8 us -> none
    dot_general x7 -> x0, matrix products: 21.8 us -> none  [the longest x1 6.52 us: local(): jnp.einsum('hcbrk,cbrhd->bkhd', dscores.reshape(block_shape), queries.res...]
    mul x31 -> x0, local copies, waits for them, and re-layouts: 18.1 us -> none  [the longest x30 17.1 us: rescale(): outputs.reshape(row_count, head_count, -1) * factor.T[:, :, None]]
  transfers between devices with their start and end apart: 5 -> 10, of which waited for: 2 -> 6; matrix products, arithmetic and copies ran while one was open for 11% -> 2% of each run, Pallas kernels for 0% -> 11%
where the time goes in v1:
time: 53.3 us; the launch traced here: 53 us
  waiting for transfers between devices  16.9 us (32%)
  Pallas kernels  12.7 us (24%)
  starting transfers between devices  12.3 us (23%)
  local copies, waits for them, and re-layouts  7.35 us (14%)
  other arithmetic  2.4 us (5%)
  between operations  1.39 us (3%)
    ppermute x4, waiting for transfers between devices, local(): stat_came = lax.ppermute(stat, 'ctx', swap)  10.4 us
    unnamed x22, local copies, waits for them, and re-layouts  7.26 us
    pallas_call x1, Pallas kernels, local(): call(functools.partial(backward_body, plan), (jax.ShapeDtypeStruct(key_st...  5.07 us
    pallas_call x1, Pallas kernels, local(): call(functools.partial(forward_body, plan, pairwise), (part_shape(0), sen...  4.61 us
    ppermute x4, starting transfers between devices, local(): came = lax.ppermute(send, 'ctx', swap)  3.92 us
    ppermute x4, starting transfers between devices, local(): stat_came = lax.ppermute(stat, 'ctx', swap)  3.75 us
    ppermute x1, waiting for transfers between devices, local(): moved = lax.ppermute(theirs, 'query', [(0, 1), (1, 0)])  3.35 us
    ppermute x4, waiting for transfers between devices, local(): came = lax.ppermute(send, 'ctx', swap)  3.14 us
  transfers between devices with their start and end apart: 10, of which 6 were waited for; matrix products, arithmetic and copies ran while one was open for 2% of the time, Pallas kernels for 11%

profile of v1, /device:TPU:0, one launch (start us, length us, event | category | flops | bytes accessed | tf_op | source)
XLA Modules:
  0.0 53.0 jit_solution(16474506771646076858)
XLA Ops:
  0.6 0.0 copy-start
  0.7 1.0 %fusion = bf16[2,32,1536]{2,1,0:T(8,128)(2,1)S(1)} fusion(s32[]{:T(128)S(6)} %select_n.39, bf16[1,32,3072]{2,1,0:T(8,128)(2,1)} %bitcast.18, bf16[1,32,3072]{2,1,0:T(8,128)(2,1)} %bitcast.19), kind=kLoop, calls=%fused_computation.2 | loop fusion | flops 393216 | bytes 589828 | tf_op jit(solution)/shard_map/stack | solution.py:253
  1.6 3.1 %collective-permute-start = (bf16[2,32,1536]{2,1,0:T(8,128)(2,1)S(1)}, bf16[2,32,1536]{2,1,0:T(8,128)(2,1)S(1)}, u32[]{:S(2)}, u32[]{:S(2)}) collective-permute-start(bf16[2,32,1536]{2,1,0:T(8,128)(2,1)S(1)} %fusion), channel_id=1, source_target_pairs={{0,16},{16,0},{1,17},{17,1},{2,18},{18,2},{3,19},{19,3},{4,20},{20... | collective-permute-start | bytes 589832 | tf_op jit(solution)/shard_map/ppermute | solution.py:256
  5.3 0.0 copy-done
  5.3 0.1 constant_dynamic-slice_fusion
  5.4 0.7 %broadcast_compare_fusion.4 = (pred[1024]{0:T(1024)(128)(4,1)S(1)}, pred[1024]{0:T(1024)(128)(4,1)S(1)}, pred[1024]{0:T(1024)(128)(4,1)S(1)}, pred[1024]{0:T(1024)(128)(4,1)S(1)}, pred[1024]{0:T(1024)(128)(4,1)S(1)}) fusion(s32[1024]{0:T(1024)} %param.10), kind=kLoop, calls=%fused_computation.17 | loop fusion | flops 5120 | bytes 9216 | tf_op jit(solution)/shard_map/eq | solution.py:263
  6.1 0.1 select_select_fusion.refs_5_
  6.2 3.4 %collective-permute-done.refs_2_ = bf16[2,32,1536]{2,1,0:T(8,128)(2,1)S(1)} collective-permute-done((bf16[2,32,1536]{2,1,0:T(8,128)(2,1)S(1)}, bf16[2,32,1536]{2,1,0:T(8,128)(2,1)S(1)}, u32[]{:S(2)}, u32[]{:S(2)}) %collective-permute-start) | collective-permute-done | bytes 196640 | tf_op jit(solution)/shard_map/ppermute | solution.py:256
  9.6 0.0 copy-start.5
  9.6 0.7 %copy-done.5 = bf16[2,32,1536]{2,1,0:T(8,128)(2,1)} copy-done((bf16[2,32,1536]{2,1,0:T(8,128)(2,1)}, bf16[2,32,1536]{2,1,0:T(8,128)(2,1)S(1)}, u32[]{:S(2)}) %copy-start.5) | copy-done | bytes 196632
  10.3 0.0 copy-start.1
  10.3 0.9 %copy-done.1 = bf16[32,3072]{1,0:T(8,128)(2,1)S(1)} copy-done((bf16[32,3072]{1,0:T(8,128)(2,1)S(1)}, bf16[32,3072]{1,0:T(8,128)(2,1)}, u32[]{:S(2)}) %copy-start.1) | copy-done | bytes 196632
  11.2 0.9 %copy-done.2 = bf16[32,3072]{1,0:T(8,128)(2,1)S(1)} copy-done((bf16[32,3072]{1,0:T(8,128)(2,1)S(1)}, bf16[32,3072]{1,0:T(8,128)(2,1)}, u32[]{:S(2)}) %copy-start.2) | copy-done | bytes 196632
  12.1 1.9 %copy-done.3 = bf16[1024,1536]{1,0:T(8,128)(2,1)S(1)} copy-done((bf16[1024,1536]{1,0:T(8,128)(2,1)S(1)}, bf16[1024,1536]{1,0:T(8,128)(2,1)}, u32[]{:S(2)}) %copy-start.3) | copy-done | bytes 3145752
  14.0 1.9 %copy-done.4 = bf16[1024,1536]{1,0:T(8,128)(2,1)S(1)} copy-done((bf16[1024,1536]{1,0:T(8,128)(2,1)S(1)}, bf16[1024,1536]{1,0:T(8,128)(2,1)}, u32[]{:S(2)}) %copy-start.4) | copy-done | bytes 3145752
  15.9 0.9 %copy-done.6 = bf16[2,32,1536]{2,1,0:T(8,128)(2,1)S(1)} copy-done((bf16[2,32,1536]{2,1,0:T(8,128)(2,1)S(1)}, bf16[2,32,1536]{2,1,0:T(8,128)(2,1)}, u32[]{:S(2)}) %copy-start.6) | copy-done | bytes 196632
  16.8 4.6 %forward.1 = (f32[3,12,64,128]{3,2,1,0:T(8,128)S(1)}, bf16[3,12,32,128]{3,2,1,0:T(8,128)(2,1)S(1)}, f32[24,128]{1,0:T(8,128)S(1)}, bf16[6,256,1024]{2,1,0:T(8,12...) custom-call(bf16[32,3072]{1,0:T(8,128)(2,1)S(1)} %copy-done.1, ...), custom_call_target="tpu_custom_call" | custom-call | flops 4000000000 | bytes 1048576 | tf_op jit(solution)/shard_map/forward/pallas_call | solution.py:271
  21.4 0.0 copy-start.7
  21.4 0.0 copy-start.9
  21.5 0.1 collective-permute-start.1
  21.5 0.5 collective-permute-start.2
  22.0 1.1 %collective-permute-done.2.stat_came_ref = f32[24,128]{1,0:T(8,128)S(1)} collective-permute-done((f32[24,128]{1,0:T(8,128)S(1)}, f32[24,128]{1,0:T(8,128)S(1)}, u32[]{:S(2)}, u32[]{:S(2)}) %collective-permute-start.2) | collective-permute-done | bytes 12320 | tf_op jit(solution)/shard_map/ppermute | solution.py:308
  23.1 0.0 collective-permute-done.1.came_ref
  23.1 0.5 merge0.1
  23.6 1.8 %collective-permute-start.3 = (bf16[3,12,16,128]{3,2,1,0:T(8,128)(2,1)S(1)}, bf16[3,12,16,128]{3,2,1,0:T(8,128)(2,1)S(1)}, u32[]{:S(2)}, u32[]{:S(2)}) collective-permute-start(bf16[3,12,16,128]{3,2,1,0:T(8,128)(2,1)S(1)} %get-tuple-element.28), channel_id=1, source_target_pairs={{0,2},{1,3},{2,0},{3,1},{4,6},{5,7},{6,4},{7,5},{8,10},{9,11},{10,... | collective-permute-start | bytes 442376 | tf_op jit(solution)/shard_map/ppermute | solution.py:307
  25.4 0.3 collective-permute-start.4
  25.7 4.1 %collective-permute-done.4.stat_came_ref = f32[24,128]{1,0:T(8,128)S(1)} collective-permute-done((f32[24,128]{1,0:T(8,128)S(1)}, f32[24,128]{1,0:T(8,128)S(1)}, u32[]{:S(2)}, u32[]{:S(2)}) %collective-permute-start.4) | collective-permute-done | bytes 12320 | tf_op jit(solution)/shard_map/ppermute | solution.py:308
  29.9 0.0 collective-permute-done.3.came_ref
  29.9 1.0 %merge1.1 = (f32[3,12,16,128]{3,2,1,0:T(8,128)S(1)}, bf16[3,12,8,128]{3,2,1,0:T(8,128)(2,1)}, f32[24,128]{1,0:T(8,128)S(1)}) custom-call(f32[3,12,32,128]{3,2,1,0:T(8,128)S(1)} %get-tuple-element.27.part_ref, bf16[3,12,16,128]{3,2,1,0:T(8,128)(2,1)S(1)} %collective-permute-done.3.came_ref, f32[24,128]{1,0:T(8,128)S(1)} %get-tuple-element.29.stat_ref, ...), custom_call_target="tpu_custom_call" | custom-call | flops 100000000 | bytes 1048576 | tf_op jit(solution)/shard_map/merge1/pallas_call | solution.py:320
  30.9 1.8 %collective-permute-start.5 = (bf16[3,12,8,128]{3,2,1,0:T(8,128)(2,1)}, bf16[3,12,8,128]{3,2,1,0:T(8,128)(2,1)S(1)}, u32[]{:S(2)}, u32[]{:S(2)}) collective-permute-start(bf16[3,12,8,128]{3,2,1,0:T(8,128)(2,1)} %get-tuple-element.31), channel_id=1, source_target_pairs={{0,4},{1,5},{2,6},{3,7},{4,0},{5,1},{6,2},{7,3},{8,12},{9,13},{10,... | collective-permute-start | bytes 221192 | tf_op jit(solution)/shard_map/ppermute | solution.py:307
  32.6 0.0 copy-done.7
  32.6 0.0 copy-done.9
  32.6 0.3 collective-permute-start.6
  32.9 3.4 %collective-permute-done.6.stat_came_ref = f32[24,128]{1,0:T(8,128)S(1)} collective-permute-done((f32[24,128]{1,0:T(8,128)S(1)}, f32[24,128]{1,0:T(8,128)S(1)}, u32[]{:S(2)}, u32[]{:S(2)}) %collective-permute-start.6) | collective-permute-done | bytes 12320 | tf_op jit(solution)/shard_map/ppermute | solution.py:308
  36.3 0.0 collective-permute-done.5.came_ref
  36.3 0.3 merge2.1
  36.6 2.7 %collective-permute-start.8 = (f32[24,128]{1,0:T(8,128)S(1)}, f32[24,128]{1,0:T(8,128)S(1)}, u32[]{:S(2)}, u32[]{:S(2)}) collective-permute-start(f32[24,128]{1,0:T(8,128)S(1)} %get-tuple-element.35.stat_ref), channel_id=1, source_target_pairs={{0,8},{1,9},{2,10},{3,11},{4,12},{5,13},{6,14},{7,15},{8,0},{9,1},... | collective-permute-start | bytes 36872 | tf_op jit(solution)/shard_map/ppermute | solution.py:308
  39.3 0.3 collective-permute-start.7
  39.6 0.9 %turn.1.turned_ref = bf16[6,1024,256]{2,1,0:T(8,128)(2,1)S(1)} custom-call(bf16[6,256,1024]{2,1,0:T(8,128)(2,1)S(1)} %get-tuple-element.41.pair_ref), custom_call_target="tpu_custom_call" | custom-call | flops 1000000000 | bytes 1048576 | tf_op jit(solution)/shard_map/turn/pallas_call | solution.py:294
  40.5 1.7 %collective-permute-done.8.stat_came_ref = f32[24,128]{1,0:T(8,128)S(1)} collective-permute-done((f32[24,128]{1,0:T(8,128)S(1)}, f32[24,128]{1,0:T(8,128)S(1)}, u32[]{:S(2)}, u32[]{:S(2)}) %collective-permute-start.8) | collective-permute-done | bytes 12320 | tf_op jit(solution)/shard_map/ppermute | solution.py:308
  42.2 3.1 %collective-permute-done.7.came_ref = bf16[3,12,8,128]{3,2,1,0:T(8,128)(2,1)S(1)} collective-permute-done((bf16[3,12,8,128]{3,2,1,0:T(8,128)(2,1)S(1)}, bf16[3,12,8,128]{3,2,1,0:T(8,128)(2,1)S(1)}, u32[]{:S(2)}, u32[]{:S(2)}) %collective-permute-start.7) | collective-permute-done | bytes 73760 | tf_op jit(solution)/shard_map/ppermute | solution.py:307
  45.3 0.3 merge3.1
  45.7 1.6 %collective-permute-start.9 = (bf16[2,2,1536]{2,1,0:T(2,128)(2,1)S(1)}, bf16[2,2,1536]{2,1,0:T(2,128)(2,1)S(1)}, u32[]{:S(2)}, u32[]{:S(2)}) collective-permute-start(bf16[2,2,1536]{2,1,0:T(2,128)(2,1)S(1)} %get-tuple-element.37), channel_id=1, source_target_pairs={{0,16},{16,0},{1,17},{17,1},{2,18},{18,2},{3,19},{19,3},{4,20},{20... | collective-permute-start | bytes 36872 | tf_op jit(solution)/shard_map/ppermute | solution.py:335
  47.2 0.0 copy-done.8
  47.2 0.0 copy-done.10
  47.3 5.1 %backward.1 = (bf16[1024,1536]{1,0:T(8,128)(2,1)}, bf16[1024,1536]{1,0:T(8,128)(2,1)}) custom-call(f32[24,128]{1,0:T(8,128)S(1)} %get-tuple-element.26.stat_ref, f32[24,128]{1,0:T(8,128)S(1)} %get-tuple-element.38.stat_all_ref, bf16[6,128,256]{2,1,0:T(8,128)(2,1)S(1)} %copy-done.8, bf16[6,128,256]{2,1,0:T(8,128)(2,1)S(1)} %copy-done.10, ...), custom_call_target="tpu_custom_call" | custom-call | flops 4000000000 | bytes 1048576 | tf_op jit(solution)/shard_map/backward/pallas_call | solution.py:337
  52.3 0.0 collective-permute-done.9
  52.3 0.6 %fusion.2 = (bf16[2,3072]{1,0:T(2,128)(2,1)}, bf16[2,3072]{1,0:T(2,128)(2,1)}) fusion(bf16[2,2,1536]{2,1,0:T(2,128)(2,1)S(1)} %get-tuple-element.47, bf16[2,2,1536]{2,1,0:T(2,128)(2,1)S(1)} %get-tuple-element.46), kind=kLoop, calls=%fused_computation.10 | loop fusion | flops 49152 | bytes 49152 | tf_op jit(solution)/shard_map/squeeze | solution.py:365
  (9 shorter events, 0.0 us)
Async XLA Ops:
  0.6 4.7 %copy-start = (f32[5,24]{1,0:T(8,128)S(1)}, f32[5,24]{1,0:T(8,128)}, u32[]{:S(2)}) copy-start(f32[5,24]{1,0:T(8,128)} %param.11) | copy-start | bytes 1444
  1.6 8.0 %collective-permute-start = (bf16[2,32,1536]{2,1,0:T(8,128)(2,1)S(1)}, bf16[2,32,1536]{2,1,0:T(8,128)(2,1)S(1)}, u32[]{:S(2)}, u32[]{:S(2)}) collective-permute-start(bf16[2,32,1536]{2,1,0:T(8,128)(2,1)S(1)} %fusion), channel_id=1, source_target_pairs={{0,16},{16,0},{1,17},{17,1},{2,18},{18,2},{3,19},{19,3},{4,20},{20... | collective-permute-start | bytes 589832 | tf_op jit(solution)/shard_map/ppermute | solution.py:256
  9.6 0.7 %copy-start.5 = (bf16[2,32,1536]{2,1,0:T(8,128)(2,1)}, bf16[2,32,1536]{2,1,0:T(8,128)(2,1)S(1)}, u32[]{:S(2)}) copy-start(bf16[2,32,1536]{2,1,0:T(8,128)(2,1)S(1)} %collective-permute-done.refs_2_) | copy-start | bytes 589828
  10.3 0.9 %copy-start.1 = (bf16[32,3072]{1,0:T(8,128)(2,1)S(1)}, bf16[32,3072]{1,0:T(8,128)(2,1)}, u32[]{:S(2)}) copy-start(bf16[32,3072]{1,0:T(8,128)(2,1)} %refs_0_.1) | copy-start | bytes 589828
  11.2 0.9 %copy-start.2 = (bf16[32,3072]{1,0:T(8,128)(2,1)S(1)}, bf16[32,3072]{1,0:T(8,128)(2,1)}, u32[]{:S(2)}) copy-start(bf16[32,3072]{1,0:T(8,128)(2,1)} %refs_1_.1) | copy-start | bytes 589828
  12.1 1.9 %copy-start.3 = (bf16[1024,1536]{1,0:T(8,128)(2,1)S(1)}, bf16[1024,1536]{1,0:T(8,128)(2,1)}, u32[]{:S(2)}) copy-start(bf16[1024,1536]{1,0:T(8,128)(2,1)} %refs_3_.1) | copy-start | bytes 9437188
  14.0 1.9 %copy-start.4 = (bf16[1024,1536]{1,0:T(8,128)(2,1)S(1)}, bf16[1024,1536]{1,0:T(8,128)(2,1)}, u32[]{:S(2)}) copy-start(bf16[1024,1536]{1,0:T(8,128)(2,1)} %refs_4_.1) | copy-start | bytes 9437188
  15.9 0.9 %copy-start.6 = (bf16[2,32,1536]{2,1,0:T(8,128)(2,1)S(1)}, bf16[2,32,1536]{2,1,0:T(8,128)(2,1)}, u32[]{:S(2)}) copy-start(bf16[2,32,1536]{2,1,0:T(8,128)(2,1)} %copy-done.5) | copy-start | bytes 589828
  21.4 11.2 %copy-start.7 = (bf16[6,128,256]{2,1,0:T(8,128)(2,1)}, bf16[6,128,256]{2,1,0:T(8,128)(2,1)S(1)}, u32[]{:S(2)}) copy-start(bf16[6,128,256]{2,1,0:T(8,128)(2,1)S(1)} %get-tuple-element.39.qb_ref) | copy-start | bytes 1179652
  21.4 11.2 %copy-start.9 = (bf16[6,128,256]{2,1,0:T(8,128)(2,1)}, bf16[6,128,256]{2,1,0:T(8,128)(2,1)S(1)}, u32[]{:S(2)}) copy-start(bf16[6,128,256]{2,1,0:T(8,128)(2,1)S(1)} %get-tuple-element.40.gb_ref) | copy-start | bytes 1179652
  21.5 1.7 %collective-permute-start.1 = (bf16[3,12,32,128]{3,2,1,0:T(8,128)(2,1)S(1)}, bf16[3,12,32,128]{3,2,1,0:T(8,128)(2,1)S(1)}, u32[]{:S(2)}, u32[]{:S(2)}) collective-permute-start(bf16[3,12,32,128]{3,2,1,0:T(8,128)(2,1)S(1)} %get-tuple-element.25), channel_id=1, source_target_pairs={{0,1},{1,0},{2,3},{3,2},{4,5},{5,4},{6,7},{7,6},{8,9},{9,8},{10,11... | collective-permute-start | bytes 884744 | tf_op jit(solution)/shard_map/ppermute | solution.py:307
  21.5 1.6 %collective-permute-start.2 = (f32[24,128]{1,0:T(8,128)S(1)}, f32[24,128]{1,0:T(8,128)S(1)}, u32[]{:S(2)}, u32[]{:S(2)}) collective-permute-start(f32[24,128]{1,0:T(8,128)S(1)} %get-tuple-element.26.stat_ref), channel_id=1, source_target_pairs={{0,1},{1,0},{2,3},{3,2},{4,5},{5,4},{6,7},{7,6},{8,9},{9,8},{10,11... | collective-permute-start | bytes 36872 | tf_op jit(solution)/shard_map/ppermute | solution.py:308
  23.6 6.2 %collective-permute-start.3 = (bf16[3,12,16,128]{3,2,1,0:T(8,128)(2,1)S(1)}, bf16[3,12,16,128]{3,2,1,0:T(8,128)(2,1)S(1)}, u32[]{:S(2)}, u32[]{:S(2)}) collective-permute-start(bf16[3,12,16,128]{3,2,1,0:T(8,128)(2,1)S(1)} %get-tuple-element.28), channel_id=1, source_target_pairs={{0,2},{1,3},{2,0},{3,1},{4,6},{5,7},{6,4},{7,5},{8,10},{9,11},{10,... | collective-permute-start | bytes 442376 | tf_op jit(solution)/shard_map/ppermute | solution.py:307
  25.4 4.5 %collective-permute-start.4 = (f32[24,128]{1,0:T(8,128)S(1)}, f32[24,128]{1,0:T(8,128)S(1)}, u32[]{:S(2)}, u32[]{:S(2)}) collective-permute-start(f32[24,128]{1,0:T(8,128)S(1)} %get-tuple-element.29.stat_ref), channel_id=1, source_target_pairs={{0,2},{1,3},{2,0},{3,1},{4,6},{5,7},{6,4},{7,5},{8,10},{9,11},{10,... | collective-permute-start | bytes 36872 | tf_op jit(solution)/shard_map/ppermute | solution.py:308
  30.9 5.5 %collective-permute-start.5 = (bf16[3,12,8,128]{3,2,1,0:T(8,128)(2,1)}, bf16[3,12,8,128]{3,2,1,0:T(8,128)(2,1)S(1)}, u32[]{:S(2)}, u32[]{:S(2)}) collective-permute-start(bf16[3,12,8,128]{3,2,1,0:T(8,128)(2,1)} %get-tuple-element.31), channel_id=1, source_target_pairs={{0,4},{1,5},{2,6},{3,7},{4,0},{5,1},{6,2},{7,3},{8,12},{9,13},{10,... | collective-permute-start | bytes 221192 | tf_op jit(solution)/shard_map/ppermute | solution.py:307
  32.6 3.7 %collective-permute-start.6 = (f32[24,128]{1,0:T(8,128)S(1)}, f32[24,128]{1,0:T(8,128)S(1)}, u32[]{:S(2)}, u32[]{:S(2)}) collective-permute-start(f32[24,128]{1,0:T(8,128)S(1)} %get-tuple-element.32.stat_ref), channel_id=1, source_target_pairs={{0,4},{1,5},{2,6},{3,7},{4,0},{5,1},{6,2},{7,3},{8,12},{9,13},{10,... | collective-permute-start | bytes 36872 | tf_op jit(solution)/shard_map/ppermute | solution.py:308
  36.6 5.6 %collective-permute-start.8 = (f32[24,128]{1,0:T(8,128)S(1)}, f32[24,128]{1,0:T(8,128)S(1)}, u32[]{:S(2)}, u32[]{:S(2)}) collective-permute-start(f32[24,128]{1,0:T(8,128)S(1)} %get-tuple-element.35.stat_ref), channel_id=1, source_target_pairs={{0,8},{1,9},{2,10},{3,11},{4,12},{5,13},{6,14},{7,15},{8,0},{9,1},... | collective-permute-start | bytes 36872 | tf_op jit(solution)/shard_map/ppermute | solution.py:308
  39.3 6.0 %collective-permute-start.7 = (bf16[3,12,8,128]{3,2,1,0:T(8,128)(2,1)S(1)}, bf16[3,12,8,128]{3,2,1,0:T(8,128)(2,1)S(1)}, u32[]{:S(2)}, u32[]{:S(2)}) collective-permute-start(bf16[3,12,8,128]{3,2,1,0:T(8,128)(2,1)S(1)} %get-tuple-element.34), channel_id=1, source_target_pairs={{0,8},{1,9},{2,10},{3,11},{4,12},{5,13},{6,14},{7,15},{8,0},{9,1},... | collective-permute-start | bytes 221192 | tf_op jit(solution)/shard_map/ppermute | solution.py:307
  39.6 7.6 %copy-start.8 = (bf16[6,128,256]{2,1,0:T(8,128)(2,1)S(1)}, bf16[6,128,256]{2,1,0:T(8,128)(2,1)}, u32[]{:S(2)}) copy-start(bf16[6,128,256]{2,1,0:T(8,128)(2,1)} %copy-done.7) | copy-start | bytes 1179652
  39.6 7.6 %copy-start.10 = (bf16[6,128,256]{2,1,0:T(8,128)(2,1)S(1)}, bf16[6,128,256]{2,1,0:T(8,128)(2,1)}, u32[]{:S(2)}) copy-start(bf16[6,128,256]{2,1,0:T(8,128)(2,1)} %copy-done.9) | copy-start | bytes 1179652
  45.7 6.7 %collective-permute-start.9 = (bf16[2,2,1536]{2,1,0:T(2,128)(2,1)S(1)}, bf16[2,2,1536]{2,1,0:T(2,128)(2,1)S(1)}, u32[]{:S(2)}, u32[]{:S(2)}) collective-permute-start(bf16[2,2,1536]{2,1,0:T(2,128)(2,1)S(1)} %get-tuple-element.37), channel_id=1, source_target_pairs={{0,16},{16,0},{1,17},{17,1},{2,18},{18,2},{3,19},{19,3},{4,20},{20... | collective-permute-start | bytes 36872 | tf_op jit(solution)/shard_map/ppermute | solution.py:335

commit v2 on v1

v2 whole, which is shorter than its diff:
```python
import functools
import math

import jax
import jax.numpy as jnp
from jax import lax
from jax.experimental import pallas as pl
from jax.experimental.pallas import tpu as pltpu
from jax.sharding import PartitionSpec as P


F32 = jnp.float32
BF16 = jnp.bfloat16
MIB = 1024 * 1024
VMEM = pl.BlockSpec(memory_space=pltpu.VMEM)
HBM = pl.BlockSpec(memory_space=pltpu.HBM)


def call(body, out_shape, vmem_mib, flops, **kwargs):
    return pl.pallas_call(
        body,
        out_shape=out_shape,
        compiler_params=pltpu.CompilerParams(vmem_limit_bytes=vmem_mib * MIB),
        cost_estimate=pl.CostEstimate(flops=flops, bytes_accessed=MIB, transcendentals=0),
        **kwargs,
    )


def nt(a, b):
    return lax.dot_general(a, b, (((1,), (1,)), ((), ())), preferred_element_type=F32)


def nn(a, b):
    return lax.dot_general(a, b, (((1,), (0,)), ((), ())), preferred_element_type=F32)


class Plan:
    def __init__(self, query_states, key_states, level_bias):
        self.query_ways = lax.axis_size("query")
        self.owner_ways = lax.axis_size("ctx")
        self.slots, self.features = key_states.shape
        self.heads = level_bias.shape[1] // self.query_ways
        self.head_size = self.features // self.heads
        self.scale = 1.0 / math.sqrt(self.head_size)
        self.own_rows = query_states.shape[0]
        self.rows = self.own_rows * self.query_ways
        self.part_rows = self.own_rows // self.owner_ways
        self.last_rows = self.part_rows * self.query_ways
        self.group = 2 if self.heads % 2 == 0 and self.rows <= 128 else 1
        self.groups = self.heads // self.group
        self.lanes = self.group * self.rows
        self.rounds = self.owner_ways.bit_length() - 1
        assert 1 << self.rounds == self.owner_ways and self.groups <= 8
        counts = [self.rows]
        for _ in range(self.rounds):
            half = counts[-1] // 2
            counts.append(half if half >= 8 else counts[-1])
        self.counts = counts
        self.packed = None
        if self.rounds and counts[-2] == counts[-1] == 8 and self.rows >> self.rounds == 4 and self.group == 2:
            self.packed = self.rounds - 1

    def split(self, k):
        return k < self.rounds and self.counts[k + 1] < self.counts[k]

    def sent_heads(self, k):
        return self.heads // 2 if k == self.packed else self.heads

    def bit(self, k):
        return (lax.axis_index("ctx") >> k) & 1

    def keep(self, k):
        return self.bit(k) * self.counts[k + 1] if self.split(k) else 0

    def give(self, k):
        return (1 - self.bit(k)) * self.counts[k + 1] if self.split(k) else 0

    def base(self, k):
        return sum((self.keep(j) for j in range(k)), 0)

    def last_offset(self):
        offset = 0
        for k in range(self.rounds):
            if not self.split(k) and k != self.packed:
                offset = offset + self.bit(k) * (self.rows >> (k + 1))
        return offset


def aligned(x, by):
    return pl.multiple_of(x, by) if by >= 8 and not isinstance(x, int) else x


def halves(first, second, upper):
    top = lax.broadcasted_iota(jnp.int32, first.shape, 0) < 4
    lower_rows = jnp.where(top, first, pltpu.roll(second, 4, 0))
    upper_rows = jnp.where(top, pltpu.roll(first, 4, 0), second)
    return jnp.where(upper == 1, upper_rows, lower_rows)


def load_body(plan, split_parts, *refs):
    count = 4 if split_parts else 2
    ins, outs, semaphores = refs[:count], refs[count : 2 * count], refs[2 * count]
    copies = []
    for n, (source, target) in enumerate(zip(ins, outs)):
        if n >= 2:
            start = pl.multiple_of(lax.axis_index("query") * plan.features, 128)
            source = source.at[:, pl.ds(start, plan.features)]
        copies.append(pltpu.make_async_copy(source, target, semaphores.at[n]))
    for copy in copies:
        copy.start()
    for copy in copies:
        copy.wait()


def forward_body(plan, split_parts, *refs):
    if split_parts:
        q_ref, g_ref, moved_ref = refs[:3]
        refs = refs[3:]
    else:
        moved_ref = refs[0]
        refs = refs[1:]
    (k_ref, v_ref, term_ref, part_ref, send_ref, stat_ref, pair_ref, qb_ref, gb_ref) = refs[:9]
    source, scores, dprobs, columns = refs[9:]
    rows, size, group = plan.rows, plan.head_size, plan.group
    width = group * size
    place = lax.broadcasted_iota(jnp.int32, (rows, rows), 0)
    column = lax.broadcasted_iota(jnp.int32, (rows, rows), 1)
    inner = place % plan.last_rows
    outer = place // plan.last_rows
    owner = jnp.zeros_like(outer)
    for k in range(plan.rounds):
        owner = owner | (((outer >> (plan.rounds - 1 - k)) & 1) << k)
    wanted = (
        inner // plan.part_rows * plan.own_rows + owner * plan.part_rows + inner % plan.part_rows
    )
    permute = (column == wanted).astype(F32).astype(BF16)
    qb_ref[...] = jnp.zeros_like(qb_ref)
    gb_ref[...] = jnp.zeros_like(gb_ref)
    for which, own_ref, block_ref in ((0, 0, qb_ref), (1, 1, gb_ref)):
        if split_parts:
            source[: plan.own_rows] = (q_ref, g_ref)[own_ref][...]
            source[plan.own_rows :] = moved_ref[which]
        else:
            source[...] = moved_ref[which]
        for p in range(plan.groups):
            ordered = nn(permute, source[:, p * width : (p + 1) * width]).astype(BF16)
            for q in range(group):
                block_ref[p, q * rows : (q + 1) * rows, q * size : (q + 1) * size] = ordered[
                    :, q * size : (q + 1) * size
                ]
    columns[...] = jnp.zeros_like(columns)
    step = 16
    for p in range(plan.groups):
        keys = k_ref[:, p * width : (p + 1) * width]
        values = v_ref[:, p * width : (p + 1) * width]
        scores[p % 2] = nt(qb_ref[p], keys)
        dprobs[p % 2] = nt(gb_ref[p], values)
        for r in range(0, plan.lanes, step):
            h = p * group + r // rows
            s = scores[p % 2, r : r + step] * plan.scale + term_ref[h : h + 1, :]
            top = jnp.max(s, axis=1, keepdims=True)
            e = jnp.exp(s - top)
            total = jnp.sum(e, axis=1, keepdims=True)
            d = dprobs[p % 2, r : r + step]
            mean = jnp.sum(e * d, axis=1, keepdims=True) / total
            pair_ref[p, r : r + step, :] = e.astype(BF16)
            pair_ref[p, plan.lanes + r : plan.lanes + r + step, :] = (e * (d - mean)).astype(BF16)
            columns[r : r + step, p : p + 1] = top
            columns[r : r + step, 8 + p : 9 + p] = total
            columns[r : r + step, 16 + p : 17 + p] = mean
        with_values = nn(pair_ref[p, : plan.lanes, :], values)
        with_keys = nn(pair_ref[p], keys)
        for q in range(group):
            at = slice(q * rows, (q + 1) * rows)
            of = slice(q * size, (q + 1) * size)
            part_ref[0, p * group + q] = with_values[at, of]
            part_ref[1, p * group + q] = with_keys[at, of]
            part_ref[2, p * group + q] = with_keys[plan.lanes + q * rows : plan.lanes + (q + 1) * rows, of]
    give(plan, 0, part_ref, send_ref)
    stat_ref[...] = columns[...].T[:24]


def statistics(stat_ref, stat_came_ref):
    top1, total1, mean1 = (stat_ref[8 * t : 8 * t + 8] for t in range(3))
    top2, total2, mean2 = (stat_came_ref[8 * t : 8 * t + 8] for t in range(3))
    top = jnp.maximum(top1, top2)
    f1 = jnp.exp(top1 - top)
    f2 = jnp.exp(top2 - top)
    total = f1 * total1 + f2 * total2
    inverse = 1.0 / jnp.where(total > 0.0, total, 1.0)
    w1 = f1 * total1 * inverse
    w2 = f2 * total2 * inverse
    gap = mean1 - mean2
    merged = (top, total, mean1 * w1 + mean2 * w2)
    return merged, (f1, f2, f1 * w2 * gap, -f2 * w1 * gap, inverse)


def merge_statistics_body(stat_ref, stat_came_ref, stat_new_ref):
    merged, _ = statistics(stat_ref, stat_came_ref)
    for t in range(3):
        stat_new_ref[8 * t : 8 * t + 8] = merged[t]


def merge_body(plan, k, part_ref, came_ref, stat_ref, stat_came_ref, *refs):
    last = k == plan.rounds - 1
    if last:
        own_ref, away_ref, table = refs if len(refs) == 3 else (None, *refs)
    else:
        part_new_ref, send_ref, table = refs
    _, factors = statistics(stat_ref, stat_came_ref)
    rest = jnp.zeros((128 - 40, plan.lanes), F32)
    table[...] = jnp.concatenate([*factors, rest], axis=0).T
    count = plan.counts[k + 1]
    kept = pl.ds(aligned(plan.keep(k), count), count)
    base = plan.base(k + 1)
    rows_of = [pl.ds(aligned(q * plan.rows + base, count), count) for q in range(plan.group)]
    packed = k == plan.packed
    bit = plan.bit(k)
    if packed:
        joined = halves(table[rows_of[0], :], table[rows_of[1], :], bit)
    for n in range(plan.sent_heads(k)):
        if packed:
            p = n
            mine = [halves(part_ref[a, 2 * n], part_ref[a, 2 * n + 1], bit) for a in range(3)]
            rows = joined
        else:
            p = n // plan.group
            mine = [part_ref[a, n, kept, :] for a in range(3)]
            rows = table[rows_of[n % plan.group], :]
        col = lambda t: rows[:, 8 * t + p : 8 * t + p + 1]
        out1, key1, dif1 = mine
        out2, key2, dif2 = (came_ref[a, n].astype(F32) for a in range(3))
        c1, c2 = col(0), col(1)
        out = c1 * out1 + c2 * out2
        dif = c1 * dif1 + c2 * dif2 + col(2) * key1 + col(3) * key2
        if not last:
            part_new_ref[0, n] = out
            part_new_ref[1, n] = c1 * key1 + c2 * key2
            part_new_ref[2, n] = dif
            continue
        share = col(4)
        for a, x in ((0, out * share), (1, dif * (share * plan.scale))):
            offset = plan.last_offset()
            if not isinstance(offset, int):
                x = pltpu.roll(x, (count - offset) % count, 0)
            for h, start in ((2 * n, 0), (2 * n + 1, 4)) if packed else ((n, 0),):
                of = slice(h * plan.head_size, (h + 1) * plan.head_size)
                middle, end = start + plan.part_rows, start + plan.last_rows
                if own_ref is not None:
                    own_ref[a, :, of] = x[start:middle].astype(BF16)
                    away_ref[a, :, of] = x[middle:end].astype(BF16)
                else:
                    away_ref[a, :, of] = x[start:end].astype(BF16)
    if not last:
        give(plan, k + 1, part_new_ref, send_ref)


def give(plan, k, part_ref, send_ref):
    if k == plan.packed:
        for a in range(3):
            for n in range(plan.heads // 2):
                x = halves(part_ref[a, 2 * n], part_ref[a, 2 * n + 1], 1 - plan.bit(k))
                send_ref[a, n] = x.astype(BF16)
        return
    count = plan.counts[k + 1]
    gone = pl.ds(aligned(plan.give(k), count), count)
    for a in range(3):
        for h in range(plan.heads):
            send_ref[a, h] = part_ref[a, h, gone, :].astype(BF16)


def turn_body(pair_ref, turned_ref):
    for p in range(pair_ref.shape[0]):
        turned_ref[p] = pair_ref[p].T


def backward_body(plan, stat_ref, stat_all_ref, qb_ref, gb_ref, turned_ref, dk_ref, dv_ref, table, dk, dv, semaphores):
    lanes = plan.lanes
    width = dk.shape[2]
    total = stat_all_ref[8:16]
    inverse = 1.0 / jnp.where(total > 0.0, total, 1.0)
    f = jnp.exp(stat_ref[0:8] - stat_all_ref[0:8]) * inverse
    c = f * (stat_ref[16:24] - stat_all_ref[16:24])
    rest = jnp.zeros((128 - 24, lanes), F32)
    table[...] = jnp.concatenate([f, f * plan.scale, c * plan.scale, rest], axis=0).T
    copies = []
    for p in range(plan.groups):
        queries = qb_ref[p].astype(F32)
        wv = (gb_ref[p].astype(F32) * table[:, p : p + 1]).astype(BF16)
        wc = (queries * table[:, 16 + p : 17 + p]).astype(BF16)
        wf = (queries * table[:, 8 + p : 9 + p]).astype(BF16)
        for n, (buffer, target) in enumerate(((dk, dk_ref), (dv, dv_ref))):
            if n == 0:
                buffer[p] = nn(turned_ref[p], jnp.concatenate([wc, wf], axis=0)).astype(BF16)
            else:
                buffer[p] = nn(turned_ref[p, :, :lanes], wv).astype(BF16)
            copy = pltpu.make_async_copy(
                buffer.at[p], target.at[:, p * width : (p + 1) * width], semaphores.at[n, p]
            )
            copy.start()
            copies.append(copy)
    for copy in copies:
        copy.wait()


def local(query_states, key_states, value_states, level_ids, level_bias, live_counts, out_grad):
    plan = Plan(query_states, key_states, level_bias)
    qi = lax.axis_index("query")
    size, slots, lanes, groups, heads = plan.head_size, plan.slots, plan.lanes, plan.groups, plan.heads
    width = plan.group * size
    pairwise = plan.query_ways == 2
    both = jnp.stack([query_states, out_grad])
    if pairwise:
        theirs = lax.dynamic_slice_in_dim(both, (1 - qi) * plan.features, plan.features, 2)
        moved = lax.ppermute(theirs, "query", [(0, 1), (1, 0)])
    else:
        moved = lax.all_to_all(both, "query", split_axis=2, concat_axis=1, tiled=True)
    table = lax.dynamic_slice_in_dim(level_bias, qi * heads, heads, 1)
    term = jnp.zeros((heads, slots), F32)
    for level in range(level_bias.shape[0]):
        term = jnp.where(level_ids[None, :] == level, table[level][:, None], term)
    slot = lax.broadcasted_iota(jnp.int32, (1, slots), 1)
    term = jnp.where(slot < live_counts[0], term, -1e30)

    stat_shape = jax.ShapeDtypeStruct((24, lanes), F32)
    block_shape = jax.ShapeDtypeStruct((groups, lanes, width), BF16)
    part_shape = lambda k: jax.ShapeDtypeStruct((3, heads, plan.counts[k], size), F32)
    send_shape = lambda k: jax.ShapeDtypeStruct(
        (3, plan.sent_heads(k), plan.counts[k + 1], size), BF16
    )
    from_hbm = [key_states, value_states] + ([query_states, out_grad] if pairwise else [])
    from_hbm = [pltpu.with_memory_space_constraint(x, pltpu.HBM) for x in from_hbm]
    own_shape = jax.ShapeDtypeStruct((plan.own_rows, plan.features), BF16)
    context_shape = jax.ShapeDtypeStruct(key_states.shape, BF16)
    keys, values, *own_rows = call(
        functools.partial(load_body, plan, pairwise),
        [context_shape] * 2 + [own_shape] * (len(from_hbm) - 2),
        2,
        10**9,
        in_specs=[HBM] * len(from_hbm),
        out_specs=[VMEM] * len(from_hbm),
        scratch_shapes=[pltpu.SemaphoreType.DMA((len(from_hbm),))],
        name="load",
    )(*from_hbm)
    part, send, stat_own, pair, qb, gb = call(
        functools.partial(forward_body, plan, pairwise),
        (
            part_shape(0),
            send_shape(0),
            stat_shape,
            jax.ShapeDtypeStruct((groups, 2 * lanes, slots), BF16),
            block_shape,
            block_shape,
        ),
        12,
        4 * 10**9,
        in_specs=[VMEM] * (len(own_rows) + 4),
        out_specs=[VMEM] * 6,
        scratch_shapes=[
            pltpu.VMEM((plan.rows, plan.features), BF16),
            pltpu.VMEM((2, lanes, slots), F32),
            pltpu.VMEM((2, lanes, slots), F32),
            pltpu.VMEM((lanes, 128), F32),
        ],
        name="forward",
    )(*own_rows, moved, keys, values, term)

    turned = call(
        turn_body,
        jax.ShapeDtypeStruct((groups, slots, 2 * lanes), BF16),
        4,
        10**9,
        in_specs=[VMEM],
        out_specs=VMEM,
        name="turn",
    )(pair)

    stat = stat_own
    for k in range(plan.rounds):
        swap = [(i, i ^ (1 << k)) for i in range(plan.owner_ways)]
        stat_came = lax.ppermute(stat, "ctx", swap)
        came = lax.ppermute(send, "ctx", swap)
        merged = call(
            merge_statistics_body,
            stat_shape,
            2,
            10**6,
            in_specs=[VMEM] * 2,
            out_specs=VMEM,
            name=f"statistics{k}",
        )(stat, stat_came)
        if k < plan.rounds - 1:
            outs = (part_shape(k + 1), send_shape(k + 1))
        elif pairwise:
            outs = (jax.ShapeDtypeStruct((2, plan.part_rows, plan.features), BF16),) * 2
        else:
            outs = (jax.ShapeDtypeStruct((2, plan.last_rows, plan.features), BF16),)
        part, send, *_ = call(
            functools.partial(merge_body, plan, k),
            outs,
            4,
            10**8,
            in_specs=[VMEM] * 4,
            out_specs=[VMEM] * len(outs),
            scratch_shapes=[pltpu.VMEM((lanes, 128), F32)],
            name=f"merge{k}",
        )(part, came, stat, stat_came) + (None,) * (2 - len(outs))
        stat = merged
    if pairwise:
        own, away = part, send
        back = lax.ppermute(away, "query", [(0, 1), (1, 0)])

    key_grad, value_grad = call(
        functools.partial(backward_body, plan),
        (context_shape, context_shape),
        12,
        4 * 10**9,
        in_specs=[VMEM] * 5,
        out_specs=[HBM] * 2,
        scratch_shapes=[
            pltpu.VMEM((lanes, 128), F32),
            pltpu.VMEM((groups, slots, width), BF16),
            pltpu.VMEM((groups, slots, width), BF16),
            pltpu.SemaphoreType.DMA((2, groups)),
        ],
        name="backward",
    )(stat_own, stat, qb, gb, turned)

    if pairwise:
        first = jnp.where(qi == 0, own, back)
        second = jnp.where(qi == 0, back, own)
        final = jnp.concatenate([first, second], axis=2)
    else:
        final = lax.all_to_all(part, "query", split_axis=1, concat_axis=2, tiled=True)
    return final[0], final[1], key_grad, value_grad


def solution(mesh):
    placed = (
        P("query", None),
        P("ctx", "query"),
        P("ctx", "query"),
        P("ctx"),
        P(),
        P("ctx"),
        P("query", None),
    )

    return jax.shard_map(
        local,
        mesh=mesh,
        in_specs=placed,
        out_specs=(
            P(("query", "ctx"), None),
            P(("query", "ctx"), None),
            P("ctx", "query"),
            P("ctx", "query"),
        ),
        check_vma=False,
    )
```

time: 53.3 us -> 44.9 us (0.84)
  local copies, waits for them, and re-layouts: 7.35 us -> 1.72 us
  waiting for transfers between devices: 16.9 us -> 12.7 us
  Pallas kernels: 12.7 us -> 13.9 us
    unnamed x22 -> x14, local copies, waits for them, and re-layouts: 7.26 us -> 1.63 us
    ppermute x1, waiting for transfers between devices: 3.35 us -> 0.46 us  [local(): moved = lax.ppermute(theirs, 'query', [(0, 1), (1, 0)])]
    ppermute x4, waiting for transfers between devices: 10.4 us -> 9.03 us  [local(): stat_came = lax.ppermute(stat, 'ctx', swap)]
    pallas_call x6 -> x11, Pallas kernels: 8.05 us -> 9.27 us  [the longest x1 3.4 us: local(): call(functools.partial(backward_body, plan), (context_shape, context_shap...]
  transfers between devices with their start and end apart: 10 -> 10, of which waited for: 6 -> 6; matrix products, arithmetic and copies ran while one was open for 2% -> 2% of each run, Pallas kernels for 11% -> 17%
where the time goes in v2:
time: 44.9 us; the launch traced here: 44.6 us
  Pallas kernels  13.9 us (31%)
  waiting for transfers between devices  12.7 us (28%)
  starting transfers between devices  12.5 us (28%)
  other arithmetic  2.4 us (5%)
  local copies, waits for them, and re-layouts  1.72 us (4%)
  between operations  1.43 us (3%)
    ppermute x4, waiting for transfers between devices, local(): stat_came = lax.ppermute(stat, 'ctx', swap)  9.03 us
    pallas_call x1, Pallas kernels, local(): call(functools.partial(forward_body, plan, pairwise), (part_shape(0), sen...  4.62 us
    ppermute x4, starting transfers between devices, local(): came = lax.ppermute(send, 'ctx', swap)  4.01 us
    ppermute x4, starting transfers between devices, local(): stat_came = lax.ppermute(stat, 'ctx', swap)  3.86 us
    pallas_call x1, Pallas kernels, local(): call(functools.partial(backward_body, plan), (context_shape, context_shap...  3.4 us
    ppermute x4, waiting for transfers between devices, local(): came = lax.ppermute(send, 'ctx', swap)  3.2 us
    ppermute x1, starting transfers between devices, local(): moved = lax.ppermute(theirs, 'query', [(0, 1), (1, 0)])  3.06 us
    pallas_call x1, Pallas kernels, local(): call(functools.partial(load_body, plan, pairwise), [context_shape] * 2 +...  2.88 us
  transfers between devices with their start and end apart: 10, of which 6 were waited for; matrix products, arithmetic and copies ran while one was open for 2% of the time, Pallas kernels for 17%

profile of v2, /device:TPU:0, one launch (start us, length us, event | category | flops | bytes accessed | tf_op | source)
XLA Modules:
  0.0 44.6 jit_solution(15800382292595062781)
XLA Ops:
  0.6 0.0 copy-start
  0.7 1.0 %fusion = bf16[2,32,1536]{2,1,0:T(8,128)(2,1)S(1)} fusion(s32[]{:T(128)S(6)} %select_n.39, bf16[1,32,3072]{2,1,0:T(8,128)(2,1)} %bitcast.18, bf16[1,32,3072]{2,1,0:T(8,128)(2,1)} %bitcast.19), kind=kLoop, calls=%fused_computation.2 | loop fusion | flops 393216 | bytes 589828 | tf_op jit(solution)/shard_map/stack | solution.py:312
  1.6 3.1 %collective-permute-start = (bf16[2,32,1536]{2,1,0:T(8,128)(2,1)S(1)}, bf16[2,32,1536]{2,1,0:T(8,128)(2,1)S(1)}, u32[]{:S(2)}, u32[]{:S(2)}) collective-permute-start(bf16[2,32,1536]{2,1,0:T(8,128)(2,1)S(1)} %fusion), channel_id=1, source_target_pairs={{0,16},{16,0},{1,17},{17,1},{2,18},{18,2},{3,19},{19,3},{4,20},{20... | collective-permute-start | bytes 589832 | tf_op jit(solution)/shard_map/ppermute | solution.py:315
  5.3 0.0 copy-done
  5.3 0.1 constant_dynamic-slice_fusion
  5.4 0.7 %broadcast_compare_fusion.4 = (pred[1024]{0:T(1024)(128)(4,1)S(1)}, pred[1024]{0:T(1024)(128)(4,1)S(1)}, pred[1024]{0:T(1024)(128)(4,1)S(1)}, pred[1024]{0:T(1024)(128)(4,1)S(1)}, pred[1024]{0:T(1024)(128)(4,1)S(1)}) fusion(s32[1024]{0:T(1024)} %param.10), kind=kLoop, calls=%fused_computation.17 | loop fusion | flops 5120 | bytes 9216 | tf_op jit(solution)/shard_map/eq | solution.py:321
  6.1 2.9 %load.1 = (bf16[1024,1536]{1,0:T(8,128)(2,1)S(1)}, bf16[1024,1536]{1,0:T(8,128)(2,1)S(1)}, bf16[32,1536]{1,0:T(8,128)(2,1)S(1)}, bf16[32,1536]{1,0:T(8,128)(2,1)S(1)}) custom-call(bf16[1024,1536]{1,0:T(8,128)(2,1)} %refs_0_.1, bf16[1024,1536]{1,0:T(8,128)(2,1)} %refs_1_.1, bf16[32,3072]{1,0:T(8,128)(2,1)} %refs_2_.1, bf16[32,3072]{1,0:T(8,128)(2,1)} %refs_3_.1), custom_call_target="tpu_custom_call" | custom-call | flops 1000000000 | bytes 1048576 | tf_op jit(solution)/shard_map/load/pallas_call | solution.py:335
  9.0 0.1 select_select_fusion.refs_5_
  9.1 0.5 %collective-permute-done.refs_2_ = bf16[2,32,1536]{2,1,0:T(8,128)(2,1)S(1)} collective-permute-done((bf16[2,32,1536]{2,1,0:T(8,128)(2,1)S(1)}, bf16[2,32,1536]{2,1,0:T(8,128)(2,1)S(1)}, u32[]{:S(2)}, u32[]{:S(2)}) %collective-permute-start) | collective-permute-done | bytes 196640 | tf_op jit(solution)/shard_map/ppermute | solution.py:315
  9.6 0.0 copy-start.1
  9.6 0.7 %copy-done.1 = bf16[2,32,1536]{2,1,0:T(8,128)(2,1)} copy-done((bf16[2,32,1536]{2,1,0:T(8,128)(2,1)}, bf16[2,32,1536]{2,1,0:T(8,128)(2,1)S(1)}, u32[]{:S(2)}) %copy-start.1) | copy-done | bytes 196632
  10.3 0.0 copy-start.2
  10.3 0.9 %copy-done.2 = bf16[2,32,1536]{2,1,0:T(8,128)(2,1)S(1)} copy-done((bf16[2,32,1536]{2,1,0:T(8,128)(2,1)S(1)}, bf16[2,32,1536]{2,1,0:T(8,128)(2,1)}, u32[]{:S(2)}) %copy-start.2) | copy-done | bytes 196632
  11.2 4.6 %forward.1 = (f32[3,12,64,128]{3,2,1,0:T(8,128)S(1)}, bf16[3,12,32,128]{3,2,1,0:T(8,128)(2,1)S(1)}, f32[24,128]{1,0:T(8,128)S(1)}, bf16[6,256,1024]{2,1,0:T(8,12...) custom-call(bf16[32,1536]{1,0:T(8,128)(2,1)S(1)} %get-tuple-element.24.refs_0_, ...), custom_call_target="tpu_custom_call" | custom-call | flops 4000000000 | bytes 1048576 | tf_op jit(solution)/shard_map/forward/pallas_call | solution.py:345
  15.8 0.0 copy-start.3
  15.8 0.0 copy-start.5
  15.8 0.1 collective-permute-start.1
  15.9 0.5 %collective-permute-start.2 = (f32[24,128]{1,0:T(8,128)S(1)}, f32[24,128]{1,0:T(8,128)S(1)}, u32[]{:S(2)}, u32[]{:S(2)}) collective-permute-start(f32[24,128]{1,0:T(8,128)S(1)} %get-tuple-element.30.stat_ref), channel_id=1, source_target_pairs={{0,1},{1,0},{2,3},{3,2},{4,5},{5,4},{6,7},{7,6},{8,9},{9,8},{10,11... | collective-permute-start | bytes 36872 | tf_op jit(solution)/shard_map/ppermute | solution.py:381
  16.4 1.1 %collective-permute-done.2.stat_came_ref = f32[24,128]{1,0:T(8,128)S(1)} collective-permute-done((f32[24,128]{1,0:T(8,128)S(1)}, f32[24,128]{1,0:T(8,128)S(1)}, u32[]{:S(2)}, u32[]{:S(2)}) %collective-permute-start.2) | collective-permute-done | bytes 12320 | tf_op jit(solution)/shard_map/ppermute | solution.py:381
  17.5 0.0 collective-permute-done.1.came_ref
  17.5 0.5 %merge0.1 = (f32[3,12,32,128]{3,2,1,0:T(8,128)S(1)}, bf16[3,12,16,128]{3,2,1,0:T(8,128)(2,1)S(1)}) custom-call(f32[3,12,64,128]{3,2,1,0:T(8,128)S(1)} %get-tuple-element.28.part_ref, bf16[3,12,32,128]{3,2,1,0:T(8,128)(2,1)S(1)} %collective-permute-done.1.came_ref, f32[24,128]{1,0:T(8,128)S(1)} %get-tuple-element.30.stat_ref, ...), custom_call_target="tpu_custom_call" | custom-call | flops 100000000 | bytes 1048576 | tf_op jit(solution)/shard_map/merge0/pallas_call | solution.py:398
  18.0 1.8 %collective-permute-start.3 = (bf16[3,12,16,128]{3,2,1,0:T(8,128)(2,1)S(1)}, bf16[3,12,16,128]{3,2,1,0:T(8,128)(2,1)S(1)}, u32[]{:S(2)}, u32[]{:S(2)}) collective-permute-start(bf16[3,12,16,128]{3,2,1,0:T(8,128)(2,1)S(1)} %get-tuple-element.32), channel_id=1, source_target_pairs={{0,2},{1,3},{2,0},{3,1},{4,6},{5,7},{6,4},{7,5},{8,10},{9,11},{10,... | collective-permute-start | bytes 442376 | tf_op jit(solution)/shard_map/ppermute | solution.py:382
  19.8 0.4 collective-permute-start.4
  20.2 4.1 %collective-permute-done.4.stat_came_ref = f32[24,128]{1,0:T(8,128)S(1)} collective-permute-done((f32[24,128]{1,0:T(8,128)S(1)}, f32[24,128]{1,0:T(8,128)S(1)}, u32[]{:S(2)}, u32[]{:S(2)}) %collective-permute-start.4) | collective-permute-done | bytes 12320 | tf_op jit(solution)/shard_map/ppermute | solution.py:381
  24.2 0.0 collective-permute-done.3.came_ref
  24.2 1.0 %merge1.1 = (f32[3,12,16,128]{3,2,1,0:T(8,128)S(1)}, bf16[3,12,8,128]{3,2,1,0:T(8,128)(2,1)}) custom-call(f32[3,12,32,128]{3,2,1,0:T(8,128)S(1)} %get-tuple-element.31.part_ref, bf16[3,12,16,128]{3,2,1,0:T(8,128)(2,1)S(1)} %collective-permute-done.3.came_ref, f32[24,128]{1,0:T(8,128)S(1)} %statistics0.1.stat_ref, ...), custom_call_target="tpu_custom_call" | custom-call | flops 100000000 | bytes 1048576 | tf_op jit(solution)/shard_map/merge1/pallas_call | solution.py:398
  25.2 1.8 %collective-permute-start.5 = (bf16[3,12,8,128]{3,2,1,0:T(8,128)(2,1)}, bf16[3,12,8,128]{3,2,1,0:T(8,128)(2,1)S(1)}, u32[]{:S(2)}, u32[]{:S(2)}) collective-permute-start(bf16[3,12,8,128]{3,2,1,0:T(8,128)(2,1)} %get-tuple-element.34), channel_id=1, source_target_pairs={{0,4},{1,5},{2,6},{3,7},{4,0},{5,1},{6,2},{7,3},{8,12},{9,13},{10,... | collective-permute-start | bytes 221192 | tf_op jit(solution)/shard_map/ppermute | solution.py:382
  27.0 0.0 copy-done.3
  27.0 0.0 copy-done.5
  27.1 0.3 collective-permute-start.6
  27.4 3.4 %collective-permute-done.6.stat_came_ref = f32[24,128]{1,0:T(8,128)S(1)} collective-permute-done((f32[24,128]{1,0:T(8,128)S(1)}, f32[24,128]{1,0:T(8,128)S(1)}, u32[]{:S(2)}, u32[]{:S(2)}) %collective-permute-start.6) | collective-permute-done | bytes 12320 | tf_op jit(solution)/shard_map/ppermute | solution.py:381
  30.8 2.6 %collective-permute-start.8 = (f32[24,128]{1,0:T(8,128)S(1)}, f32[24,128]{1,0:T(8,128)S(1)}, u32[]{:S(2)}, u32[]{:S(2)}) collective-permute-start(f32[24,128]{1,0:T(8,128)S(1)} %statistics2.1.stat_ref), channel_id=1, source_target_pairs={{0,8},{1,9},{2,10},{3,11},{4,12},{5,13},{6,14},{7,15},{8,0},{9,1},... | collective-permute-start | bytes 36872 | tf_op jit(solution)/shard_map/ppermute | solution.py:381
  33.5 0.0 collective-permute-done.5.came_ref
  33.5 0.3 merge2.1
  33.8 0.4 collective-permute-start.7
  34.2 0.0 copy-start.4
  34.2 0.0 copy-start.6
  34.2 0.9 %turn.1.turned_ref = bf16[6,1024,256]{2,1,0:T(8,128)(2,1)S(1)} custom-call(bf16[6,256,1024]{2,1,0:T(8,128)(2,1)S(1)} %get-tuple-element.41.pair_ref), custom_call_target="tpu_custom_call" | custom-call | flops 1000000000 | bytes 1048576 | tf_op jit(solution)/shard_map/turn/pallas_call | solution.py:368
  35.0 0.4 collective-permute-done.8.stat_came_ref
  35.5 3.2 %collective-permute-done.7.came_ref = bf16[3,6,8,128]{3,2,1,0:T(8,128)(2,1)S(1)} collective-permute-done((bf16[3,6,8,128]{3,2,1,0:T(8,128)(2,1)S(1)}, bf16[3,6,8,128]{3,2,1,0:T(8,128)(2,1)S(1)}, u32[]{:S(2)}, u32[]{:S(2)}) %collective-permute-start.7) | collective-permute-done | bytes 36896 | tf_op jit(solution)/shard_map/ppermute | solution.py:382
  38.7 0.3 merge3.1
  39.0 1.6 %collective-permute-start.9 = (bf16[2,2,1536]{2,1,0:T(2,128)(2,1)S(1)}, bf16[2,2,1536]{2,1,0:T(2,128)(2,1)S(1)}, u32[]{:S(2)}, u32[]{:S(2)}) collective-permute-start(bf16[2,2,1536]{2,1,0:T(2,128)(2,1)S(1)} %get-tuple-element.38), channel_id=1, source_target_pairs={{0,16},{16,0},{1,17},{17,1},{2,18},{18,2},{3,19},{19,3},{4,20},{20... | collective-permute-start | bytes 36872 | tf_op jit(solution)/shard_map/ppermute | solution.py:411
  40.6 0.0 copy-done.4
  40.6 0.0 copy-done.6
  40.6 3.4 %backward.1 = (bf16[1024,1536]{1,0:T(8,128)(2,1)}, bf16[1024,1536]{1,0:T(8,128)(2,1)}) custom-call(f32[24,128]{1,0:T(8,128)S(1)} %get-tuple-element.30.stat_ref, f32[24,128]{1,0:T(8,128)S(1)} %statistics3.1.stat_all_ref, bf16[6,128,256]{2,1,0:T(8,128)(2,1)S(1)} %copy-done.4, bf16[6,128,256]{2,1,0:T(8,128)(2,1)S(1)} %copy-done.6, ...), custom_call_target="tpu_custom_call" | custom-call | flops 4000000000 | bytes 1048576 | tf_op jit(solution)/shard_map/backward/pallas_call | solution.py:413
  44.0 0.0 collective-permute-done.9
  44.0 0.6 %fusion.2 = (bf16[2,3072]{1,0:T(2,128)(2,1)}, bf16[2,3072]{1,0:T(2,128)(2,1)}) fusion(bf16[2,2,1536]{2,1,0:T(2,128)(2,1)S(1)} %get-tuple-element.47, bf16[2,2,1536]{2,1,0:T(2,128)(2,1)S(1)} %get-tuple-element.46), kind=kLoop, calls=%fused_computation.10 | loop fusion | flops 49152 | bytes 49152 | tf_op jit(solution)/shard_map/squeeze | solution.py:435
  (7 shorter events, 0.1 us)
Async XLA Ops:
  0.6 4.7 %copy-start = (f32[5,24]{1,0:T(8,128)S(1)}, f32[5,24]{1,0:T(8,128)}, u32[]{:S(2)}) copy-start(f32[5,24]{1,0:T(8,128)} %param.11) | copy-start | bytes 1444
  1.6 8.0 %collective-permute-start = (bf16[2,32,1536]{2,1,0:T(8,128)(2,1)S(1)}, bf16[2,32,1536]{2,1,0:T(8,128)(2,1)S(1)}, u32[]{:S(2)}, u32[]{:S(2)}) collective-permute-start(bf16[2,32,1536]{2,1,0:T(8,128)(2,1)S(1)} %fusion), channel_id=1, source_target_pairs={{0,16},{16,0},{1,17},{17,1},{2,18},{18,2},{3,19},{19,3},{4,20},{20... | collective-permute-start | bytes 589832 | tf_op jit(solution)/shard_map/ppermute | solution.py:315
  9.6 0.7 %copy-start.1 = (bf16[2,32,1536]{2,1,0:T(8,128)(2,1)}, bf16[2,32,1536]{2,1,0:T(8,128)(2,1)S(1)}, u32[]{:S(2)}) copy-start(bf16[2,32,1536]{2,1,0:T(8,128)(2,1)S(1)} %collective-permute-done.refs_2_) | copy-start | bytes 589828
  10.3 0.9 %copy-start.2 = (bf16[2,32,1536]{2,1,0:T(8,128)(2,1)S(1)}, bf16[2,32,1536]{2,1,0:T(8,128)(2,1)}, u32[]{:S(2)}) copy-start(bf16[2,32,1536]{2,1,0:T(8,128)(2,1)} %copy-done.1) | copy-start | bytes 589828
  15.8 11.2 %copy-start.3 = (bf16[6,128,256]{2,1,0:T(8,128)(2,1)}, bf16[6,128,256]{2,1,0:T(8,128)(2,1)S(1)}, u32[]{:S(2)}) copy-start(bf16[6,128,256]{2,1,0:T(8,128)(2,1)S(1)} %get-tuple-element.39.qb_ref) | copy-start | bytes 1179652
  15.8 11.2 %copy-start.5 = (bf16[6,128,256]{2,1,0:T(8,128)(2,1)}, bf16[6,128,256]{2,1,0:T(8,128)(2,1)S(1)}, u32[]{:S(2)}) copy-start(bf16[6,128,256]{2,1,0:T(8,128)(2,1)S(1)} %get-tuple-element.40.gb_ref) | copy-start | bytes 1179652
  15.8 1.7 %collective-permute-start.1 = (bf16[3,12,32,128]{3,2,1,0:T(8,128)(2,1)S(1)}, bf16[3,12,32,128]{3,2,1,0:T(8,128)(2,1)S(1)}, u32[]{:S(2)}, u32[]{:S(2)}) collective-permute-start(bf16[3,12,32,128]{3,2,1,0:T(8,128)(2,1)S(1)} %get-tuple-element.29), channel_id=1, source_target_pairs={{0,1},{1,0},{2,3},{3,2},{4,5},{5,4},{6,7},{7,6},{8,9},{9,8},{10,11... | collective-permute-start | bytes 884744 | tf_op jit(solution)/shard_map/ppermute | solution.py:382
  15.9 1.6 %collective-permute-start.2 = (f32[24,128]{1,0:T(8,128)S(1)}, f32[24,128]{1,0:T(8,128)S(1)}, u32[]{:S(2)}, u32[]{:S(2)}) collective-permute-start(f32[24,128]{1,0:T(8,128)S(1)} %get-tuple-element.30.stat_ref), channel_id=1, source_target_pairs={{0,1},{1,0},{2,3},{3,2},{4,5},{5,4},{6,7},{7,6},{8,9},{9,8},{10,11... | collective-permute-start | bytes 36872 | tf_op jit(solution)/shard_map/ppermute | solution.py:381
  18.0 6.2 %collective-permute-start.3 = (bf16[3,12,16,128]{3,2,1,0:T(8,128)(2,1)S(1)}, bf16[3,12,16,128]{3,2,1,0:T(8,128)(2,1)S(1)}, u32[]{:S(2)}, u32[]{:S(2)}) collective-permute-start(bf16[3,12,16,128]{3,2,1,0:T(8,128)(2,1)S(1)} %get-tuple-element.32), channel_id=1, source_target_pairs={{0,2},{1,3},{2,0},{3,1},{4,6},{5,7},{6,4},{7,5},{8,10},{9,11},{10,... | collective-permute-start | bytes 442376 | tf_op jit(solution)/shard_map/ppermute | solution.py:382
  19.8 4.5 %collective-permute-start.4 = (f32[24,128]{1,0:T(8,128)S(1)}, f32[24,128]{1,0:T(8,128)S(1)}, u32[]{:S(2)}, u32[]{:S(2)}) collective-permute-start(f32[24,128]{1,0:T(8,128)S(1)} %statistics0.1.stat_ref), channel_id=1, source_target_pairs={{0,2},{1,3},{2,0},{3,1},{4,6},{5,7},{6,4},{7,5},{8,10},{9,11},{10,... | collective-permute-start | bytes 36872 | tf_op jit(solution)/shard_map/ppermute | solution.py:381
  25.2 8.2 %collective-permute-start.5 = (bf16[3,12,8,128]{3,2,1,0:T(8,128)(2,1)}, bf16[3,12,8,128]{3,2,1,0:T(8,128)(2,1)S(1)}, u32[]{:S(2)}, u32[]{:S(2)}) collective-permute-start(bf16[3,12,8,128]{3,2,1,0:T(8,128)(2,1)} %get-tuple-element.34), channel_id=1, source_target_pairs={{0,4},{1,5},{2,6},{3,7},{4,0},{5,1},{6,2},{7,3},{8,12},{9,13},{10,... | collective-permute-start | bytes 221192 | tf_op jit(solution)/shard_map/ppermute | solution.py:382
  27.1 3.8 %collective-permute-start.6 = (f32[24,128]{1,0:T(8,128)S(1)}, f32[24,128]{1,0:T(8,128)S(1)}, u32[]{:S(2)}, u32[]{:S(2)}) collective-permute-start(f32[24,128]{1,0:T(8,128)S(1)} %statistics1.1.stat_ref), channel_id=1, source_target_pairs={{0,4},{1,5},{2,6},{3,7},{4,0},{5,1},{6,2},{7,3},{8,12},{9,13},{10,... | collective-permute-start | bytes 36872 | tf_op jit(solution)/shard_map/ppermute | solution.py:381
  30.8 4.7 %collective-permute-start.8 = (f32[24,128]{1,0:T(8,128)S(1)}, f32[24,128]{1,0:T(8,128)S(1)}, u32[]{:S(2)}, u32[]{:S(2)}) collective-permute-start(f32[24,128]{1,0:T(8,128)S(1)} %statistics2.1.stat_ref), channel_id=1, source_target_pairs={{0,8},{1,9},{2,10},{3,11},{4,12},{5,13},{6,14},{7,15},{8,0},{9,1},... | collective-permute-start | bytes 36872 | tf_op jit(solution)/shard_map/ppermute | solution.py:381
  33.8 4.9 %collective-permute-start.7 = (bf16[3,6,8,128]{3,2,1,0:T(8,128)(2,1)S(1)}, bf16[3,6,8,128]{3,2,1,0:T(8,128)(2,1)S(1)}, u32[]{:S(2)}, u32[]{:S(2)}) collective-permute-start(bf16[3,6,8,128]{3,2,1,0:T(8,128)(2,1)S(1)} %get-tuple-element.36), channel_id=1, source_target_pairs={{0,8},{1,9},{2,10},{3,11},{4,12},{5,13},{6,14},{7,15},{8,0},{9,1},... | collective-permute-start | bytes 110600 | tf_op jit(solution)/shard_map/ppermute | solution.py:382
  34.2 6.4 %copy-start.4 = (bf16[6,128,256]{2,1,0:T(8,128)(2,1)S(1)}, bf16[6,128,256]{2,1,0:T(8,128)(2,1)}, u32[]{:S(2)}) copy-start(bf16[6,128,256]{2,1,0:T(8,128)(2,1)} %copy-done.3) | copy-start | bytes 1179652
  34.2 6.4 %copy-start.6 = (bf16[6,128,256]{2,1,0:T(8,128)(2,1)S(1)}, bf16[6,128,256]{2,1,0:T(8,128)(2,1)}, u32[]{:S(2)}) copy-start(bf16[6,128,256]{2,1,0:T(8,128)(2,1)} %copy-done.5) | copy-start | bytes 1179652
  39.0 5.0 %collective-permute-start.9 = (bf16[2,2,1536]{2,1,0:T(2,128)(2,1)S(1)}, bf16[2,2,1536]{2,1,0:T(2,128)(2,1)S(1)}, u32[]{:S(2)}, u32[]{:S(2)}) collective-permute-start(bf16[2,2,1536]{2,1,0:T(2,128)(2,1)S(1)} %get-tuple-element.38), channel_id=1, source_target_pairs={{0,16},{16,0},{1,17},{17,1},{2,18},{18,2},{3,19},{19,3},{4,20},{20... | collective-permute-start | bytes 36872 | tf_op jit(solution)/shard_map/ppermute | solution.py:411

commit v3 on v2

--- a/solution.py
+++ b/solution.py
@@ -56,15 +56,10 @@
             half = counts[-1] // 2
             counts.append(half if half >= 8 else counts[-1])
         self.counts = counts
-        self.packed = None
-        if self.rounds and counts[-2] == counts[-1] == 8 and self.rows >> self.rounds == 4 and self.group == 2:
-            self.packed = self.rounds - 1
+        self.direct = self.query_ways == 2 and self.rounds >= 3 and counts[-2] == 2 * self.last_rows >= 8
 
     def split(self, k):
         return k < self.rounds and self.counts[k + 1] < self.counts[k]
-
-    def sent_heads(self, k):
-        return self.heads // 2 if k == self.packed else self.heads
 
     def bit(self, k):
         return (lax.axis_index("ctx") >> k) & 1
@@ -81,20 +76,13 @@
     def last_offset(self):
         offset = 0
         for k in range(self.rounds):
-            if not self.split(k) and k != self.packed:
+            if not self.split(k):
                 offset = offset + self.bit(k) * (self.rows >> (k + 1))
         return offset
 
 
 def aligned(x, by):
     return pl.multiple_of(x, by) if by >= 8 and not isinstance(x, int) else x
-
-
-def halves(first, second, upper):
-    top = lax.broadcasted_iota(jnp.int32, first.shape, 0) < 4
-    lower_rows = jnp.where(top, first, pltpu.roll(second, 4, 0))
-    upper_rows = jnp.where(top, pltpu.roll(first, 4, 0), second)
-    return jnp.where(upper == 1, upper_rows, lower_rows)
 
 
 def load_body(plan, split_parts, *refs):
@@ -204,7 +192,7 @@
 def merge_body(plan, k, part_ref, came_ref, stat_ref, stat_came_ref, *refs):
     last = k == plan.rounds - 1
     if last:
-        own_ref, away_ref, table = refs if len(refs) == 3 else (None, *refs)
+        rows_ref, table = refs
     else:
         part_new_ref, send_ref, table = refs
     _, factors = statistics(stat_ref, stat_came_ref)
@@ -214,54 +202,73 @@
     kept = pl.ds(aligned(plan.keep(k), count), count)
     base = plan.base(k + 1)
     rows_of = [pl.ds(aligned(q * plan.rows + base, count), count) for q in range(plan.group)]
-    packed = k == plan.packed
-    bit = plan.bit(k)
-    if packed:
-        joined = halves(table[rows_of[0], :], table[rows_of[1], :], bit)
-    for n in range(plan.sent_heads(k)):
-        if packed:
-            p = n
-            mine = [halves(part_ref[a, 2 * n], part_ref[a, 2 * n + 1], bit) for a in range(3)]
-            rows = joined
-        else:
-            p = n // plan.group
-            mine = [part_ref[a, n, kept, :] for a in range(3)]
-            rows = table[rows_of[n % plan.group], :]
+    for h in range(plan.heads):
+        p = h // plan.group
+        rows = table[rows_of[h % plan.group], :]
         col = lambda t: rows[:, 8 * t + p : 8 * t + p + 1]
-        out1, key1, dif1 = mine
-        out2, key2, dif2 = (came_ref[a, n].astype(F32) for a in range(3))
+        out1, key1, dif1 = (part_ref[a, h, kept, :] for a in range(3))
+        out2, key2, dif2 = (came_ref[a, h].astype(F32) for a in range(3))
         c1, c2 = col(0), col(1)
         out = c1 * out1 + c2 * out2
         dif = c1 * dif1 + c2 * dif2 + col(2) * key1 + col(3) * key2
         if not last:
-            part_new_ref[0, n] = out
-            part_new_ref[1, n] = c1 * key1 + c2 * key2
-            part_new_ref[2, n] = dif
+            part_new_ref[0, h] = out
+            part_new_ref[1, h] = c1 * key1 + c2 * key2
+            part_new_ref[2, h] = dif
             continue
         share = col(4)
         for a, x in ((0, out * share), (1, dif * (share * plan.scale))):
             offset = plan.last_offset()
             if not isinstance(offset, int):
                 x = pltpu.roll(x, (count - offset) % count, 0)
-            for h, start in ((2 * n, 0), (2 * n + 1, 4)) if packed else ((n, 0),):
-                of = slice(h * plan.head_size, (h + 1) * plan.head_size)
-                middle, end = start + plan.part_rows, start + plan.last_rows
-                if own_ref is not None:
-                    own_ref[a, :, of] = x[start:middle].astype(BF16)
-                    away_ref[a, :, of] = x[middle:end].astype(BF16)
-                else:
-                    away_ref[a, :, of] = x[start:end].astype(BF16)
+            of = slice(h * plan.head_size, (h + 1) * plan.head_size)
+            rows_ref[a, :, of] = x[: plan.last_rows].astype(BF16)
     if not last:
         give(plan, k + 1, part_new_ref, send_ref)
 
 
+def finish_body(plan, part_ref, came_ref, stat_ref, stat_came_ref, stat_all_ref, own_ref, *refs):
+    *away_refs, table = refs
+    k = plan.rounds - 2
+    top, total, mean = (stat_all_ref[8 * t : 8 * t + 8] for t in range(3))
+    inverse = 1.0 / jnp.where(total > 0.0, total, 1.0)
+    factors = []
+    for ref in (stat_ref, stat_came_ref):
+        f = jnp.exp(ref[0:8] - top) * inverse
+        factors += [f, f * plan.scale, f * plan.scale * (ref[16:24] - mean)]
+    rest = jnp.zeros((128 - 48, plan.lanes), F32)
+    table[...] = jnp.concatenate([*factors, rest], axis=0).T
+    count = plan.counts[k + 1]
+    kept = pl.ds(aligned(plan.keep(k), count), count)
+    base = plan.base(k + 1)
+    rows_of = [pl.ds(aligned(q * plan.rows + base, count), count) for q in range(plan.group)]
+    turn = plan.bit(k + 1) * plan.last_rows
+    for h in range(plan.heads):
+        p = h // plan.group
+        rows = table[rows_of[h % plan.group], :]
+        col = lambda t: rows[:, 8 * t + p : 8 * t + p + 1]
+        out1, key1, dif1 = (part_ref[a, h, kept, :] for a in range(3))
+        out2, key2, dif2 = (came_ref[a, h].astype(F32) for a in range(3))
+        out = col(0) * out1 + col(3) * out2
+        dif = col(1) * dif1 + col(4) * dif2 + col(2) * key1 + col(5) * key2
+        of = slice(h * plan.head_size, (h + 1) * plan.head_size)
+        for a, x in ((0, out), (1, dif)):
+            x = pltpu.roll(x, (count - turn) % count, 0)
+            for n, ref in enumerate((own_ref, *away_refs)):
+                ref[a, :, of] = x[n * plan.part_rows : (n + 1) * plan.part_rows].astype(ref.dtype)
+
+
+def gather_body(plan, own_ref, query_ref, owner_ref, both_ref, attn_ref, dq_ref):
+    me = lax.axis_index("query")
+    for a, out_ref in ((0, attn_ref), (1, dq_ref)):
+        mine = own_ref[a] + owner_ref[a].astype(F32)
+        theirs = query_ref[a].astype(F32) + both_ref[a].astype(F32)
+        for at, x in ((me, mine), (1 - me, theirs)):
+            start = pl.multiple_of(at * plan.features, 128)
+            out_ref[:, pl.ds(start, plan.features)] = x.astype(BF16)
+
+
 def give(plan, k, part_ref, send_ref):
-    if k == plan.packed:
-        for a in range(3):
-            for n in range(plan.heads // 2):
-                x = halves(part_ref[a, 2 * n], part_ref[a, 2 * n + 1], 1 - plan.bit(k))
-                send_ref[a, n] = x.astype(BF16)
-        return
     count = plan.counts[k + 1]
     gone = pl.ds(aligned(plan.give(k), count), count)
     for a in range(3):
@@ -274,7 +281,8 @@
         turned_ref[p] = pair_ref[p].T
 
 
-def backward_body(plan, stat_ref, stat_all_ref, qb_ref, gb_ref, turned_ref, dk_ref, dv_ref, table, dk, dv, semaphores):
+def backward_body(plan, first, count, stat_ref, stat_all_ref, qb_ref, gb_ref, turned_ref, *refs):
+    dk_ref, dv_ref, table, dk, dv, semaphores = refs[-6:]
     lanes = plan.lanes
     width = dk.shape[2]
     total = stat_all_ref[8:16]
@@ -284,18 +292,18 @@
     rest = jnp.zeros((128 - 24, lanes), F32)
     table[...] = jnp.concatenate([f, f * plan.scale, c * plan.scale, rest], axis=0).T
     copies = []
-    for p in range(plan.groups):
+    for p in range(first, first + count):
         queries = qb_ref[p].astype(F32)
         wv = (gb_ref[p].astype(F32) * table[:, p : p + 1]).astype(BF16)
         wc = (queries * table[:, 16 + p : 17 + p]).astype(BF16)
         wf = (queries * table[:, 8 + p : 9 + p]).astype(BF16)
         for n, (buffer, target) in enumerate(((dk, dk_ref), (dv, dv_ref))):
             if n == 0:
-                buffer[p] = nn(turned_ref[p], jnp.concatenate([wc, wf], axis=0)).astype(BF16)
+                buffer[p - first] = nn(turned_ref[p], jnp.concatenate([wc, wf], axis=0)).astype(BF16)
             else:
-                buffer[p] = nn(turned_ref[p, :, :lanes], wv).astype(BF16)
+                buffer[p - first] = nn(turned_ref[p, :, :lanes], wv).astype(BF16)
             copy = pltpu.make_async_copy(
-                buffer.at[p], target.at[:, p * width : (p + 1) * width], semaphores.at[n, p]
+                buffer.at[p - first], target.at[:, p * width : (p + 1) * width], semaphores.at[n, p - first]
             )
             copy.start()
             copies.append(copy)
@@ -325,9 +333,7 @@
     stat_shape = jax.ShapeDtypeStruct((24, lanes), F32)
     block_shape = jax.ShapeDtypeStruct((groups, lanes, width), BF16)
     part_shape = lambda k: jax.ShapeDtypeStruct((3, heads, plan.counts[k], size), F32)
-    send_shape = lambda k: jax.ShapeDtypeStruct(
-        (3, plan.sent_heads(k), plan.counts[k + 1], size), BF16
-    )
+    send_shape = lambda k: jax.ShapeDtypeStruct((3, heads, plan.counts[k + 1], size), BF16)
     from_hbm = [key_states, value_states] + ([query_states, out_grad] if pairwise else [])
     from_hbm = [pltpu.with_memory_space_constraint(x, pltpu.HBM) for x in from_hbm]
     own_shape = jax.ShapeDtypeStruct((plan.own_rows, plan.features), BF16)
@@ -375,11 +381,23 @@
         name="turn",
     )(pair)
 
-    stat = stat_own
-    for k in range(plan.rounds):
-        swap = [(i, i ^ (1 << k)) for i in range(plan.owner_ways)]
-        stat_came = lax.ppermute(stat, "ctx", swap)
-        came = lax.ppermute(send, "ctx", swap)
+    def swap(k):
+        return [(i, i ^ (1 << k)) for i in range(plan.owner_ways)]
+
+    def kernel(name, body, outs, *ins, vmem_mib=4, flops=10**8):
+        return call(
+            body,
+            outs,
+            vmem_mib,
+            flops,
+            in_specs=[VMEM] * len(ins),
+            out_specs=[VMEM] * len(outs),
+            scratch_shapes=[pltpu.VMEM((lanes, 128), F32)],
+            name=name,
+        )(*ins)
+
+    def exchange_statistics(k, stat):
+        came = lax.ppermute(stat, "ctx", swap(k))
         merged = call(
             merge_statistics_body,
             stat_shape,
@@ -388,51 +406,88 @@
             in_specs=[VMEM] * 2,
             out_specs=VMEM,
             name=f"statistics{k}",
-        )(stat, stat_came)
-        if k < plan.rounds - 1:
-            outs = (part_shape(k + 1), send_shape(k + 1))
-        elif pairwise:
-            outs = (jax.ShapeDtypeStruct((2, plan.part_rows, plan.features), BF16),) * 2
+        )(stat, came)
+        return came, merged
+
+    stats = [stat_own]
+    stats_came = []
+    for k in range(plan.rounds):
+        came, merged = exchange_statistics(k, stats[k])
+        stats_came.append(came)
+        stats.append(merged)
+    stat_all = stats[-1]
+
+    def gradients(name, first, count, *into):
+        return call(
+            functools.partial(backward_body, plan, first, count),
+            (context_shape, context_shape),
+            8,
+            4 * 10**9,
+            in_specs=[VMEM] * 5 + [HBM] * len(into),
+            out_specs=[HBM] * 2,
+            scratch_shapes=[
+                pltpu.VMEM((lanes, 128), F32),
+                pltpu.VMEM((count, slots, width), BF16),
+                pltpu.VMEM((count, slots, width), BF16),
+                pltpu.SemaphoreType.DMA((2, count)),
+            ],
+            input_output_aliases={5 + n: n for n in range(len(into))},
+            name=name,
+        )(stat_own, stat_all, qb, gb, turned, *into)
+
+    split = (groups + 1) // 2
+    grads = gradients("backward0", 0, split)
+    grads = gradients("backward1", split, groups - split, *grads)
+
+    for k in range(plan.rounds):
+        if plan.direct and k == plan.rounds - 1:
+            continue
+        came = lax.ppermute(send, "ctx", swap(k))
+        inputs = (part, came, stats[k], stats_came[k])
+        if plan.direct and k == plan.rounds - 2:
+            rows_shape = lambda dtype: jax.ShapeDtypeStruct((2, plan.part_rows, plan.features), dtype)
+            own, *away = kernel(
+                "finish",
+                functools.partial(finish_body, plan),
+                (rows_shape(F32),) + (rows_shape(BF16),) * 3,
+                *inputs,
+                stat_all,
+            )
+        elif k < plan.rounds - 1:
+            part, send = kernel(
+                f"merge{k}",
+                functools.partial(merge_body, plan, k),
+                (part_shape(k + 1), send_shape(k + 1)),
+                *inputs,
+            )
         else:
-            outs = (jax.ShapeDtypeStruct((2, plan.last_rows, plan.features), BF16),)
-        part, send, *_ = call(
-            functools.partial(merge_body, plan, k),
-            outs,
-            4,
-            10**8,
-            in_specs=[VMEM] * 4,
-            out_specs=[VMEM] * len(outs),
-            scratch_shapes=[pltpu.VMEM((lanes, 128), F32)],
-            name=f"merge{k}",
-        )(part, came, stat, stat_came) + (None,) * (2 - len(outs))
-        stat = merged
-    if pairwise:
-        own, away = part, send
-        back = lax.ppermute(away, "query", [(0, 1), (1, 0)])
-
-    key_grad, value_grad = call(
-        functools.partial(backward_body, plan),
-        (context_shape, context_shape),
-        12,
-        4 * 10**9,
-        in_specs=[VMEM] * 5,
-        out_specs=[HBM] * 2,
-        scratch_shapes=[
-            pltpu.VMEM((lanes, 128), F32),
-            pltpu.VMEM((groups, slots, width), BF16),
-            pltpu.VMEM((groups, slots, width), BF16),
-            pltpu.SemaphoreType.DMA((2, groups)),
-        ],
-        name="backward",
-    )(stat_own, stat, qb, gb, turned)
-
-    if pairwise:
-        first = jnp.where(qi == 0, own, back)
-        second = jnp.where(qi == 0, back, own)
-        final = jnp.concatenate([first, second], axis=2)
-    else:
-        final = lax.all_to_all(part, "query", split_axis=1, concat_axis=2, tiled=True)
-    return final[0], final[1], key_grad, value_grad
+            (rows,) = kernel(
+                f"merge{k}",
+                functools.partial(merge_body, plan, k),
+                (jax.ShapeDtypeStruct((2, plan.last_rows, plan.features), BF16),),
+                *inputs,
+            )
+    if not plan.direct:
+        final = lax.all_to_all(rows, "query", split_axis=1, concat_axis=2, tiled=True)
+        return final[0], final[1], *grads
+
+    ways = plan.owner_ways
+    both_axes = ("query", "ctx")
+    jump = ways >> 1
+    from_query = lax.ppermute(away[0], "query", [(0, 1), (1, 0)])
+    from_owner = lax.ppermute(away[1], "ctx", swap(plan.rounds - 1))
+    from_both = lax.ppermute(away[2], both_axes, [(i, i ^ ways ^ jump) for i in range(2 * ways)])
+    outs = (jax.ShapeDtypeStruct((plan.part_rows, 2 * plan.features), BF16),) * 2
+    attn, query_grad = call(
+        functools.partial(gather_body, plan),
+        outs,
+        2,
+        10**6,
+        in_specs=[VMEM] * 4,
+        out_specs=[VMEM] * 2,
+        name="gather",
+    )(own, from_query, from_owner, from_both)
+    return attn, query_grad, *grads
 
 
 def solution(mesh):

time: 44.9 us -> 47 us (1.047)
  starting transfers between devices: 12.5 us -> 16.9 us
  local copies, waits for them, and re-layouts: 1.72 us -> 0.09 us
  Pallas kernels: 13.9 us -> 15 us
  waiting for transfers between devices: 12.7 us -> 11.7 us
  other arithmetic: 2.4 us -> 1.75 us
    ppermute x9 -> x10, starting transfers between devices: 9.45 us -> 13.8 us  [the longest x4 5.63 us: exchange_statistics(): came = lax.ppermute(stat, 'ctx', swap(k))]
    unnamed x14 -> x2, local copies, waits for them, and re-layouts: 1.63 us -> 0.01 us
    pallas_call x9 -> x10, Pallas kernels: 5.52 us -> 6.59 us  [the longest x2 4.7 us: gradients(): call(functools.partial(backward_body, plan, first, count), (context_shape...]
    ppermute x9 -> x10, waiting for transfers between devices: 12.2 us -> 11.3 us  [the longest x4 7.95 us: exchange_statistics(): came = lax.ppermute(stat, 'ctx', swap(k))]
    squeeze x1 -> x0, other arithmetic: 0.63 us -> none  [local(): return (final[0], final[1], key_grad, value_grad)]
  transfers between devices with their start and end apart: 10 -> 11, of which waited for: 6 -> 7; matrix products, arithmetic and copies ran while one was open for 2% -> 2% of each run, Pallas kernels for 17% -> 18%
where the time goes in v3:
time: 47 us; the launch traced here: 46.8 us
  starting transfers between devices  16.9 us (36%)
  Pallas kernels  15 us (32%)
  waiting for transfers between devices  11.7 us (25%)
  other arithmetic  1.75 us (4%)
  between operations  1.41 us (3%)
    ppermute x4, waiting for transfers between devices, exchange_statistics(): came = lax.ppermute(stat, 'ctx', swap(k))  7.95 us
    ppermute x4, starting transfers between devices, exchange_statistics(): came = lax.ppermute(stat, 'ctx', swap(k))  5.63 us
    pallas_call x2, Pallas kernels, gradients(): call(functools.partial(backward_body, plan, first, count), (context_shape...  4.7 us
    pallas_call x1, Pallas kernels, local(): call(functools.partial(forward_body, plan, pairwise), (part_shape(0), sen...  4.62 us
    ppermute x3, starting transfers between devices, local(): came = lax.ppermute(send, 'ctx', swap(k))  3.67 us
    ppermute x1, waiting for transfers between devices, local(): lax.ppermute(away[2], both_axes, [(i, i ^ ways ^ jump) for i in range(2 *...  3.09 us
    ppermute x1, starting transfers between devices, local(): moved = lax.ppermute(theirs, 'query', [(0, 1), (1, 0)])  3.06 us
    pallas_call x1, Pallas kernels, local(): call(functools.partial(load_body, plan, pairwise), [context_shape] * 2 +...  2.88 us
  transfers between devices with their start and end apart: 11, of which 7 were waited for; matrix products, arithmetic and copies ran while one was open for 2% of the time, Pallas kernels for 18%

profile of v3, /device:TPU:0, one launch (start us, length us, event | category | flops | bytes accessed | tf_op | source)
XLA Modules:
  0.0 46.8 jit_solution(1100558429446700766)
XLA Ops:
  0.6 0.0 copy-start
  0.7 1.0 %fusion = bf16[2,32,1536]{2,1,0:T(8,128)(2,1)S(1)} fusion(s32[]{:T(128)S(6)} %select_n.26, bf16[1,32,3072]{2,1,0:T(8,128)(2,1)} %bitcast.14, bf16[1,32,3072]{2,1,0:T(8,128)(2,1)} %bitcast.15), kind=kLoop, calls=%fused_computation.2 | loop fusion | flops 393216 | bytes 589828 | tf_op jit(solution)/shard_map/stack | solution.py:320
  1.6 3.1 %collective-permute-start = (bf16[2,32,1536]{2,1,0:T(8,128)(2,1)S(1)}, bf16[2,32,1536]{2,1,0:T(8,128)(2,1)S(1)}, u32[]{:S(2)}, u32[]{:S(2)}) collective-permute-start(bf16[2,32,1536]{2,1,0:T(8,128)(2,1)S(1)} %fusion), channel_id=1, source_target_pairs={{0,16},{16,0},{1,17},{17,1},{2,18},{18,2},{3,19},{19,3},{4,20},{20... | collective-permute-start | bytes 589832 | tf_op jit(solution)/shard_map/ppermute | solution.py:323
  5.3 0.0 copy-done
  5.3 0.1 constant_dynamic-slice_fusion
  5.4 0.7 %broadcast_compare_fusion.4 = (pred[1024]{0:T(1024)(128)(4,1)S(1)}, pred[1024]{0:T(1024)(128)(4,1)S(1)}, pred[1024]{0:T(1024)(128)(4,1)S(1)}, pred[1024]{0:T(1024)(128)(4,1)S(1)}, pred[1024]{0:T(1024)(128)(4,1)S(1)}) fusion(s32[1024]{0:T(1024)} %param.10), kind=kLoop, calls=%fused_computation.9 | loop fusion | flops 5120 | bytes 9216 | tf_op jit(solution)/shard_map/eq | solution.py:329
  6.1 2.9 %load.1 = (bf16[1024,1536]{1,0:T(8,128)(2,1)S(1)}, bf16[1024,1536]{1,0:T(8,128)(2,1)S(1)}, bf16[32,1536]{1,0:T(8,128)(2,1)S(1)}, bf16[32,1536]{1,0:T(8,128)(2,1)S(1)}) custom-call(bf16[1024,1536]{1,0:T(8,128)(2,1)} %refs_0_.1, bf16[1024,1536]{1,0:T(8,128)(2,1)} %refs_1_.1, bf16[32,3072]{1,0:T(8,128)(2,1)} %refs_2_.1, bf16[32,3072]{1,0:T(8,128)(2,1)} %refs_3_.1), custom_call_target="tpu_custom_call" | custom-call | flops 1000000000 | bytes 1048576 | tf_op jit(solution)/shard_map/load/pallas_call | solution.py:341
  9.0 0.1 select_select_fusion.refs_5_
  9.1 0.5 collective-permute-done.refs_2_
  9.6 4.6 %forward.1 = (f32[3,12,64,128]{3,2,1,0:T(8,128)S(1)}, bf16[3,12,32,128]{3,2,1,0:T(8,128)(2,1)S(1)}, f32[24,128]{1,0:T(8,128)S(1)}, bf16[6,256,1024]{2,1,0:T(8,12...) custom-call(bf16[32,1536]{1,0:T(8,128)(2,1)S(1)} %get-tuple-element.28.refs_0_, ...), custom_call_target="tpu_custom_call" | custom-call | flops 4000000000 | bytes 1048576 | tf_op jit(solution)/shard_map/forward/pallas_call | solution.py:351
  14.2 0.1 collective-permute-start.1
  14.3 0.5 %collective-permute-start.2 = (f32[24,128]{1,0:T(8,128)S(1)}, f32[24,128]{1,0:T(8,128)S(1)}, u32[]{:S(2)}, u32[]{:S(2)}) collective-permute-start(f32[24,128]{1,0:T(8,128)S(1)} %get-tuple-element.34.stat_ref), channel_id=1, source_target_pairs={{0,1},{1,0},{2,3},{3,2},{4,5},{5,4},{6,7},{7,6},{8,9},{9,8},{10,11... | collective-permute-start | bytes 36872 | tf_op jit(solution)/shard_map/ppermute | solution.py:400
  14.8 1.1 %collective-permute-done.2.stat_came_ref = f32[24,128]{1,0:T(8,128)S(1)} collective-permute-done((f32[24,128]{1,0:T(8,128)S(1)}, f32[24,128]{1,0:T(8,128)S(1)}, u32[]{:S(2)}, u32[]{:S(2)}) %collective-permute-start.2) | collective-permute-done | bytes 12320 | tf_op jit(solution)/shard_map/ppermute | solution.py:400
  15.9 0.0 collective-permute-done.1.came_ref
  15.9 0.5 %merge0.1 = (f32[3,12,32,128]{3,2,1,0:T(8,128)S(1)}, bf16[3,12,16,128]{3,2,1,0:T(8,128)(2,1)S(1)}) custom-call(f32[3,12,64,128]{3,2,1,0:T(8,128)S(1)} %get-tuple-element.32.part_ref, bf16[3,12,32,128]{3,2,1,0:T(8,128)(2,1)S(1)} %collective-permute-done.1.came_ref, f32[24,128]{1,0:T(8,128)S(1)} %get-tuple-element.34.stat_ref, ...), custom_call_target="tpu_custom_call" | custom-call | flops 100000000 | bytes 1048576 | tf_op jit(solution)/shard_map/merge0/pallas_call | solution.py:388
  16.4 1.8 %collective-permute-start.3 = (bf16[3,12,16,128]{3,2,1,0:T(8,128)(2,1)S(1)}, bf16[3,12,16,128]{3,2,1,0:T(8,128)(2,1)S(1)}, u32[]{:S(2)}, u32[]{:S(2)}) collective-permute-start(bf16[3,12,16,128]{3,2,1,0:T(8,128)(2,1)S(1)} %get-tuple-element.36), channel_id=1, source_target_pairs={{0,2},{1,3},{2,0},{3,1},{4,6},{5,7},{6,4},{7,5},{8,10},{9,11},{10,... | collective-permute-start | bytes 442376 | tf_op jit(solution)/shard_map/ppermute | solution.py:445
  18.2 0.4 collective-permute-start.4
  18.6 4.1 %collective-permute-done.4.stat_came_ref = f32[24,128]{1,0:T(8,128)S(1)} collective-permute-done((f32[24,128]{1,0:T(8,128)S(1)}, f32[24,128]{1,0:T(8,128)S(1)}, u32[]{:S(2)}, u32[]{:S(2)}) %collective-permute-start.4) | collective-permute-done | bytes 12320 | tf_op jit(solution)/shard_map/ppermute | solution.py:400
  22.6 1.9 %collective-permute-start.6 = (f32[24,128]{1,0:T(8,128)S(1)}, f32[24,128]{1,0:T(8,128)S(1)}, u32[]{:S(2)}, u32[]{:S(2)}) collective-permute-start(f32[24,128]{1,0:T(8,128)S(1)} %statistics1.1.stat_ref), channel_id=1, source_target_pairs={{0,4},{1,5},{2,6},{3,7},{4,0},{5,1},{6,2},{7,3},{8,12},{9,13},{10,... | collective-permute-start | bytes 36872 | tf_op jit(solution)/shard_map/ppermute | solution.py:400
  24.5 1.9 %collective-permute-done.6.stat_came_ref = f32[24,128]{1,0:T(8,128)S(1)} collective-permute-done((f32[24,128]{1,0:T(8,128)S(1)}, f32[24,128]{1,0:T(8,128)S(1)}, u32[]{:S(2)}, u32[]{:S(2)}) %collective-permute-start.6) | collective-permute-done | bytes 12320 | tf_op jit(solution)/shard_map/ppermute | solution.py:400
  26.4 2.9 %collective-permute-start.7 = (f32[24,128]{1,0:T(8,128)S(1)}, f32[24,128]{1,0:T(8,128)S(1)}, u32[]{:S(2)}, u32[]{:S(2)}) collective-permute-start(f32[24,128]{1,0:T(8,128)S(1)} %statistics2.1.stat_ref), channel_id=1, source_target_pairs={{0,8},{1,9},{2,10},{3,11},{4,12},{5,13},{6,14},{7,15},{8,0},{9,1},... | collective-permute-start | bytes 36872 | tf_op jit(solution)/shard_map/ppermute | solution.py:400
  29.3 0.9 %turn.1.turned_ref = bf16[6,1024,256]{2,1,0:T(8,128)(2,1)S(1)} custom-call(bf16[6,256,1024]{2,1,0:T(8,128)(2,1)S(1)} %get-tuple-element.47.pair_ref), custom_call_target="tpu_custom_call" | custom-call | flops 1000000000 | bytes 1048576 | tf_op jit(solution)/shard_map/turn/pallas_call | solution.py:374
  30.1 0.9 %collective-permute-done.7.stat_came_ref = f32[24,128]{1,0:T(8,128)S(1)} collective-permute-done((f32[24,128]{1,0:T(8,128)S(1)}, f32[24,128]{1,0:T(8,128)S(1)}, u32[]{:S(2)}, u32[]{:S(2)}) %collective-permute-start.7) | collective-permute-done | bytes 12320 | tf_op jit(solution)/shard_map/ppermute | solution.py:400
  31.1 0.0 collective-permute-done.3.came_ref
  31.1 0.4 merge1.1
  31.5 1.8 %collective-permute-start.5 = (bf16[3,12,8,128]{3,2,1,0:T(8,128)(2,1)S(1)}, bf16[3,12,8,128]{3,2,1,0:T(8,128)(2,1)S(1)}, u32[]{:S(2)}, u32[]{:S(2)}) collective-permute-start(bf16[3,12,8,128]{3,2,1,0:T(8,128)(2,1)S(1)} %get-tuple-element.38), channel_id=1, source_target_pairs={{0,4},{1,5},{2,6},{3,7},{4,0},{5,1},{6,2},{7,3},{8,12},{9,13},{10,... | collective-permute-start | bytes 221192 | tf_op jit(solution)/shard_map/ppermute | solution.py:445
  33.3 2.3 %backward0.1 = (bf16[1024,1536]{1,0:T(8,128)(2,1)}, bf16[1024,1536]{1,0:T(8,128)(2,1)}) custom-call(f32[24,128]{1,0:T(8,128)S(1)} %get-tuple-element.34.stat_ref, f32[24,128]{1,0:T(8,128)S(1)} %statistics3.1.stat_all_ref, bf16[6,128,256]{2,1,0:T(8,128)(2,1)S(1)} %get-tuple-element.45.qb_ref, bf16[6,128,256]{2,1,0:T(8,128)(2,1)S(1)} %get-tuple-element.46.gb_ref, ...), custom_call_target="tpu_custom_call" | custom-call | flops 4000000000 | bytes 1048576 | tf_op jit(solution)/shard_map/backward0/pallas_call | solution.py:421
  35.7 0.2 collective-permute-done.5.came_ref
  35.9 0.3 finish.1
  36.2 1.8 %collective-permute-start.8 = (bf16[2,2,1536]{2,1,0:T(2,128)(2,1)S(1)}, bf16[2,2,1536]{2,1,0:T(2,128)(2,1)S(1)}, u32[]{:S(2)}, u32[]{:S(2)}) collective-permute-start(bf16[2,2,1536]{2,1,0:T(2,128)(2,1)S(1)} %get-tuple-element.40), channel_id=1, source_target_pairs={{0,16},{16,0},{1,17},{17,1},{2,18},{18,2},{3,19},{19,3},{4,20},{20... | collective-permute-start | bytes 36872 | tf_op jit(solution)/shard_map/ppermute | solution.py:477
  38.0 2.7 %collective-permute-start.9 = (bf16[2,2,1536]{2,1,0:T(2,128)(2,1)S(1)}, bf16[2,2,1536]{2,1,0:T(2,128)(2,1)S(1)}, u32[]{:S(2)}, u32[]{:S(2)}) collective-permute-start(bf16[2,2,1536]{2,1,0:T(2,128)(2,1)S(1)} %get-tuple-element.41), channel_id=1, source_target_pairs={{0,8},{1,9},{2,10},{3,11},{4,12},{5,13},{6,14},{7,15},{8,0},{9,1},... | collective-permute-start | bytes 36872 | tf_op jit(solution)/shard_map/ppermute | solution.py:478
  40.7 0.0 collective-permute-start.10
  40.7 2.3 %backward1.1 = (bf16[1024,1536]{1,0:T(8,128)(2,1)}, bf16[1024,1536]{1,0:T(8,128)(2,1)}) custom-call(f32[24,128]{1,0:T(8,128)S(1)} %get-tuple-element.34.stat_ref, f32[24,128]{1,0:T(8,128)S(1)} %statistics3.1.stat_all_ref, bf16[6,128,256]{2,1,0:T(8,128)(2,1)S(1)} %get-tuple-element.45.qb_ref, ...), custom_call_target="tpu_custom_call", output_to_operand_aliasing={{0}: (5, {}), {1}: (6, {})} | custom-call | flops 4000000000 | bytes 1048576 | tf_op jit(solution)/shard_map/backward1/pallas_call | solution.py:421
  43.1 0.0 collective-permute-done.8.query_ref
  43.1 0.0 collective-permute-done.9.owner_ref
  43.1 3.1 %collective-permute-done.10.both_ref = bf16[2,2,1536]{2,1,0:T(2,128)(2,1)S(1)} collective-permute-done((bf16[2,2,1536]{2,1,0:T(2,128)(2,1)S(1)}, bf16[2,2,1536]{2,1,0:T(2,128)(2,1)S(1)}, u32[]{:S(2)}, u32[]{:S(2)}) %collective-permute-start.10) | collective-permute-done | bytes 12320 | tf_op jit(solution)/shard_map/ppermute | solution.py:479
  46.2 0.6 %gather.1 = (bf16[2,3072]{1,0:T(2,128)(2,1)}, bf16[2,3072]{1,0:T(2,128)(2,1)}) custom-call(f32[2,2,1536]{2,1,0:T(2,128)S(1)} %get-tuple-element.39.own_ref, bf16[2,2,1536]{2,1,0:T(2,128)(2,1)S(1)} %collective-permute-done.8.query_ref, bf16[2,2,1536]{2,1,0:T(2,128)(2,1)S(1)} %collective-permute-done.9.owner_ref, ...), custom_call_target="tpu_custom_call" | custom-call | flops 1000000 | bytes 1048576 | tf_op jit(solution)/shard_map/gather/pallas_call | solution.py:481
  (6 shorter events, 0.1 us)
Async XLA Ops:
  0.6 4.7 %copy-start = (f32[5,24]{1,0:T(8,128)S(1)}, f32[5,24]{1,0:T(8,128)}, u32[]{:S(2)}) copy-start(f32[5,24]{1,0:T(8,128)} %param.11) | copy-start | bytes 1444
  1.6 8.0 %collective-permute-start = (bf16[2,32,1536]{2,1,0:T(8,128)(2,1)S(1)}, bf16[2,32,1536]{2,1,0:T(8,128)(2,1)S(1)}, u32[]{:S(2)}, u32[]{:S(2)}) collective-permute-start(bf16[2,32,1536]{2,1,0:T(8,128)(2,1)S(1)} %fusion), channel_id=1, source_target_pairs={{0,16},{16,0},{1,17},{17,1},{2,18},{18,2},{3,19},{19,3},{4,20},{20... | collective-permute-start | bytes 589832 | tf_op jit(solution)/shard_map/ppermute | solution.py:323
  14.2 1.7 %collective-permute-start.1 = (bf16[3,12,32,128]{3,2,1,0:T(8,128)(2,1)S(1)}, bf16[3,12,32,128]{3,2,1,0:T(8,128)(2,1)S(1)}, u32[]{:S(2)}, u32[]{:S(2)}) collective-permute-start(bf16[3,12,32,128]{3,2,1,0:T(8,128)(2,1)S(1)} %get-tuple-element.33), channel_id=1, source_target_pairs={{0,1},{1,0},{2,3},{3,2},{4,5},{5,4},{6,7},{7,6},{8,9},{9,8},{10,11... | collective-permute-start | bytes 884744 | tf_op jit(solution)/shard_map/ppermute | solution.py:445
  14.3 1.6 %collective-permute-start.2 = (f32[24,128]{1,0:T(8,128)S(1)}, f32[24,128]{1,0:T(8,128)S(1)}, u32[]{:S(2)}, u32[]{:S(2)}) collective-permute-start(f32[24,128]{1,0:T(8,128)S(1)} %get-tuple-element.34.stat_ref), channel_id=1, source_target_pairs={{0,1},{1,0},{2,3},{3,2},{4,5},{5,4},{6,7},{7,6},{8,9},{9,8},{10,11... | collective-permute-start | bytes 36872 | tf_op jit(solution)/shard_map/ppermute | solution.py:400
  16.4 14.7 %collective-permute-start.3 = (bf16[3,12,16,128]{3,2,1,0:T(8,128)(2,1)S(1)}, bf16[3,12,16,128]{3,2,1,0:T(8,128)(2,1)S(1)}, u32[]{:S(2)}, u32[]{:S(2)}) collective-permute-start(bf16[3,12,16,128]{3,2,1,0:T(8,128)(2,1)S(1)} %get-tuple-element.36), channel_id=1, source_target_pairs={{0,2},{1,3},{2,0},{3,1},{4,6},{5,7},{6,4},{7,5},{8,10},{9,11},{10,... | collective-permute-start | bytes 442376 | tf_op jit(solution)/shard_map/ppermute | solution.py:445
  18.2 4.5 %collective-permute-start.4 = (f32[24,128]{1,0:T(8,128)S(1)}, f32[24,128]{1,0:T(8,128)S(1)}, u32[]{:S(2)}, u32[]{:S(2)}) collective-permute-start(f32[24,128]{1,0:T(8,128)S(1)} %statistics0.1.stat_ref), channel_id=1, source_target_pairs={{0,2},{1,3},{2,0},{3,1},{4,6},{5,7},{6,4},{7,5},{8,10},{9,11},{10,... | collective-permute-start | bytes 36872 | tf_op jit(solution)/shard_map/ppermute | solution.py:400
  22.6 3.8 %collective-permute-start.6 = (f32[24,128]{1,0:T(8,128)S(1)}, f32[24,128]{1,0:T(8,128)S(1)}, u32[]{:S(2)}, u32[]{:S(2)}) collective-permute-start(f32[24,128]{1,0:T(8,128)S(1)} %statistics1.1.stat_ref), channel_id=1, source_target_pairs={{0,4},{1,5},{2,6},{3,7},{4,0},{5,1},{6,2},{7,3},{8,12},{9,13},{10,... | collective-permute-start | bytes 36872 | tf_op jit(solution)/shard_map/ppermute | solution.py:400
  26.4 4.7 %collective-permute-start.7 = (f32[24,128]{1,0:T(8,128)S(1)}, f32[24,128]{1,0:T(8,128)S(1)}, u32[]{:S(2)}, u32[]{:S(2)}) collective-permute-start(f32[24,128]{1,0:T(8,128)S(1)} %statistics2.1.stat_ref), channel_id=1, source_target_pairs={{0,8},{1,9},{2,10},{3,11},{4,12},{5,13},{6,14},{7,15},{8,0},{9,1},... | collective-permute-start | bytes 36872 | tf_op jit(solution)/shard_map/ppermute | solution.py:400
  31.5 4.4 %collective-permute-start.5 = (bf16[3,12,8,128]{3,2,1,0:T(8,128)(2,1)S(1)}, bf16[3,12,8,128]{3,2,1,0:T(8,128)(2,1)S(1)}, u32[]{:S(2)}, u32[]{:S(2)}) collective-permute-start(bf16[3,12,8,128]{3,2,1,0:T(8,128)(2,1)S(1)} %get-tuple-element.38), channel_id=1, source_target_pairs={{0,4},{1,5},{2,6},{3,7},{4,0},{5,1},{6,2},{7,3},{8,12},{9,13},{10,... | collective-permute-start | bytes 221192 | tf_op jit(solution)/shard_map/ppermute | solution.py:445
  36.2 6.9 %collective-permute-start.8 = (bf16[2,2,1536]{2,1,0:T(2,128)(2,1)S(1)}, bf16[2,2,1536]{2,1,0:T(2,128)(2,1)S(1)}, u32[]{:S(2)}, u32[]{:S(2)}) collective-permute-start(bf16[2,2,1536]{2,1,0:T(2,128)(2,1)S(1)} %get-tuple-element.40), channel_id=1, source_target_pairs={{0,16},{16,0},{1,17},{17,1},{2,18},{18,2},{3,19},{19,3},{4,20},{20... | collective-permute-start | bytes 36872 | tf_op jit(solution)/shard_map/ppermute | solution.py:477
  38.0 5.1 %collective-permute-start.9 = (bf16[2,2,1536]{2,1,0:T(2,128)(2,1)S(1)}, bf16[2,2,1536]{2,1,0:T(2,128)(2,1)S(1)}, u32[]{:S(2)}, u32[]{:S(2)}) collective-permute-start(bf16[2,2,1536]{2,1,0:T(2,128)(2,1)S(1)} %get-tuple-element.41), channel_id=1, source_target_pairs={{0,8},{1,9},{2,10},{3,11},{4,12},{5,13},{6,14},{7,15},{8,0},{9,1},... | collective-permute-start | bytes 36872 | tf_op jit(solution)/shard_map/ppermute | solution.py:478
  40.7 5.5 %collective-permute-start.10 = (bf16[2,2,1536]{2,1,0:T(2,128)(2,1)S(1)}, bf16[2,2,1536]{2,1,0:T(2,128)(2,1)S(1)}, u32[]{:S(2)}, u32[]{:S(2)}) collective-permute-start(bf16[2,2,1536]{2,1,0:T(2,128)(2,1)S(1)} %get-tuple-element.42), channel_id=1, source_target_pairs={{0,24},{1,25},{2,26},{3,27},{4,28},{5,29},{6,30},{7,31},{8,16},{9,... | collective-permute-start | bytes 36872 | tf_op jit(solution)/shard_map/ppermute | solution.py:479

commit v4 on v2

--- a/solution.py
+++ b/solution.py
@@ -66,8 +66,17 @@
     def sent_heads(self, k):
         return self.heads // 2 if k == self.packed else self.heads
 
+    def swapped(self, k):
+        return 3 - k if self.rounds >= 3 and k in (1, 2) else k
+
     def bit(self, k):
-        return (lax.axis_index("ctx") >> k) & 1
+        owner = lax.axis_index("ctx")
+        return (owner >> jnp.where(owner % 2 == 1, self.swapped(k), k)) & 1
+
+    def swap(self, k):
+        return [
+            (i, i ^ (1 << (self.swapped(k) if i % 2 else k))) for i in range(self.owner_ways)
+        ]
 
     def keep(self, k):
         return self.bit(k) * self.counts[k + 1] if self.split(k) else 0
@@ -97,85 +106,181 @@
     return jnp.where(upper == 1, upper_rows, lower_rows)
 
 
-def load_body(plan, split_parts, *refs):
-    count = 4 if split_parts else 2
-    ins, outs, semaphores = refs[:count], refs[count : 2 * count], refs[2 * count]
-    copies = []
-    for n, (source, target) in enumerate(zip(ins, outs)):
-        if n >= 2:
-            start = pl.multiple_of(lax.axis_index("query") * plan.features, 128)
-            source = source.at[:, pl.ds(start, plan.features)]
-        copies.append(pltpu.make_async_copy(source, target, semaphores.at[n]))
+def copy_all(pairs, semaphores):
+    copies = [
+        pltpu.make_async_copy(source, target, semaphores.at[n]) for n, (source, target) in enumerate(pairs)
+    ]
     for copy in copies:
         copy.start()
-    for copy in copies:
+    return copies
+
+
+def columns_at(plan, ref, at):
+    return ref.at[:, pl.ds(pl.multiple_of(at * plan.features, 128), plan.features)]
+
+
+def cut_body(plan, q_ref, g_ref, their_q_ref, their_g_ref, semaphores):
+    at = 1 - lax.axis_index("query")
+    pairs = [(columns_at(plan, q_ref, at), their_q_ref), (columns_at(plan, g_ref, at), their_g_ref)]
+    for copy in copy_all(pairs, semaphores):
         copy.wait()
 
 
-def forward_body(plan, split_parts, *refs):
-    if split_parts:
-        q_ref, g_ref, moved_ref = refs[:3]
-        refs = refs[3:]
-    else:
-        moved_ref = refs[0]
-        refs = refs[1:]
-    (k_ref, v_ref, term_ref, part_ref, send_ref, stat_ref, pair_ref, qb_ref, gb_ref) = refs[:9]
-    source, scores, dprobs, columns = refs[9:]
-    rows, size, group = plan.rows, plan.head_size, plan.group
-    width = group * size
+def load_body(plan, pairwise, live_ref, *refs):
+    count = 6 if pairwise else 4
+    ids_hbm, bias_hbm, k_hbm, v_hbm, *rows_hbm = refs[:count]
+    k_ref, v_ref, *rows_refs, term_ref, ids_ref, bias_ref, semaphores = refs[count:]
+    me = lax.axis_index("query")
+    copies = copy_all(
+        [
+            (ids_hbm, ids_ref),
+            (bias_hbm, bias_ref),
+            (k_hbm, k_ref),
+            (v_hbm, v_ref),
+            *((columns_at(plan, source, me), target) for source, target in zip(rows_hbm, rows_refs)),
+        ],
+        semaphores,
+    )
+    for copy in copies[:2]:
+        copy.wait()
+    ids = ids_ref[...]
+    live = lax.broadcasted_iota(jnp.int32, ids.shape, 1) < live_ref[0]
+    masks = [ids == level for level in range(bias_ref.shape[0])]
+    for h in range(plan.heads):
+        row = jnp.zeros(ids.shape, F32)
+        for level, mask in enumerate(masks):
+            row = jnp.where(mask, bias_ref[level, me * plan.heads + h], row)
+        term_ref[h : h + 1, :] = jnp.where(live, row, -1e30)
+    for copy in copies[2:]:
+        copy.wait()
+
+
+def row_order(plan):
+    rows = plan.rows
     place = lax.broadcasted_iota(jnp.int32, (rows, rows), 0)
     column = lax.broadcasted_iota(jnp.int32, (rows, rows), 1)
     inner = place % plan.last_rows
     outer = place // plan.last_rows
     owner = jnp.zeros_like(outer)
     for k in range(plan.rounds):
-        owner = owner | (((outer >> (plan.rounds - 1 - k)) & 1) << k)
+        bit = (outer >> (plan.rounds - 1 - k)) & 1
+        odd = (outer >> (plan.rounds - 1)) & 1
+        owner = owner | (bit << jnp.where(odd == 1, plan.swapped(k), k))
     wanted = (
         inner // plan.part_rows * plan.own_rows + owner * plan.part_rows + inner % plan.part_rows
     )
-    permute = (column == wanted).astype(F32).astype(BF16)
-    qb_ref[...] = jnp.zeros_like(qb_ref)
-    gb_ref[...] = jnp.zeros_like(gb_ref)
-    for which, own_ref, block_ref in ((0, 0, qb_ref), (1, 1, gb_ref)):
-        if split_parts:
-            source[: plan.own_rows] = (q_ref, g_ref)[own_ref][...]
-            source[plan.own_rows :] = moved_ref[which]
-        else:
-            source[...] = moved_ref[which]
-        for p in range(plan.groups):
-            ordered = nn(permute, source[:, p * width : (p + 1) * width]).astype(BF16)
+    return (column == wanted).astype(F32).astype(BF16)
+
+
+def place_rows(plan, own_ref, moved_ref, block_ref, source):
+    rows, size = plan.rows, plan.head_size
+    width = plan.group * size
+    if own_ref is None:
+        source[...] = moved_ref[...]
+    else:
+        source[: plan.own_rows] = own_ref[...]
+        source[plan.own_rows :] = moved_ref[...]
+    if plan.group > 1:
+        block_ref[...] = jnp.zeros_like(block_ref)
+    permute = row_order(plan)
+    for p in range(plan.groups):
+        ordered = nn(permute, source[:, p * width : (p + 1) * width]).astype(BF16)
+        for q in range(plan.group):
+            block_ref[p, q * rows : (q + 1) * rows, q * size : (q + 1) * size] = ordered[
+                :, q * size : (q + 1) * size
+            ]
+
+
+STEP = 16
+TILE = 256
+
+
+def pipeline(plan, product, chunk, finish):
+    tiles = range(0, plan.slots, TILE)
+    for j in tiles:
+        product(0, j)
+    chunks = range(0, plan.lanes, STEP)
+    for p in range(plan.groups):
+        pending = [functools.partial(product, p + 1, j) for j in tiles] if p + 1 < plan.groups else []
+        if p:
+            pending.insert(1, functools.partial(finish, p - 1))
+        share = -(-len(pending) // len(chunks)) if pending else 0
+        gap = max(1, len(chunks) // max(1, len(pending)))
+        for i, r in enumerate(chunks):
+            chunk(p, r)
+            if i % gap == gap - 1:
+                for _ in range(share):
+                    if pending:
+                        pending.pop(0)()
+        for work in pending:
+            work()
+    finish(plan.groups - 1)
+
+
+def attend_body(plan, pairwise, *refs):
+    own_ref = refs[0] if pairwise else None
+    refs = refs[1:] if pairwise else refs
+    moved_ref, k_ref, v_ref, term_ref, e_ref, eb_ref, out_ref, columns, block_ref, source, scores = refs
+    place_rows(plan, own_ref, moved_ref, block_ref, source)
+    rows, size, group = plan.rows, plan.head_size, plan.group
+    width = group * size
+    columns[...] = jnp.zeros_like(columns)
+
+    def product(p, j):
+        keys = k_ref[j : j + TILE, p * width : (p + 1) * width]
+        scores[p % 2, :, j : j + TILE] = nt(block_ref[p], keys)
+
+    def chunk(p, r):
+        h = p * group + r // rows
+        s = scores[p % 2, r : r + STEP] * plan.scale + term_ref[h : h + 1, :]
+        top = jnp.max(s, axis=1, keepdims=True)
+        e = jnp.exp(s - top)
+        e_ref[p, r : r + STEP, :] = e
+        eb_ref[p, r : r + STEP, :] = e.astype(BF16)
+        columns[r : r + STEP, p : p + 1] = top
+        columns[r : r + STEP, 8 + p : 9 + p] = jnp.sum(e, axis=1, keepdims=True)
+
+    def finish(p):
+        with_values = nn(eb_ref[p], v_ref[:, p * width : (p + 1) * width])
+        for q in range(group):
+            at, of = slice(q * rows, (q + 1) * rows), slice(q * size, (q + 1) * size)
+            out_ref[p * group + q] = with_values[at, of]
+
+    pipeline(plan, product, chunk, finish)
+
+
+def differ_body(plan, pairwise, *refs):
+    own_ref = refs[0] if pairwise else None
+    refs = refs[1:] if pairwise else refs
+    moved_ref, k_ref, v_ref, e_ref, eb_ref, out_ref, columns_ref = refs[:7]
+    part_ref, send_ref, stat_ref, yb_ref, block_ref, source, dprobs, columns = refs[7:]
+    place_rows(plan, own_ref, moved_ref, block_ref, source)
+    rows, size, group = plan.rows, plan.head_size, plan.group
+    width = group * size
+    columns[...] = columns_ref[...]
+    part_ref[0] = out_ref[...]
+
+    def product(p, j):
+        values = v_ref[j : j + TILE, p * width : (p + 1) * width]
+        dprobs[p % 2, :, j : j + TILE] = nt(block_ref[p], values)
+
+    def chunk(p, r):
+        e = e_ref[p, r : r + STEP, :]
+        d = dprobs[p % 2, r : r + STEP]
+        total = columns_ref[r : r + STEP, 8 + p : 9 + p]
+        mean = jnp.sum(e * d, axis=1, keepdims=True) / total
+        yb_ref[p, r : r + STEP, :] = (e * (d - mean)).astype(BF16)
+        columns[r : r + STEP, 16 + p : 17 + p] = mean
+
+    def finish(p):
+        both = jnp.concatenate([eb_ref[p], yb_ref[p]], axis=0)
+        with_keys = nn(both, k_ref[:, p * width : (p + 1) * width])
+        for a in range(2):
             for q in range(group):
-                block_ref[p, q * rows : (q + 1) * rows, q * size : (q + 1) * size] = ordered[
-                    :, q * size : (q + 1) * size
-                ]
-    columns[...] = jnp.zeros_like(columns)
-    step = 16
-    for p in range(plan.groups):
-        keys = k_ref[:, p * width : (p + 1) * width]
-        values = v_ref[:, p * width : (p + 1) * width]
-        scores[p % 2] = nt(qb_ref[p], keys)
-        dprobs[p % 2] = nt(gb_ref[p], values)
-        for r in range(0, plan.lanes, step):
-            h = p * group + r // rows
-            s = scores[p % 2, r : r + step] * plan.scale + term_ref[h : h + 1, :]
-            top = jnp.max(s, axis=1, keepdims=True)
-            e = jnp.exp(s - top)
-            total = jnp.sum(e, axis=1, keepdims=True)
-            d = dprobs[p % 2, r : r + step]
-            mean = jnp.sum(e * d, axis=1, keepdims=True) / total
-            pair_ref[p, r : r + step, :] = e.astype(BF16)
-            pair_ref[p, plan.lanes + r : plan.lanes + r + step, :] = (e * (d - mean)).astype(BF16)
-            columns[r : r + step, p : p + 1] = top
-            columns[r : r + step, 8 + p : 9 + p] = total
-            columns[r : r + step, 16 + p : 17 + p] = mean
-        with_values = nn(pair_ref[p, : plan.lanes, :], values)
-        with_keys = nn(pair_ref[p], keys)
-        for q in range(group):
-            at = slice(q * rows, (q + 1) * rows)
-            of = slice(q * size, (q + 1) * size)
-            part_ref[0, p * group + q] = with_values[at, of]
-            part_ref[1, p * group + q] = with_keys[at, of]
-            part_ref[2, p * group + q] = with_keys[plan.lanes + q * rows : plan.lanes + (q + 1) * rows, of]
+                start, of = a * plan.lanes + q * rows, slice(q * size, (q + 1) * size)
+                part_ref[1 + a, p * group + q] = with_keys[start : start + rows, of]
+
+    pipeline(plan, product, chunk, finish)
     give(plan, 0, part_ref, send_ref)
     stat_ref[...] = columns[...].T[:24]
 
@@ -269,12 +374,23 @@
             send_ref[a, h] = part_ref[a, h, gone, :].astype(BF16)
 
 
-def turn_body(pair_ref, turned_ref):
-    for p in range(pair_ref.shape[0]):
-        turned_ref[p] = pair_ref[p].T
-
-
-def backward_body(plan, stat_ref, stat_all_ref, qb_ref, gb_ref, turned_ref, dk_ref, dv_ref, table, dk, dv, semaphores):
+def gather_body(plan, own_ref, back_ref, attn_ref, dq_ref):
+    me = lax.axis_index("query")
+    for a, out_ref in ((0, attn_ref), (1, dq_ref)):
+        for at, ref in ((me, own_ref), (1 - me, back_ref)):
+            start = pl.multiple_of(at * plan.features, 128)
+            out_ref[:, pl.ds(start, plan.features)] = ref[a]
+
+
+def turn_body(eb_ref, yb_ref, turned_ref):
+    lanes = eb_ref.shape[1]
+    for p in range(eb_ref.shape[0]):
+        turned_ref[p, :, :lanes] = eb_ref[p].T
+        turned_ref[p, :, lanes:] = yb_ref[p].T
+
+
+def backward_body(plan, first, count, stat_ref, stat_all_ref, qb_ref, gb_ref, turned_ref, *refs):
+    dk_ref, dv_ref, table, dk, dv, semaphores = refs[-6:]
     lanes = plan.lanes
     width = dk.shape[2]
     total = stat_all_ref[8:16]
@@ -284,18 +400,18 @@
     rest = jnp.zeros((128 - 24, lanes), F32)
     table[...] = jnp.concatenate([f, f * plan.scale, c * plan.scale, rest], axis=0).T
     copies = []
-    for p in range(plan.groups):
+    for p in range(first, first + count):
         queries = qb_ref[p].astype(F32)
         wv = (gb_ref[p].astype(F32) * table[:, p : p + 1]).astype(BF16)
         wc = (queries * table[:, 16 + p : 17 + p]).astype(BF16)
         wf = (queries * table[:, 8 + p : 9 + p]).astype(BF16)
         for n, (buffer, target) in enumerate(((dk, dk_ref), (dv, dv_ref))):
             if n == 0:
-                buffer[p] = nn(turned_ref[p], jnp.concatenate([wc, wf], axis=0)).astype(BF16)
+                buffer[p - first] = nn(turned_ref[p], jnp.concatenate([wc, wf], axis=0)).astype(BF16)
             else:
-                buffer[p] = nn(turned_ref[p, :, :lanes], wv).astype(BF16)
+                buffer[p - first] = nn(turned_ref[p, :, :lanes], wv).astype(BF16)
             copy = pltpu.make_async_copy(
-                buffer.at[p], target.at[:, p * width : (p + 1) * width], semaphores.at[n, p]
+                buffer.at[p - first], target.at[:, p * width : (p + 1) * width], semaphores.at[n, p - first]
             )
             copy.start()
             copies.append(copy)
@@ -305,79 +421,103 @@
 
 def local(query_states, key_states, value_states, level_ids, level_bias, live_counts, out_grad):
     plan = Plan(query_states, key_states, level_bias)
-    qi = lax.axis_index("query")
     size, slots, lanes, groups, heads = plan.head_size, plan.slots, plan.lanes, plan.groups, plan.heads
     width = plan.group * size
     pairwise = plan.query_ways == 2
-    both = jnp.stack([query_states, out_grad])
+    own_shape = jax.ShapeDtypeStruct((plan.own_rows, plan.features), BF16)
+    pairwise = plan.query_ways == 2
+    in_hbm = lambda arrays: [pltpu.with_memory_space_constraint(x, pltpu.HBM) for x in arrays]
     if pairwise:
-        theirs = lax.dynamic_slice_in_dim(both, (1 - qi) * plan.features, plan.features, 2)
-        moved = lax.ppermute(theirs, "query", [(0, 1), (1, 0)])
+        their_queries, their_grads = call(
+            functools.partial(cut_body, plan),
+            [own_shape] * 2,
+            2,
+            10**6,
+            in_specs=[HBM] * 2,
+            out_specs=[VMEM] * 2,
+            scratch_shapes=[pltpu.SemaphoreType.DMA((2,))],
+            name="cut",
+        )(*in_hbm([query_states, out_grad]))
+        moved_queries = lax.ppermute(their_queries, "query", [(0, 1), (1, 0)])
+        moved_grads = lax.ppermute(their_grads, "query", [(0, 1), (1, 0)])
     else:
-        moved = lax.all_to_all(both, "query", split_axis=2, concat_axis=1, tiled=True)
-    table = lax.dynamic_slice_in_dim(level_bias, qi * heads, heads, 1)
-    term = jnp.zeros((heads, slots), F32)
-    for level in range(level_bias.shape[0]):
-        term = jnp.where(level_ids[None, :] == level, table[level][:, None], term)
-    slot = lax.broadcasted_iota(jnp.int32, (1, slots), 1)
-    term = jnp.where(slot < live_counts[0], term, -1e30)
+        moved_queries, moved_grads = (
+            lax.all_to_all(x, "query", split_axis=1, concat_axis=0, tiled=True)
+            for x in (query_states, out_grad)
+        )
 
     stat_shape = jax.ShapeDtypeStruct((24, lanes), F32)
     block_shape = jax.ShapeDtypeStruct((groups, lanes, width), BF16)
+    square_shape = lambda dtype: jax.ShapeDtypeStruct((groups, lanes, slots), dtype)
     part_shape = lambda k: jax.ShapeDtypeStruct((3, heads, plan.counts[k], size), F32)
     send_shape = lambda k: jax.ShapeDtypeStruct(
         (3, plan.sent_heads(k), plan.counts[k + 1], size), BF16
     )
-    from_hbm = [key_states, value_states] + ([query_states, out_grad] if pairwise else [])
-    from_hbm = [pltpu.with_memory_space_constraint(x, pltpu.HBM) for x in from_hbm]
-    own_shape = jax.ShapeDtypeStruct((plan.own_rows, plan.features), BF16)
     context_shape = jax.ShapeDtypeStruct(key_states.shape, BF16)
-    keys, values, *own_rows = call(
+    columns_shape = jax.ShapeDtypeStruct((lanes, 128), F32)
+    source_scratch = pltpu.VMEM((plan.rows, plan.features), BF16)
+    square_scratch = pltpu.VMEM((2, lanes, slots), F32)
+
+    def kernel(name, body, outs, ins, scratch, vmem_mib=4, flops=10**9):
+        single = not isinstance(outs, (tuple, list))
+        return call(
+            body,
+            outs,
+            vmem_mib,
+            flops,
+            in_specs=[VMEM] * len(ins),
+            out_specs=VMEM if single else [VMEM] * len(outs),
+            scratch_shapes=scratch,
+            name=name,
+        )(*ins)
+
+    from_hbm = [level_ids.reshape(1, slots), level_bias, key_states, value_states]
+    from_hbm += [query_states, out_grad] if pairwise else []
+    own_shapes = [own_shape] * 2 if pairwise else []
+    keys, values, *own, term = call(
         functools.partial(load_body, plan, pairwise),
-        [context_shape] * 2 + [own_shape] * (len(from_hbm) - 2),
+        [context_shape] * 2 + own_shapes + [jax.ShapeDtypeStruct((heads, slots), F32)],
         2,
         10**9,
-        in_specs=[HBM] * len(from_hbm),
-        out_specs=[VMEM] * len(from_hbm),
-        scratch_shapes=[pltpu.SemaphoreType.DMA((len(from_hbm),))],
+        in_specs=[pl.BlockSpec(memory_space=pltpu.SMEM)] + [HBM] * len(from_hbm),
+        out_specs=[VMEM] * (3 + len(own_shapes)),
+        scratch_shapes=[
+            pltpu.VMEM((1, slots), jnp.int32),
+            pltpu.SMEM(level_bias.shape, F32),
+            pltpu.SemaphoreType.DMA((len(from_hbm),)),
+        ],
         name="load",
-    )(*from_hbm)
-    part, send, stat_own, pair, qb, gb = call(
-        functools.partial(forward_body, plan, pairwise),
+    )(live_counts, *in_hbm(from_hbm))
+    own_queries, own_grads = ([own[0]], [own[1]]) if pairwise else ([], [])
+    e, eb, out, columns, qb = kernel(
+        "attend",
+        functools.partial(attend_body, plan, pairwise),
         (
-            part_shape(0),
-            send_shape(0),
-            stat_shape,
-            jax.ShapeDtypeStruct((groups, 2 * lanes, slots), BF16),
-            block_shape,
+            square_shape(F32),
+            square_shape(BF16),
+            jax.ShapeDtypeStruct((heads, plan.rows, size), F32),
+            columns_shape,
             block_shape,
         ),
-        12,
-        4 * 10**9,
-        in_specs=[VMEM] * (len(own_rows) + 4),
-        out_specs=[VMEM] * 6,
-        scratch_shapes=[
-            pltpu.VMEM((plan.rows, plan.features), BF16),
-            pltpu.VMEM((2, lanes, slots), F32),
-            pltpu.VMEM((2, lanes, slots), F32),
-            pltpu.VMEM((lanes, 128), F32),
-        ],
-        name="forward",
-    )(*own_rows, moved, keys, values, term)
-
-    turned = call(
-        turn_body,
-        jax.ShapeDtypeStruct((groups, slots, 2 * lanes), BF16),
-        4,
-        10**9,
-        in_specs=[VMEM],
-        out_specs=VMEM,
-        name="turn",
-    )(pair)
+        (*own_queries, moved_queries, keys, values, term),
+        [source_scratch, square_scratch],
+        vmem_mib=6,
+    )
+    part, send, stat_own, yb, gb = kernel(
+        "differ",
+        functools.partial(differ_body, plan, pairwise),
+        (part_shape(0), send_shape(0), stat_shape, square_shape(BF16), block_shape),
+        (*own_grads, moved_grads, keys, values, e, eb, out, columns),
+        [source_scratch, square_scratch, pltpu.VMEM((lanes, 128), F32)],
+        vmem_mib=6,
+    )
+    turned = kernel(
+        "turn", turn_body, jax.ShapeDtypeStruct((groups, slots, 2 * lanes), BF16), (eb, yb), []
+    )
 
     stat = stat_own
     for k in range(plan.rounds):
-        swap = [(i, i ^ (1 << k)) for i in range(plan.owner_ways)]
+        swap = plan.swap(k)
         stat_came = lax.ppermute(stat, "ctx", swap)
         came = lax.ppermute(send, "ctx", swap)
         merged = call(
@@ -410,29 +550,36 @@
         own, away = part, send
         back = lax.ppermute(away, "query", [(0, 1), (1, 0)])
 
-    key_grad, value_grad = call(
-        functools.partial(backward_body, plan),
-        (context_shape, context_shape),
-        12,
-        4 * 10**9,
-        in_specs=[VMEM] * 5,
-        out_specs=[HBM] * 2,
-        scratch_shapes=[
-            pltpu.VMEM((lanes, 128), F32),
-            pltpu.VMEM((groups, slots, width), BF16),
-            pltpu.VMEM((groups, slots, width), BF16),
-            pltpu.SemaphoreType.DMA((2, groups)),
-        ],
-        name="backward",
-    )(stat_own, stat, qb, gb, turned)
-
-    if pairwise:
-        first = jnp.where(qi == 0, own, back)
-        second = jnp.where(qi == 0, back, own)
-        final = jnp.concatenate([first, second], axis=2)
-    else:
+    def gradients(name, first, count, *into):
+        return call(
+            functools.partial(backward_body, plan, first, count),
+            (context_shape, context_shape),
+            8,
+            4 * 10**9,
+            in_specs=[VMEM] * 5 + [HBM] * len(into),
+            out_specs=[HBM] * 2,
+            scratch_shapes=[
+                pltpu.VMEM((lanes, 128), F32),
+                pltpu.VMEM((count, slots, width), BF16),
+                pltpu.VMEM((count, slots, width), BF16),
+                pltpu.SemaphoreType.DMA((2, count)),
+            ],
+            input_output_aliases={5 + n: n for n in range(len(into))},
+            name=name,
+        )(stat_own, stat, qb, gb, turned, *into)
+
+    split = (groups + 1) // 2
+    grads = gradients("backward0", 0, split)
+    key_grad, value_grad = gradients("backward1", split, groups - split, *grads)
+
+    if not pairwise:
         final = lax.all_to_all(part, "query", split_axis=1, concat_axis=2, tiled=True)
-    return final[0], final[1], key_grad, value_grad
+        return final[0], final[1], key_grad, value_grad
+    whole_rows = jax.ShapeDtypeStruct((plan.part_rows, 2 * plan.features), BF16)
+    attn, query_grad = kernel(
+        "gather", functools.partial(gather_body, plan), (whole_rows, whole_rows), (own, back), []
+    )
+    return attn, query_grad, key_grad, value_grad
 
 
 def solution(mesh):

time: 44.9 us -> 43 us (0.958)
  Pallas kernels: 13.9 us -> 16.8 us
  other arithmetic: 2.4 us -> 0 us
  waiting for transfers between devices: 12.7 us -> 10.9 us
  local copies, waits for them, and re-layouts: 1.72 us -> 0 us
  starting transfers between devices: 12.5 us -> 13.8 us
    pallas_call x3 -> x7, Pallas kernels: 8.88 us -> 12.4 us  [the longest x4 6.69 us: kernel(): call(body, outs, vmem_mib, flops, in_specs=[VMEM] * len(ins), out_specs=V...]
    ppermute x4, waiting for transfers between devices: 9.03 us -> 6.75 us  [local(): stat_came = lax.ppermute(stat, 'ctx', swap)]
    unnamed x14 -> x0, local copies, waits for them, and re-layouts: 1.63 us -> none
    ppermute x4, starting transfers between devices: 3.86 us -> 5.03 us  [local(): stat_came = lax.ppermute(stat, 'ctx', swap)]
    another operation x1 -> x0, other arithmetic: 0.96 us -> none  [local(): both = jnp.stack([query_states, out_grad])]
    ppermute x4, waiting for transfers between devices: 3.2 us -> 4.09 us  [local(): came = lax.ppermute(send, 'ctx', swap)]
    eq x1 -> x0, other arithmetic: 0.69 us -> none  [local(): term = jnp.where(level_ids[None, :] == level, table[level][:, None], term)]
    squeeze x1 -> x0, other arithmetic: 0.63 us -> none  [local(): return (final[0], final[1], key_grad, value_grad)]
  transfers between devices with their start and end apart: 10 -> 11, of which waited for: 6 -> 5; matrix products, arithmetic and copies ran while one was open for 2% -> 0% of each run, Pallas kernels for 17% -> 27%
where the time goes in v4:
time: 43 us; the launch traced here: 42.8 us
  Pallas kernels  16.8 us (39%)
  starting transfers between devices  13.8 us (32%)
  waiting for transfers between devices  10.9 us (25%)
  between operations  1.39 us (3%)
    ppermute x4, waiting for transfers between devices, local(): stat_came = lax.ppermute(stat, 'ctx', swap)  6.75 us
    pallas_call x4, Pallas kernels, kernel(): call(body, outs, vmem_mib, flops, in_specs=[VMEM] * len(ins), out_specs=V...  6.69 us
    ppermute x4, starting transfers between devices, local(): stat_came = lax.ppermute(stat, 'ctx', swap)  5.03 us
    pallas_call x2, Pallas kernels, gradients(): call(functools.partial(backward_body, plan, first, count), (context_shape...  4.7 us
    ppermute x4, waiting for transfers between devices, local(): came = lax.ppermute(send, 'ctx', swap)  4.09 us
    ppermute x4, starting transfers between devices, local(): came = lax.ppermute(send, 'ctx', swap)  4.04 us
    ppermute x1, starting transfers between devices, local(): moved_queries = lax.ppermute(their_queries, 'query', [(0, 1), (1, 0)])  3.06 us
    pallas_call x1, Pallas kernels, local(): call(functools.partial(load_body, plan, pairwise), [context_shape] * 2 +...  2.92 us
  transfers between devices with their start and end apart: 11, of which 5 were waited for; matrix products, arithmetic and copies ran while one was open for 0% of the time, Pallas kernels for 27%

profile of v4, /device:TPU:0, one launch (start us, length us, event | category | flops | bytes accessed | tf_op | source)
XLA Modules:
  0.0 42.8 jit_solution(3668325359710429384)
XLA Ops:
  0.6 1.0 %cut.1 = (bf16[32,1536]{1,0:T(8,128)(2,1)S(1)}, bf16[32,1536]{1,0:T(8,128)(2,1)S(1)}) custom-call(bf16[32,3072]{1,0:T(8,128)(2,1)} %q_ref.1, bf16[32,3072]{1,0:T(8,128)(2,1)} %g_ref.1), custom_call_target="tpu_custom_call" | custom-call | flops 1000000 | bytes 1048576 | tf_op jit(solution)/shard_map/cut/pallas_call | solution.py:431
  1.6 3.1 %collective-permute-start.1 = (bf16[32,1536]{1,0:T(8,128)(2,1)S(1)}, bf16[32,1536]{1,0:T(8,128)(2,1)S(1)}, u32[]{:S(2)}, u32[]{:S(2)}) collective-permute-start(bf16[32,1536]{1,0:T(8,128)(2,1)S(1)} %get-tuple-element.40), channel_id=1, source_target_pairs={{0,16},{16,0},{1,17},{17,1},{2,18},{18,2},{3,19},{19,3},{4,20},{20... | collective-permute-start | bytes 294920 | tf_op jit(solution)/shard_map/ppermute | solution.py:441
  4.7 0.1 collective-permute-start
  5.4 2.9 %load.1 = (bf16[1024,1536]{1,0:T(8,128)(2,1)S(1)}, bf16[1024,1536]{1,0:T(8,128)(2,1)S(1)}, bf16[32,1536]{1,0:T(8,128)(2,1)S(1)}, bf16[32,1536]{1,0:T(8,128)(2,1)S(1)}, f32[12,1024]{1,0:T(8,128)S(1)}) custom-call(s32[1]{0:T(128)S(6)} %copy.15.live_ref, s32[1,1024]{1,0:T(1,128)} %bitcast.1, f32[5,24]{1,0:T(8,128)} %refs_1_.1, bf16[1024,1536]{1,0:T(8,128)(2,1)} %refs_2_.1, ...), custom_call_target="tpu_custom_call" | custom-call | flops 1000000000 | bytes 1048576 | tf_op jit(solution)/shard_map/load/pallas_call | solution.py:477
  8.3 0.0 collective-permute-done.1.refs_1_
  8.3 2.4 %attend.1 = (f32[6,128,1024]{2,1,0:T(8,128)S(1)}, bf16[6,128,1024]{2,1,0:T(8,128)(2,1)S(1)}, f32[12,64,128]{2,1,0:T(8,128)S(1)}, f32[128,128]{1,0:T(8,128)S(1)}, bf16[6,128,256]{2,1,0:T(8,128)(2,1)S(1)}) custom-call(bf16[32,1536]{1,0:T(8,128)(2,1)S(1)} %get-tuple-element.39.refs_0_, bf16[32,1536]{1,0:T(8,128)(2,1)S(1)} %collective-permute-done.1.refs_1_, ...), custom_call_target="tpu_custom_call" | custom-call | flops 1000000000 | bytes 1048576 | tf_op jit(solution)/shard_map/attend/pallas_call | solution.py:463
  10.8 0.0 collective-permute-done.refs_1_
  10.8 2.8 %differ.1 = (f32[3,12,64,128]{3,2,1,0:T(8,128)S(1)}, bf16[3,12,32,128]{3,2,1,0:T(8,128)(2,1)S(1)}, f32[24,128]{1,0:T(8,128)S(1)}, bf16[6,128,1024]{2,1,0:T(8,128)(2,1)S(1)}, bf16[6,128,256]{2,1,0:T(8,128)(2,1)S(1)}) custom-call(bf16[32,1536]{1,0:T(8,128)(2,1)S(1)} %get-tuple-element.35.refs_0_, bf16[32,1536]{1,0:T(8,128)(2,1)S(1)} %collective-permute-done.refs_1_, ...), custom_call_target="tpu_custom_call" | custom-call | flops 1000000000 | bytes 1048576 | tf_op jit(solution)/shard_map/differ/pallas_call | solution.py:463
  13.6 0.1 collective-permute-start.2
  13.7 0.5 %collective-permute-start.3 = (f32[24,128]{1,0:T(8,128)S(1)}, f32[24,128]{1,0:T(8,128)S(1)}, u32[]{:S(2)}, u32[]{:S(2)}) collective-permute-start(f32[24,128]{1,0:T(8,128)S(1)} %get-tuple-element.48.stat_ref), channel_id=1, source_target_pairs={{0,1},{1,0},{2,3},{3,2},{4,5},{5,4},{6,7},{7,6},{8,9},{9,8},{10,11... | collective-permute-start | bytes 36872 | tf_op jit(solution)/shard_map/ppermute | solution.py:521
  14.1 1.1 %collective-permute-done.3.stat_came_ref = f32[24,128]{1,0:T(8,128)S(1)} collective-permute-done((f32[24,128]{1,0:T(8,128)S(1)}, f32[24,128]{1,0:T(8,128)S(1)}, u32[]{:S(2)}, u32[]{:S(2)}) %collective-permute-start.3) | collective-permute-done | bytes 12320 | tf_op jit(solution)/shard_map/ppermute | solution.py:521
  15.2 0.0 collective-permute-done.2.came_ref
  15.2 0.5 %merge0.1 = (f32[3,12,32,128]{3,2,1,0:T(8,128)S(1)}, bf16[3,12,16,128]{3,2,1,0:T(8,128)(2,1)S(1)}) custom-call(f32[3,12,64,128]{3,2,1,0:T(8,128)S(1)} %get-tuple-element.46.part_ref, bf16[3,12,32,128]{3,2,1,0:T(8,128)(2,1)S(1)} %collective-permute-done.2.came_ref, f32[24,128]{1,0:T(8,128)S(1)} %get-tuple-element.48.stat_ref, ...), custom_call_target="tpu_custom_call" | custom-call | flops 100000000 | bytes 1048576 | tf_op jit(solution)/shard_map/merge0/pallas_call | solution.py:538
  15.8 2.0 %collective-permute-start.4 = (bf16[3,12,16,128]{3,2,1,0:T(8,128)(2,1)S(1)}, bf16[3,12,16,128]{3,2,1,0:T(8,128)(2,1)S(1)}, u32[]{:S(2)}, u32[]{:S(2)}) collective-permute-start(bf16[3,12,16,128]{3,2,1,0:T(8,128)(2,1)S(1)} %get-tuple-element.50), channel_id=1, source_target_pairs={{0,2},{1,5},{2,0},{3,7},{4,6},{5,1},{6,4},{7,3},{8,10},{9,13},{10,... | collective-permute-start | bytes 442376 | tf_op jit(solution)/shard_map/ppermute | solution.py:522
  17.7 0.2 collective-permute-start.5
  17.9 3.6 %collective-permute-done.5.stat_came_ref = f32[24,128]{1,0:T(8,128)S(1)} collective-permute-done((f32[24,128]{1,0:T(8,128)S(1)}, f32[24,128]{1,0:T(8,128)S(1)}, u32[]{:S(2)}, u32[]{:S(2)}) %collective-permute-start.5) | collective-permute-done | bytes 12320 | tf_op jit(solution)/shard_map/ppermute | solution.py:521
  21.5 1.7 %collective-permute-start.7 = (f32[24,128]{1,0:T(8,128)S(1)}, f32[24,128]{1,0:T(8,128)S(1)}, u32[]{:S(2)}, u32[]{:S(2)}) collective-permute-start(f32[24,128]{1,0:T(8,128)S(1)} %statistics1.1.stat_ref), channel_id=1, source_target_pairs={{0,4},{1,3},{2,6},{3,1},{4,0},{5,7},{6,2},{7,5},{8,12},{9,11},{10,... | collective-permute-start | bytes 36872 | tf_op jit(solution)/shard_map/ppermute | solution.py:521
  23.2 2.1 %collective-permute-done.7.stat_came_ref = f32[24,128]{1,0:T(8,128)S(1)} collective-permute-done((f32[24,128]{1,0:T(8,128)S(1)}, f32[24,128]{1,0:T(8,128)S(1)}, u32[]{:S(2)}, u32[]{:S(2)}) %collective-permute-start.7) | collective-permute-done | bytes 12320 | tf_op jit(solution)/shard_map/ppermute | solution.py:521
  25.3 2.7 %collective-permute-start.9 = (f32[24,128]{1,0:T(8,128)S(1)}, f32[24,128]{1,0:T(8,128)S(1)}, u32[]{:S(2)}, u32[]{:S(2)}) collective-permute-start(f32[24,128]{1,0:T(8,128)S(1)} %statistics2.1.stat_ref), channel_id=1, source_target_pairs={{0,8},{1,9},{2,10},{3,11},{4,12},{5,13},{6,14},{7,15},{8,0},{9,1},... | collective-permute-start | bytes 36872 | tf_op jit(solution)/shard_map/ppermute | solution.py:521
  28.0 0.0 collective-permute-done.4.came_ref
  28.0 0.4 merge1.1
  28.4 1.6 %collective-permute-start.6 = (bf16[3,12,8,128]{3,2,1,0:T(8,128)(2,1)S(1)}, bf16[3,12,8,128]{3,2,1,0:T(8,128)(2,1)S(1)}, u32[]{:S(2)}, u32[]{:S(2)}) collective-permute-start(bf16[3,12,8,128]{3,2,1,0:T(8,128)(2,1)S(1)} %get-tuple-element.52), channel_id=1, source_target_pairs={{0,4},{1,3},{2,6},{3,1},{4,0},{5,7},{6,2},{7,5},{8,12},{9,11},{10,... | collective-permute-start | bytes 221192 | tf_op jit(solution)/shard_map/ppermute | solution.py:522
  30.0 0.9 %turn.1.turned_ref = bf16[6,1024,256]{2,1,0:T(8,128)(2,1)S(1)} custom-call(bf16[6,128,1024]{2,1,0:T(8,128)(2,1)S(1)} %get-tuple-element.43.refs_5_.eb_ref, bf16[6,128,1024]{2,1,0:T(8,128)(2,1)S(1)} %get-tuple-element.61.yb_ref), custom_call_target="tpu_custom_call" | custom-call | flops 1000000000 | bytes 1048576 | tf_op jit(solution)/shard_map/turn/pallas_call | solution.py:463
  30.8 0.0 collective-permute-done.9.stat_came_ref
  30.9 1.9 %collective-permute-done.6.came_ref = bf16[3,12,8,128]{3,2,1,0:T(8,128)(2,1)S(1)} collective-permute-done((bf16[3,12,8,128]{3,2,1,0:T(8,128)(2,1)S(1)}, bf16[3,12,8,128]{3,2,1,0:T(8,128)(2,1)S(1)}, u32[]{:S(2)}, u32[]{:S(2)}) %collective-permute-start.6) | collective-permute-done | bytes 73760 | tf_op jit(solution)/shard_map/ppermute | solution.py:522
  32.8 0.3 merge2.1
  33.1 0.4 collective-permute-start.8
  33.4 2.3 %backward0.1 = (bf16[1024,1536]{1,0:T(8,128)(2,1)}, bf16[1024,1536]{1,0:T(8,128)(2,1)}) custom-call(f32[24,128]{1,0:T(8,128)S(1)} %get-tuple-element.48.stat_ref, f32[24,128]{1,0:T(8,128)S(1)} %statistics3.1.stat_all_ref, bf16[6,128,256]{2,1,0:T(8,128)(2,1)S(1)} %get-tuple-element.59.qb_ref, bf16[6,128,256]{2,1,0:T(8,128)(2,1)S(1)} %get-tuple-element.60.gb_ref, ...), custom_call_target="tpu_custom_call" | custom-call | flops 4000000000 | bytes 1048576 | tf_op jit(solution)/shard_map/backward0/pallas_call | solution.py:554
  35.8 2.2 %collective-permute-done.8.came_ref = bf16[3,6,8,128]{3,2,1,0:T(8,128)(2,1)S(1)} collective-permute-done((bf16[3,6,8,128]{3,2,1,0:T(8,128)(2,1)S(1)}, bf16[3,6,8,128]{3,2,1,0:T(8,128)(2,1)S(1)}, u32[]{:S(2)}, u32[]{:S(2)}) %collective-permute-start.8) | collective-permute-done | bytes 36896 | tf_op jit(solution)/shard_map/ppermute | solution.py:522
  38.0 0.3 merge3.1
  38.3 1.6 %collective-permute-start.10 = (bf16[2,2,1536]{2,1,0:T(2,128)(2,1)S(1)}, bf16[2,2,1536]{2,1,0:T(2,128)(2,1)S(1)}, u32[]{:S(2)}, u32[]{:S(2)}) collective-permute-start(bf16[2,2,1536]{2,1,0:T(2,128)(2,1)S(1)} %get-tuple-element.56), channel_id=1, source_target_pairs={{0,16},{16,0},{1,17},{17,1},{2,18},{18,2},{3,19},{19,3},{4,20},{20... | collective-permute-start | bytes 36872 | tf_op jit(solution)/shard_map/ppermute | solution.py:551
  39.8 2.4 %backward1.1 = (bf16[1024,1536]{1,0:T(8,128)(2,1)}, bf16[1024,1536]{1,0:T(8,128)(2,1)}) custom-call(f32[24,128]{1,0:T(8,128)S(1)} %get-tuple-element.48.stat_ref, f32[24,128]{1,0:T(8,128)S(1)} %statistics3.1.stat_all_ref, bf16[6,128,256]{2,1,0:T(8,128)(2,1)S(1)} %get-tuple-element.59.qb_ref, ...), custom_call_target="tpu_custom_call", output_to_operand_aliasing={{0}: (5, {}), {1}: (6, {})} | custom-call | flops 4000000000 | bytes 1048576 | tf_op jit(solution)/shard_map/backward1/pallas_call | solution.py:554
  42.2 0.0 collective-permute-done.10.back_ref
  42.2 0.6 %gather.1 = (bf16[2,3072]{1,0:T(2,128)(2,1)}, bf16[2,3072]{1,0:T(2,128)(2,1)}) custom-call(bf16[2,2,1536]{2,1,0:T(2,128)(2,1)S(1)} %get-tuple-element.55.own_ref, bf16[2,2,1536]{2,1,0:T(2,128)(2,1)S(1)} %collective-permute-done.10.back_ref), custom_call_target="tpu_custom_call" | custom-call | flops 1000000000 | bytes 1048576 | tf_op jit(solution)/shard_map/gather/pallas_call | solution.py:463
  (4 shorter events, 0.1 us)
Async XLA Ops:
  1.6 6.7 %collective-permute-start.1 = (bf16[32,1536]{1,0:T(8,128)(2,1)S(1)}, bf16[32,1536]{1,0:T(8,128)(2,1)S(1)}, u32[]{:S(2)}, u32[]{:S(2)}) collective-permute-start(bf16[32,1536]{1,0:T(8,128)(2,1)S(1)} %get-tuple-element.40), channel_id=1, source_target_pairs={{0,16},{16,0},{1,17},{17,1},{2,18},{18,2},{3,19},{19,3},{4,20},{20... | collective-permute-start | bytes 294920 | tf_op jit(solution)/shard_map/ppermute | solution.py:441
  4.7 6.1 %collective-permute-start = (bf16[32,1536]{1,0:T(8,128)(2,1)S(1)}, bf16[32,1536]{1,0:T(8,128)(2,1)S(1)}, u32[]{:S(2)}, u32[]{:S(2)}) collective-permute-start(bf16[32,1536]{1,0:T(8,128)(2,1)S(1)} %get-tuple-element.36), channel_id=1, source_target_pairs={{0,16},{16,0},{1,17},{17,1},{2,18},{18,2},{3,19},{19,3},{4,20},{20... | collective-permute-start | bytes 294920 | tf_op jit(solution)/shard_map/ppermute | solution.py:442
  13.6 1.7 %collective-permute-start.2 = (bf16[3,12,32,128]{3,2,1,0:T(8,128)(2,1)S(1)}, bf16[3,12,32,128]{3,2,1,0:T(8,128)(2,1)S(1)}, u32[]{:S(2)}, u32[]{:S(2)}) collective-permute-start(bf16[3,12,32,128]{3,2,1,0:T(8,128)(2,1)S(1)} %get-tuple-element.47), channel_id=1, source_target_pairs={{0,1},{1,0},{2,3},{3,2},{4,5},{5,4},{6,7},{7,6},{8,9},{9,8},{10,11... | collective-permute-start | bytes 884744 | tf_op jit(solution)/shard_map/ppermute | solution.py:522
  13.7 1.6 %collective-permute-start.3 = (f32[24,128]{1,0:T(8,128)S(1)}, f32[24,128]{1,0:T(8,128)S(1)}, u32[]{:S(2)}, u32[]{:S(2)}) collective-permute-start(f32[24,128]{1,0:T(8,128)S(1)} %get-tuple-element.48.stat_ref), channel_id=1, source_target_pairs={{0,1},{1,0},{2,3},{3,2},{4,5},{5,4},{6,7},{7,6},{8,9},{9,8},{10,11... | collective-permute-start | bytes 36872 | tf_op jit(solution)/shard_map/ppermute | solution.py:521
  15.8 12.2 %collective-permute-start.4 = (bf16[3,12,16,128]{3,2,1,0:T(8,128)(2,1)S(1)}, bf16[3,12,16,128]{3,2,1,0:T(8,128)(2,1)S(1)}, u32[]{:S(2)}, u32[]{:S(2)}) collective-permute-start(bf16[3,12,16,128]{3,2,1,0:T(8,128)(2,1)S(1)} %get-tuple-element.50), channel_id=1, source_target_pairs={{0,2},{1,5},{2,0},{3,7},{4,6},{5,1},{6,4},{7,3},{8,10},{9,13},{10,... | collective-permute-start | bytes 442376 | tf_op jit(solution)/shard_map/ppermute | solution.py:522
  17.7 3.8 %collective-permute-start.5 = (f32[24,128]{1,0:T(8,128)S(1)}, f32[24,128]{1,0:T(8,128)S(1)}, u32[]{:S(2)}, u32[]{:S(2)}) collective-permute-start(f32[24,128]{1,0:T(8,128)S(1)} %statistics0.1.stat_ref), channel_id=1, source_target_pairs={{0,2},{1,5},{2,0},{3,7},{4,6},{5,1},{6,4},{7,3},{8,10},{9,13},{10,... | collective-permute-start | bytes 36872 | tf_op jit(solution)/shard_map/ppermute | solution.py:521
  21.5 3.8 %collective-permute-start.7 = (f32[24,128]{1,0:T(8,128)S(1)}, f32[24,128]{1,0:T(8,128)S(1)}, u32[]{:S(2)}, u32[]{:S(2)}) collective-permute-start(f32[24,128]{1,0:T(8,128)S(1)} %statistics1.1.stat_ref), channel_id=1, source_target_pairs={{0,4},{1,3},{2,6},{3,1},{4,0},{5,7},{6,2},{7,5},{8,12},{9,11},{10,... | collective-permute-start | bytes 36872 | tf_op jit(solution)/shard_map/ppermute | solution.py:521
  25.3 5.6 %collective-permute-start.9 = (f32[24,128]{1,0:T(8,128)S(1)}, f32[24,128]{1,0:T(8,128)S(1)}, u32[]{:S(2)}, u32[]{:S(2)}) collective-permute-start(f32[24,128]{1,0:T(8,128)S(1)} %statistics2.1.stat_ref), channel_id=1, source_target_pairs={{0,8},{1,9},{2,10},{3,11},{4,12},{5,13},{6,14},{7,15},{8,0},{9,1},... | collective-permute-start | bytes 36872 | tf_op jit(solution)/shard_map/ppermute | solution.py:521
  28.4 4.4 %collective-permute-start.6 = (bf16[3,12,8,128]{3,2,1,0:T(8,128)(2,1)S(1)}, bf16[3,12,8,128]{3,2,1,0:T(8,128)(2,1)S(1)}, u32[]{:S(2)}, u32[]{:S(2)}) collective-permute-start(bf16[3,12,8,128]{3,2,1,0:T(8,128)(2,1)S(1)} %get-tuple-element.52), channel_id=1, source_target_pairs={{0,4},{1,3},{2,6},{3,1},{4,0},{5,7},{6,2},{7,5},{8,12},{9,11},{10,... | collective-permute-start | bytes 221192 | tf_op jit(solution)/shard_map/ppermute | solution.py:522
  33.1 4.9 %collective-permute-start.8 = (bf16[3,6,8,128]{3,2,1,0:T(8,128)(2,1)S(1)}, bf16[3,6,8,128]{3,2,1,0:T(8,128)(2,1)S(1)}, u32[]{:S(2)}, u32[]{:S(2)}) collective-permute-start(bf16[3,6,8,128]{3,2,1,0:T(8,128)(2,1)S(1)} %get-tuple-element.54), channel_id=1, source_target_pairs={{0,8},{1,9},{2,10},{3,11},{4,12},{5,13},{6,14},{7,15},{8,0},{9,1},... | collective-permute-start | bytes 110600 | tf_op jit(solution)/shard_map/ppermute | solution.py:522
  38.3 3.9 %collective-permute-start.10 = (bf16[2,2,1536]{2,1,0:T(2,128)(2,1)S(1)}, bf16[2,2,1536]{2,1,0:T(2,128)(2,1)S(1)}, u32[]{:S(2)}, u32[]{:S(2)}) collective-permute-start(bf16[2,2,1536]{2,1,0:T(2,128)(2,1)S(1)} %get-tuple-element.56), channel_id=1, source_target_pairs={{0,16},{16,0},{1,17},{17,1},{2,18},{18,2},{3,19},{19,3},{4,20},{20... | collective-permute-start | bytes 36872 | tf_op jit(solution)/shard_map/ppermute | solution.py:551

commit v5 on v4

--- a/solution.py
+++ b/solution.py
@@ -126,17 +126,18 @@
         copy.wait()
 
 
-def load_body(plan, pairwise, live_ref, *refs):
+def load_body(plan, pairwise, *refs):
     count = 6 if pairwise else 4
     ids_hbm, bias_hbm, k_hbm, v_hbm, *rows_hbm = refs[:count]
-    k_ref, v_ref, *rows_refs, term_ref, ids_ref, bias_ref, semaphores = refs[count:]
+    k_ref, v_ref, kt_ref, *rows_refs, term_ref, ids_ref, bias_ref, semaphores = refs[count:]
     me = lax.axis_index("query")
+    pieces = [slice(j, j + PIECE) for j in range(0, plan.slots, PIECE)]
+    parts = [(k_hbm, k_ref, kt_ref, of) for of in pieces] + [(v_hbm, v_ref, None, of) for of in pieces]
     copies = copy_all(
         [
             (ids_hbm, ids_ref),
             (bias_hbm, bias_ref),
-            (k_hbm, k_ref),
-            (v_hbm, v_ref),
+            *((source.at[of], target.at[of]) for source, target, _, of in parts),
             *((columns_at(plan, source, me), target) for source, target in zip(rows_hbm, rows_refs)),
         ],
         semaphores,
@@ -144,15 +145,23 @@
     for copy in copies[:2]:
         copy.wait()
     ids = ids_ref[...]
-    live = lax.broadcasted_iota(jnp.int32, ids.shape, 1) < live_ref[0]
     masks = [ids == level for level in range(bias_ref.shape[0])]
     for h in range(plan.heads):
         row = jnp.zeros(ids.shape, F32)
         for level, mask in enumerate(masks):
             row = jnp.where(mask, bias_ref[level, me * plan.heads + h], row)
-        term_ref[h : h + 1, :] = jnp.where(live, row, -1e30)
-    for copy in copies[2:]:
+        term_ref[h : h + 1, :] = row
+    for copy, (_, target, turned, of) in zip(copies[2:], parts):
         copy.wait()
+        if turned is not None:
+            turned[:, of] = target[of].T
+    for copy in copies[2 + len(parts) :]:
+        copy.wait()
+
+
+def mask_body(live_ref, term_ref, masked_ref):
+    slot = lax.broadcasted_iota(jnp.int32, term_ref.shape, 1)
+    masked_ref[...] = jnp.where(slot < live_ref[0], term_ref[...], -1e30)
 
 
 def row_order(plan):
@@ -192,6 +201,7 @@
 
 
 STEP = 16
+PIECE = 256
 TILE = 256
 
 
@@ -220,15 +230,14 @@
 def attend_body(plan, pairwise, *refs):
     own_ref = refs[0] if pairwise else None
     refs = refs[1:] if pairwise else refs
-    moved_ref, k_ref, v_ref, term_ref, e_ref, eb_ref, out_ref, columns, block_ref, source, scores = refs
+    moved_ref, kt_ref, v_ref, term_ref, e_ref, eb_ref, out_ref, columns, block_ref, source, scores = refs
     place_rows(plan, own_ref, moved_ref, block_ref, source)
     rows, size, group = plan.rows, plan.head_size, plan.group
     width = group * size
     columns[...] = jnp.zeros_like(columns)
 
     def product(p, j):
-        keys = k_ref[j : j + TILE, p * width : (p + 1) * width]
-        scores[p % 2, :, j : j + TILE] = nt(block_ref[p], keys)
+        scores[p % 2, :, j : j + TILE] = nn(block_ref[p], kt_ref[p * width : (p + 1) * width, j : j + TILE])
 
     def chunk(p, r):
         h = p * group + r // rows
@@ -252,7 +261,7 @@
 def differ_body(plan, pairwise, *refs):
     own_ref = refs[0] if pairwise else None
     refs = refs[1:] if pairwise else refs
-    moved_ref, k_ref, v_ref, e_ref, eb_ref, out_ref, columns_ref = refs[:7]
+    moved_ref, k_ref, vt_ref, e_ref, eb_ref, out_ref, columns_ref = refs[:7]
     part_ref, send_ref, stat_ref, yb_ref, block_ref, source, dprobs, columns = refs[7:]
     place_rows(plan, own_ref, moved_ref, block_ref, source)
     rows, size, group = plan.rows, plan.head_size, plan.group
@@ -261,8 +270,7 @@
     part_ref[0] = out_ref[...]
 
     def product(p, j):
-        values = v_ref[j : j + TILE, p * width : (p + 1) * width]
-        dprobs[p % 2, :, j : j + TILE] = nt(block_ref[p], values)
+        dprobs[p % 2, :, j : j + TILE] = nt(block_ref[p], vt_ref[j : j + TILE, p * width : (p + 1) * width])
 
     def chunk(p, r):
         e = e_ref[p, r : r + STEP, :]
@@ -474,20 +482,31 @@
     from_hbm = [level_ids.reshape(1, slots), level_bias, key_states, value_states]
     from_hbm += [query_states, out_grad] if pairwise else []
     own_shapes = [own_shape] * 2 if pairwise else []
-    keys, values, *own, term = call(
+    turned_shape = jax.ShapeDtypeStruct((plan.features, slots), BF16)
+    term_shape = jax.ShapeDtypeStruct((heads, slots), F32)
+    keys, values, keys_turned, *own, term = call(
         functools.partial(load_body, plan, pairwise),
-        [context_shape] * 2 + own_shapes + [jax.ShapeDtypeStruct((heads, slots), F32)],
-        2,
+        [context_shape] * 2 + [turned_shape] + own_shapes + [term_shape],
+        4,
         10**9,
-        in_specs=[pl.BlockSpec(memory_space=pltpu.SMEM)] + [HBM] * len(from_hbm),
-        out_specs=[VMEM] * (3 + len(own_shapes)),
+        in_specs=[HBM] * len(from_hbm),
+        out_specs=[VMEM] * (4 + len(own_shapes)),
         scratch_shapes=[
             pltpu.VMEM((1, slots), jnp.int32),
             pltpu.SMEM(level_bias.shape, F32),
-            pltpu.SemaphoreType.DMA((len(from_hbm),)),
+            pltpu.SemaphoreType.DMA((len(from_hbm) - 2 + 2 * slots // PIECE,)),
         ],
         name="load",
-    )(live_counts, *in_hbm(from_hbm))
+    )(*in_hbm(from_hbm))
+    term = call(
+        mask_body,
+        term_shape,
+        2,
+        10**6,
+        in_specs=[pl.BlockSpec(memory_space=pltpu.SMEM), VMEM],
+        out_specs=VMEM,
+        name="mask",
+    )(live_counts, term)
     own_queries, own_grads = ([own[0]], [own[1]]) if pairwise else ([], [])
     e, eb, out, columns, qb = kernel(
         "attend",
@@ -499,7 +518,7 @@
             columns_shape,
             block_shape,
         ),
-        (*own_queries, moved_queries, keys, values, term),
+        (*own_queries, moved_queries, keys_turned, values, term),
         [source_scratch, square_scratch],
         vmem_mib=6,
     )

time: 43 us -> 42.7 us (level)
  transfers between devices with their start and end apart: 11 -> 11, of which waited for: 5 -> 5; matrix products, arithmetic and copies ran while one was open for 0% -> 0% of each run, Pallas kernels for 27% -> 26%
where the time goes in v5:
time: 42.7 us; the launch traced here: 42.5 us
  Pallas kernels  16.5 us (39%)
  starting transfers between devices  13.8 us (32%)
  waiting for transfers between devices  10.8 us (25%)
  between operations  1.4 us (3%)
    ppermute x4, waiting for transfers between devices, local(): stat_came = lax.ppermute(stat, 'ctx', swap)  6.76 us
    pallas_call x4, Pallas kernels, kernel(): call(body, outs, vmem_mib, flops, in_specs=[VMEM] * len(ins), out_specs=V...  6.33 us
    ppermute x4, starting transfers between devices, local(): stat_came = lax.ppermute(stat, 'ctx', swap)  5.02 us
    pallas_call x2, Pallas kernels, gradients(): call(functools.partial(backward_body, plan, first, count), (context_shape...  4.7 us
    ppermute x4, waiting for transfers between devices, local(): came = lax.ppermute(send, 'ctx', swap)  4.07 us
    ppermute x4, starting transfers between devices, local(): came = lax.ppermute(send, 'ctx', swap)  4.05 us
    ppermute x1, starting transfers between devices, local(): moved_queries = lax.ppermute(their_queries, 'query', [(0, 1), (1, 0)])  3.06 us
    pallas_call x1, Pallas kernels, local(): call(functools.partial(load_body, plan, pairwise), [context_shape] * 2 +...  2.94 us
  transfers between devices with their start and end apart: 11, of which 5 were waited for; matrix products, arithmetic and copies ran while one was open for 0% of the time, Pallas kernels for 26%

profile of v5, /device:TPU:0, one launch (start us, length us, event | category | flops | bytes accessed | tf_op | source)
XLA Modules:
  0.0 42.5 jit_solution(14525537990755989716)
XLA Ops:
  0.6 1.0 %cut.1 = (bf16[32,1536]{1,0:T(8,128)(2,1)S(1)}, bf16[32,1536]{1,0:T(8,128)(2,1)S(1)}) custom-call(bf16[32,3072]{1,0:T(8,128)(2,1)} %q_ref.1, bf16[32,3072]{1,0:T(8,128)(2,1)} %g_ref.1), custom_call_target="tpu_custom_call" | custom-call | flops 1000000 | bytes 1048576 | tf_op jit(solution)/shard_map/cut/pallas_call | solution.py:439
  1.6 3.1 %collective-permute-start.1 = (bf16[32,1536]{1,0:T(8,128)(2,1)S(1)}, bf16[32,1536]{1,0:T(8,128)(2,1)S(1)}, u32[]{:S(2)}, u32[]{:S(2)}) collective-permute-start(bf16[32,1536]{1,0:T(8,128)(2,1)S(1)} %get-tuple-element.41), channel_id=1, source_target_pairs={{0,16},{16,0},{1,17},{17,1},{2,18},{18,2},{3,19},{19,3},{4,20},{20... | collective-permute-start | bytes 294920 | tf_op jit(solution)/shard_map/ppermute | solution.py:449
  4.7 0.1 collective-permute-start
  4.7 2.9 %load.1 = (bf16[1024,1536]{1,0:T(8,128)(2,1)S(1)}, bf16[1024,1536]{1,0:T(8,128)(2,1)S(1)}, bf16[1536,1024]{1,0:T(8,128)(2,1)S(1)}, bf16[32,1536]{1,0:T(8,128)(2,...) custom-call(s32[1,1024]{1,0:T(1,128)} %bitcast.1, f32[5,24]{1,0:T(8,128)} %refs_1_.1, ...), custom_call_target="tpu_custom_call" | custom-call | flops 1000000000 | bytes 1048576 | tf_op jit(solution)/shard_map/load/pallas_call | solution.py:487
  8.4 0.0 collective-permute-done.1.refs_1_
  8.4 2.1 %attend.1 = (f32[6,128,1024]{2,1,0:T(8,128)S(1)}, bf16[6,128,1024]{2,1,0:T(8,128)(2,1)S(1)}, f32[12,64,128]{2,1,0:T(8,128)S(1)}, f32[128,128]{1,0:T(8,128)S(1)}, bf16[6,128,256]{2,1,0:T(8,128)(2,1)S(1)}) custom-call(bf16[32,1536]{1,0:T(8,128)(2,1)S(1)} %get-tuple-element.40.refs_0_, bf16[32,1536]{1,0:T(8,128)(2,1)S(1)} %collective-permute-done.1.refs_1_, ...), custom_call_target="tpu_custom_call" | custom-call | flops 1000000000 | bytes 1048576 | tf_op jit(solution)/shard_map/attend/pallas_call | solution.py:471
  10.5 0.0 collective-permute-done.refs_1_
  10.5 2.8 %differ.1 = (f32[3,12,64,128]{3,2,1,0:T(8,128)S(1)}, bf16[3,12,32,128]{3,2,1,0:T(8,128)(2,1)S(1)}, f32[24,128]{1,0:T(8,128)S(1)}, bf16[6,128,1024]{2,1,0:T(8,128)(2,1)S(1)}, bf16[6,128,256]{2,1,0:T(8,128)(2,1)S(1)}) custom-call(bf16[32,1536]{1,0:T(8,128)(2,1)S(1)} %get-tuple-element.36.refs_0_, bf16[32,1536]{1,0:T(8,128)(2,1)S(1)} %collective-permute-done.refs_1_, ...), custom_call_target="tpu_custom_call" | custom-call | flops 1000000000 | bytes 1048576 | tf_op jit(solution)/shard_map/differ/pallas_call | solution.py:471
  13.2 0.1 collective-permute-start.2
  13.3 0.5 %collective-permute-start.3 = (f32[24,128]{1,0:T(8,128)S(1)}, f32[24,128]{1,0:T(8,128)S(1)}, u32[]{:S(2)}, u32[]{:S(2)}) collective-permute-start(f32[24,128]{1,0:T(8,128)S(1)} %get-tuple-element.50.stat_ref), channel_id=1, source_target_pairs={{0,1},{1,0},{2,3},{3,2},{4,5},{5,4},{6,7},{7,6},{8,9},{9,8},{10,11... | collective-permute-start | bytes 36872 | tf_op jit(solution)/shard_map/ppermute | solution.py:540
  13.8 1.1 %collective-permute-done.3.stat_came_ref = f32[24,128]{1,0:T(8,128)S(1)} collective-permute-done((f32[24,128]{1,0:T(8,128)S(1)}, f32[24,128]{1,0:T(8,128)S(1)}, u32[]{:S(2)}, u32[]{:S(2)}) %collective-permute-start.3) | collective-permute-done | bytes 12320 | tf_op jit(solution)/shard_map/ppermute | solution.py:540
  14.9 0.0 collective-permute-done.2.came_ref
  14.9 0.5 %merge0.1 = (f32[3,12,32,128]{3,2,1,0:T(8,128)S(1)}, bf16[3,12,16,128]{3,2,1,0:T(8,128)(2,1)S(1)}) custom-call(f32[3,12,64,128]{3,2,1,0:T(8,128)S(1)} %get-tuple-element.48.part_ref, bf16[3,12,32,128]{3,2,1,0:T(8,128)(2,1)S(1)} %collective-permute-done.2.came_ref, f32[24,128]{1,0:T(8,128)S(1)} %get-tuple-element.50.stat_ref, ...), custom_call_target="tpu_custom_call" | custom-call | flops 100000000 | bytes 1048576 | tf_op jit(solution)/shard_map/merge0/pallas_call | solution.py:557
  15.4 2.0 %collective-permute-start.4 = (bf16[3,12,16,128]{3,2,1,0:T(8,128)(2,1)S(1)}, bf16[3,12,16,128]{3,2,1,0:T(8,128)(2,1)S(1)}, u32[]{:S(2)}, u32[]{:S(2)}) collective-permute-start(bf16[3,12,16,128]{3,2,1,0:T(8,128)(2,1)S(1)} %get-tuple-element.52), channel_id=1, source_target_pairs={{0,2},{1,5},{2,0},{3,7},{4,6},{5,1},{6,4},{7,3},{8,10},{9,13},{10,... | collective-permute-start | bytes 442376 | tf_op jit(solution)/shard_map/ppermute | solution.py:541
  17.4 0.2 collective-permute-start.5
  17.6 3.6 %collective-permute-done.5.stat_came_ref = f32[24,128]{1,0:T(8,128)S(1)} collective-permute-done((f32[24,128]{1,0:T(8,128)S(1)}, f32[24,128]{1,0:T(8,128)S(1)}, u32[]{:S(2)}, u32[]{:S(2)}) %collective-permute-start.5) | collective-permute-done | bytes 12320 | tf_op jit(solution)/shard_map/ppermute | solution.py:540
  21.2 1.7 %collective-permute-start.7 = (f32[24,128]{1,0:T(8,128)S(1)}, f32[24,128]{1,0:T(8,128)S(1)}, u32[]{:S(2)}, u32[]{:S(2)}) collective-permute-start(f32[24,128]{1,0:T(8,128)S(1)} %statistics1.1.stat_ref), channel_id=1, source_target_pairs={{0,4},{1,3},{2,6},{3,1},{4,0},{5,7},{6,2},{7,5},{8,12},{9,11},{10,... | collective-permute-start | bytes 36872 | tf_op jit(solution)/shard_map/ppermute | solution.py:540
  22.8 2.1 %collective-permute-done.7.stat_came_ref = f32[24,128]{1,0:T(8,128)S(1)} collective-permute-done((f32[24,128]{1,0:T(8,128)S(1)}, f32[24,128]{1,0:T(8,128)S(1)}, u32[]{:S(2)}, u32[]{:S(2)}) %collective-permute-start.7) | collective-permute-done | bytes 12320 | tf_op jit(solution)/shard_map/ppermute | solution.py:540
  24.9 2.7 %collective-permute-start.9 = (f32[24,128]{1,0:T(8,128)S(1)}, f32[24,128]{1,0:T(8,128)S(1)}, u32[]{:S(2)}, u32[]{:S(2)}) collective-permute-start(f32[24,128]{1,0:T(8,128)S(1)} %statistics2.1.stat_ref), channel_id=1, source_target_pairs={{0,8},{1,9},{2,10},{3,11},{4,12},{5,13},{6,14},{7,15},{8,0},{9,1},... | collective-permute-start | bytes 36872 | tf_op jit(solution)/shard_map/ppermute | solution.py:540
  27.6 0.0 collective-permute-done.4.came_ref
  27.6 0.4 merge1.1
  28.0 1.6 %collective-permute-start.6 = (bf16[3,12,8,128]{3,2,1,0:T(8,128)(2,1)S(1)}, bf16[3,12,8,128]{3,2,1,0:T(8,128)(2,1)S(1)}, u32[]{:S(2)}, u32[]{:S(2)}) collective-permute-start(bf16[3,12,8,128]{3,2,1,0:T(8,128)(2,1)S(1)} %get-tuple-element.54), channel_id=1, source_target_pairs={{0,4},{1,3},{2,6},{3,1},{4,0},{5,7},{6,2},{7,5},{8,12},{9,11},{10,... | collective-permute-start | bytes 221192 | tf_op jit(solution)/shard_map/ppermute | solution.py:541
  29.6 0.9 %turn.1.turned_ref = bf16[6,1024,256]{2,1,0:T(8,128)(2,1)S(1)} custom-call(bf16[6,128,1024]{2,1,0:T(8,128)(2,1)S(1)} %get-tuple-element.45.refs_5_.eb_ref, bf16[6,128,1024]{2,1,0:T(8,128)(2,1)S(1)} %get-tuple-element.63.yb_ref), custom_call_target="tpu_custom_call" | custom-call | flops 1000000000 | bytes 1048576 | tf_op jit(solution)/shard_map/turn/pallas_call | solution.py:471
  30.5 0.0 collective-permute-done.9.stat_came_ref
  30.5 1.9 %collective-permute-done.6.came_ref = bf16[3,12,8,128]{3,2,1,0:T(8,128)(2,1)S(1)} collective-permute-done((bf16[3,12,8,128]{3,2,1,0:T(8,128)(2,1)S(1)}, bf16[3,12,8,128]{3,2,1,0:T(8,128)(2,1)S(1)}, u32[]{:S(2)}, u32[]{:S(2)}) %collective-permute-start.6) | collective-permute-done | bytes 73760 | tf_op jit(solution)/shard_map/ppermute | solution.py:541
  32.4 0.3 merge2.1
  32.7 0.4 collective-permute-start.8
  33.1 2.4 %backward0.1 = (bf16[1024,1536]{1,0:T(8,128)(2,1)}, bf16[1024,1536]{1,0:T(8,128)(2,1)}) custom-call(f32[24,128]{1,0:T(8,128)S(1)} %get-tuple-element.50.stat_ref, f32[24,128]{1,0:T(8,128)S(1)} %statistics3.1.stat_all_ref, bf16[6,128,256]{2,1,0:T(8,128)(2,1)S(1)} %get-tuple-element.61.qb_ref, bf16[6,128,256]{2,1,0:T(8,128)(2,1)S(1)} %get-tuple-element.62.gb_ref, ...), custom_call_target="tpu_custom_call" | custom-call | flops 4000000000 | bytes 1048576 | tf_op jit(solution)/shard_map/backward0/pallas_call | solution.py:573
  35.5 2.2 %collective-permute-done.8.came_ref = bf16[3,6,8,128]{3,2,1,0:T(8,128)(2,1)S(1)} collective-permute-done((bf16[3,6,8,128]{3,2,1,0:T(8,128)(2,1)S(1)}, bf16[3,6,8,128]{3,2,1,0:T(8,128)(2,1)S(1)}, u32[]{:S(2)}, u32[]{:S(2)}) %collective-permute-start.8) | collective-permute-done | bytes 36896 | tf_op jit(solution)/shard_map/ppermute | solution.py:541
  37.6 0.3 merge3.1
  37.9 1.6 %collective-permute-start.10 = (bf16[2,2,1536]{2,1,0:T(2,128)(2,1)S(1)}, bf16[2,2,1536]{2,1,0:T(2,128)(2,1)S(1)}, u32[]{:S(2)}, u32[]{:S(2)}) collective-permute-start(bf16[2,2,1536]{2,1,0:T(2,128)(2,1)S(1)} %get-tuple-element.58), channel_id=1, source_target_pairs={{0,16},{16,0},{1,17},{17,1},{2,18},{18,2},{3,19},{19,3},{4,20},{20... | collective-permute-start | bytes 36872 | tf_op jit(solution)/shard_map/ppermute | solution.py:570
  39.5 2.3 %backward1.1 = (bf16[1024,1536]{1,0:T(8,128)(2,1)}, bf16[1024,1536]{1,0:T(8,128)(2,1)}) custom-call(f32[24,128]{1,0:T(8,128)S(1)} %get-tuple-element.50.stat_ref, f32[24,128]{1,0:T(8,128)S(1)} %statistics3.1.stat_all_ref, bf16[6,128,256]{2,1,0:T(8,128)(2,1)S(1)} %get-tuple-element.61.qb_ref, ...), custom_call_target="tpu_custom_call", output_to_operand_aliasing={{0}: (5, {}), {1}: (6, {})} | custom-call | flops 4000000000 | bytes 1048576 | tf_op jit(solution)/shard_map/backward1/pallas_call | solution.py:573
  41.8 0.0 collective-permute-done.10.back_ref
  41.8 0.6 %gather.1 = (bf16[2,3072]{1,0:T(2,128)(2,1)}, bf16[2,3072]{1,0:T(2,128)(2,1)}) custom-call(bf16[2,2,1536]{2,1,0:T(2,128)(2,1)S(1)} %get-tuple-element.57.own_ref, bf16[2,2,1536]{2,1,0:T(2,128)(2,1)S(1)} %collective-permute-done.10.back_ref), custom_call_target="tpu_custom_call" | custom-call | flops 1000000000 | bytes 1048576 | tf_op jit(solution)/shard_map/gather/pallas_call | solution.py:471
  (5 shorter events, 0.1 us)
Async XLA Ops:
  1.6 6.8 %collective-permute-start.1 = (bf16[32,1536]{1,0:T(8,128)(2,1)S(1)}, bf16[32,1536]{1,0:T(8,128)(2,1)S(1)}, u32[]{:S(2)}, u32[]{:S(2)}) collective-permute-start(bf16[32,1536]{1,0:T(8,128)(2,1)S(1)} %get-tuple-element.41), channel_id=1, source_target_pairs={{0,16},{16,0},{1,17},{17,1},{2,18},{18,2},{3,19},{19,3},{4,20},{20... | collective-permute-start | bytes 294920 | tf_op jit(solution)/shard_map/ppermute | solution.py:449
  4.7 5.8 %collective-permute-start = (bf16[32,1536]{1,0:T(8,128)(2,1)S(1)}, bf16[32,1536]{1,0:T(8,128)(2,1)S(1)}, u32[]{:S(2)}, u32[]{:S(2)}) collective-permute-start(bf16[32,1536]{1,0:T(8,128)(2,1)S(1)} %get-tuple-element.37), channel_id=1, source_target_pairs={{0,16},{16,0},{1,17},{17,1},{2,18},{18,2},{3,19},{19,3},{4,20},{20... | collective-permute-start | bytes 294920 | tf_op jit(solution)/shard_map/ppermute | solution.py:450
  13.2 1.7 %collective-permute-start.2 = (bf16[3,12,32,128]{3,2,1,0:T(8,128)(2,1)S(1)}, bf16[3,12,32,128]{3,2,1,0:T(8,128)(2,1)S(1)}, u32[]{:S(2)}, u32[]{:S(2)}) collective-permute-start(bf16[3,12,32,128]{3,2,1,0:T(8,128)(2,1)S(1)} %get-tuple-element.49), channel_id=1, source_target_pairs={{0,1},{1,0},{2,3},{3,2},{4,5},{5,4},{6,7},{7,6},{8,9},{9,8},{10,11... | collective-permute-start | bytes 884744 | tf_op jit(solution)/shard_map/ppermute | solution.py:541
  13.3 1.6 %collective-permute-start.3 = (f32[24,128]{1,0:T(8,128)S(1)}, f32[24,128]{1,0:T(8,128)S(1)}, u32[]{:S(2)}, u32[]{:S(2)}) collective-permute-start(f32[24,128]{1,0:T(8,128)S(1)} %get-tuple-element.50.stat_ref), channel_id=1, source_target_pairs={{0,1},{1,0},{2,3},{3,2},{4,5},{5,4},{6,7},{7,6},{8,9},{9,8},{10,11... | collective-permute-start | bytes 36872 | tf_op jit(solution)/shard_map/ppermute | solution.py:540
  15.4 12.2 %collective-permute-start.4 = (bf16[3,12,16,128]{3,2,1,0:T(8,128)(2,1)S(1)}, bf16[3,12,16,128]{3,2,1,0:T(8,128)(2,1)S(1)}, u32[]{:S(2)}, u32[]{:S(2)}) collective-permute-start(bf16[3,12,16,128]{3,2,1,0:T(8,128)(2,1)S(1)} %get-tuple-element.52), channel_id=1, source_target_pairs={{0,2},{1,5},{2,0},{3,7},{4,6},{5,1},{6,4},{7,3},{8,10},{9,13},{10,... | collective-permute-start | bytes 442376 | tf_op jit(solution)/shard_map/ppermute | solution.py:541
  17.4 3.8 %collective-permute-start.5 = (f32[24,128]{1,0:T(8,128)S(1)}, f32[24,128]{1,0:T(8,128)S(1)}, u32[]{:S(2)}, u32[]{:S(2)}) collective-permute-start(f32[24,128]{1,0:T(8,128)S(1)} %statistics0.1.stat_ref), channel_id=1, source_target_pairs={{0,2},{1,5},{2,0},{3,7},{4,6},{5,1},{6,4},{7,3},{8,10},{9,13},{10,... | collective-permute-start | bytes 36872 | tf_op jit(solution)/shard_map/ppermute | solution.py:540
  21.2 3.8 %collective-permute-start.7 = (f32[24,128]{1,0:T(8,128)S(1)}, f32[24,128]{1,0:T(8,128)S(1)}, u32[]{:S(2)}, u32[]{:S(2)}) collective-permute-start(f32[24,128]{1,0:T(8,128)S(1)} %statistics1.1.stat_ref), channel_id=1, source_target_pairs={{0,4},{1,3},{2,6},{3,1},{4,0},{5,7},{6,2},{7,5},{8,12},{9,11},{10,... | collective-permute-start | bytes 36872 | tf_op jit(solution)/shard_map/ppermute | solution.py:540
  24.9 5.6 %collective-permute-start.9 = (f32[24,128]{1,0:T(8,128)S(1)}, f32[24,128]{1,0:T(8,128)S(1)}, u32[]{:S(2)}, u32[]{:S(2)}) collective-permute-start(f32[24,128]{1,0:T(8,128)S(1)} %statistics2.1.stat_ref), channel_id=1, source_target_pairs={{0,8},{1,9},{2,10},{3,11},{4,12},{5,13},{6,14},{7,15},{8,0},{9,1},... | collective-permute-start | bytes 36872 | tf_op jit(solution)/shard_map/ppermute | solution.py:540
  28.0 4.4 %collective-permute-start.6 = (bf16[3,12,8,128]{3,2,1,0:T(8,128)(2,1)S(1)}, bf16[3,12,8,128]{3,2,1,0:T(8,128)(2,1)S(1)}, u32[]{:S(2)}, u32[]{:S(2)}) collective-permute-start(bf16[3,12,8,128]{3,2,1,0:T(8,128)(2,1)S(1)} %get-tuple-element.54), channel_id=1, source_target_pairs={{0,4},{1,3},{2,6},{3,1},{4,0},{5,7},{6,2},{7,5},{8,12},{9,11},{10,... | collective-permute-start | bytes 221192 | tf_op jit(solution)/shard_map/ppermute | solution.py:541
  32.7 4.9 %collective-permute-start.8 = (bf16[3,6,8,128]{3,2,1,0:T(8,128)(2,1)S(1)}, bf16[3,6,8,128]{3,2,1,0:T(8,128)(2,1)S(1)}, u32[]{:S(2)}, u32[]{:S(2)}) collective-permute-start(bf16[3,6,8,128]{3,2,1,0:T(8,128)(2,1)S(1)} %get-tuple-element.56), channel_id=1, source_target_pairs={{0,8},{1,9},{2,10},{3,11},{4,12},{5,13},{6,14},{7,15},{8,0},{9,1},... | collective-permute-start | bytes 110600 | tf_op jit(solution)/shard_map/ppermute | solution.py:541
  37.9 3.9 %collective-permute-start.10 = (bf16[2,2,1536]{2,1,0:T(2,128)(2,1)S(1)}, bf16[2,2,1536]{2,1,0:T(2,128)(2,1)S(1)}, u32[]{:S(2)}, u32[]{:S(2)}) collective-permute-start(bf16[2,2,1536]{2,1,0:T(2,128)(2,1)S(1)} %get-tuple-element.58), channel_id=1, source_target_pairs={{0,16},{16,0},{1,17},{17,1},{2,18},{18,2},{3,19},{19,3},{4,20},{20... | collective-permute-start | bytes 36872 | tf_op jit(solution)/shard_map/ppermute | solution.py:570

commit v6 on v5

--- a/solution.py
+++ b/solution.py
@@ -12,6 +12,7 @@
 F32 = jnp.float32
 BF16 = jnp.bfloat16
 MIB = 1024 * 1024
+LOG2_E = math.log2(math.e)
 VMEM = pl.BlockSpec(memory_space=pltpu.VMEM)
 HBM = pl.BlockSpec(memory_space=pltpu.HBM)
 
@@ -42,6 +43,7 @@
         self.heads = level_bias.shape[1] // self.query_ways
         self.head_size = self.features // self.heads
         self.scale = 1.0 / math.sqrt(self.head_size)
+        self.log2_scale = self.scale * LOG2_E
         self.own_rows = query_states.shape[0]
         self.rows = self.own_rows * self.query_ways
         self.part_rows = self.own_rows // self.owner_ways
@@ -161,7 +163,7 @@
 
 def mask_body(live_ref, term_ref, masked_ref):
     slot = lax.broadcasted_iota(jnp.int32, term_ref.shape, 1)
-    masked_ref[...] = jnp.where(slot < live_ref[0], term_ref[...], -1e30)
+    masked_ref[...] = jnp.where(slot < live_ref[0], term_ref[...] * LOG2_E, -1e30)
 
 
 def row_order(plan):
@@ -230,7 +232,7 @@
 def attend_body(plan, pairwise, *refs):
     own_ref = refs[0] if pairwise else None
     refs = refs[1:] if pairwise else refs
-    moved_ref, kt_ref, v_ref, term_ref, e_ref, eb_ref, out_ref, columns, block_ref, source, scores = refs
+    moved_ref, kt_ref, v_ref, term_ref, eb_ref, out_ref, columns, block_ref, source, scores = refs
     place_rows(plan, own_ref, moved_ref, block_ref, source)
     rows, size, group = plan.rows, plan.head_size, plan.group
     width = group * size
@@ -241,10 +243,9 @@
 
     def chunk(p, r):
         h = p * group + r // rows
-        s = scores[p % 2, r : r + STEP] * plan.scale + term_ref[h : h + 1, :]
+        s = scores[p % 2, r : r + STEP] * plan.log2_scale + term_ref[h : h + 1, :]
         top = jnp.max(s, axis=1, keepdims=True)
-        e = jnp.exp(s - top)
-        e_ref[p, r : r + STEP, :] = e
+        e = jnp.exp2(s - top)
         eb_ref[p, r : r + STEP, :] = e.astype(BF16)
         columns[r : r + STEP, p : p + 1] = top
         columns[r : r + STEP, 8 + p : 9 + p] = jnp.sum(e, axis=1, keepdims=True)
@@ -261,8 +262,8 @@
 def differ_body(plan, pairwise, *refs):
     own_ref = refs[0] if pairwise else None
     refs = refs[1:] if pairwise else refs
-    moved_ref, k_ref, vt_ref, e_ref, eb_ref, out_ref, columns_ref = refs[:7]
-    part_ref, send_ref, stat_ref, yb_ref, block_ref, source, dprobs, columns = refs[7:]
+    moved_ref, k_ref, vt_ref, eb_ref, out_ref, columns_ref = refs[:6]
+    part_ref, send_ref, stat_ref, yb_ref, block_ref, source, dprobs, columns = refs[6:]
     place_rows(plan, own_ref, moved_ref, block_ref, source)
     rows, size, group = plan.rows, plan.head_size, plan.group
     width = group * size
@@ -273,7 +274,7 @@
         dprobs[p % 2, :, j : j + TILE] = nt(block_ref[p], vt_ref[j : j + TILE, p * width : (p + 1) * width])
 
     def chunk(p, r):
-        e = e_ref[p, r : r + STEP, :]
+        e = eb_ref[p, r : r + STEP, :].astype(F32)
         d = dprobs[p % 2, r : r + STEP]
         total = columns_ref[r : r + STEP, 8 + p : 9 + p]
         mean = jnp.sum(e * d, axis=1, keepdims=True) / total
@@ -297,8 +298,8 @@
     top1, total1, mean1 = (stat_ref[8 * t : 8 * t + 8] for t in range(3))
     top2, total2, mean2 = (stat_came_ref[8 * t : 8 * t + 8] for t in range(3))
     top = jnp.maximum(top1, top2)
-    f1 = jnp.exp(top1 - top)
-    f2 = jnp.exp(top2 - top)
+    f1 = jnp.exp2(top1 - top)
+    f2 = jnp.exp2(top2 - top)
     total = f1 * total1 + f2 * total2
     inverse = 1.0 / jnp.where(total > 0.0, total, 1.0)
     w1 = f1 * total1 * inverse
@@ -403,7 +404,7 @@
     width = dk.shape[2]
     total = stat_all_ref[8:16]
     inverse = 1.0 / jnp.where(total > 0.0, total, 1.0)
-    f = jnp.exp(stat_ref[0:8] - stat_all_ref[0:8]) * inverse
+    f = jnp.exp2(stat_ref[0:8] - stat_all_ref[0:8]) * inverse
     c = f * (stat_ref[16:24] - stat_all_ref[16:24])
     rest = jnp.zeros((128 - 24, lanes), F32)
     table[...] = jnp.concatenate([f, f * plan.scale, c * plan.scale, rest], axis=0).T
@@ -508,11 +509,10 @@
         name="mask",
     )(live_counts, term)
     own_queries, own_grads = ([own[0]], [own[1]]) if pairwise else ([], [])
-    e, eb, out, columns, qb = kernel(
+    eb, out, columns, qb = kernel(
         "attend",
         functools.partial(attend_body, plan, pairwise),
         (
-            square_shape(F32),
             square_shape(BF16),
             jax.ShapeDtypeStruct((heads, plan.rows, size), F32),
             columns_shape,
@@ -526,7 +526,7 @@
         "differ",
         functools.partial(differ_body, plan, pairwise),
         (part_shape(0), send_shape(0), stat_shape, square_shape(BF16), block_shape),
-        (*own_grads, moved_grads, keys, values, e, eb, out, columns),
+        (*own_grads, moved_grads, keys, values, eb, out, columns),
         [source_scratch, square_scratch, pltpu.VMEM((lanes, 128), F32)],
         vmem_mib=6,
     )

time: 42.7 us -> 42.5 us (level)
  no operation moved by 1% of the time
where the time goes in v6:
time: 42.5 us; the launch traced here: 42.3 us
  Pallas kernels  16.2 us (38%)
  starting transfers between devices  13.8 us (32%)
  waiting for transfers between devices  10.8 us (25%)
  between operations  1.4 us (3%)
    ppermute x4, waiting for transfers between devices, local(): stat_came = lax.ppermute(stat, 'ctx', swap)  6.72 us
    pallas_call x4, Pallas kernels, kernel(): call(body, outs, vmem_mib, flops, in_specs=[VMEM] * len(ins), out_specs=V...  6.12 us
    ppermute x4, starting transfers between devices, local(): stat_came = lax.ppermute(stat, 'ctx', swap)  5.07 us
    pallas_call x2, Pallas kernels, gradients(): call(functools.partial(backward_body, plan, first, count), (context_shape...  4.7 us
    ppermute x4, waiting for transfers between devices, local(): came = lax.ppermute(send, 'ctx', swap)  4.09 us
    ppermute x4, starting transfers between devices, local(): came = lax.ppermute(send, 'ctx', swap)  4.03 us
    ppermute x1, starting transfers between devices, local(): moved_queries = lax.ppermute(their_queries, 'query', [(0, 1), (1, 0)])  3.06 us
    pallas_call x1, Pallas kernels, local(): call(functools.partial(load_body, plan, pairwise), [context_shape] * 2 +...  2.94 us
  transfers between devices with their start and end apart: 11, of which 5 were waited for; matrix products, arithmetic and copies ran while one was open for 0% of the time, Pallas kernels for 26%

profile of v6, /device:TPU:0, one launch (start us, length us, event | category | flops | bytes accessed | tf_op | source)
XLA Modules:
  0.0 42.3 jit_solution(16384883751150387042)
XLA Ops:
  0.6 1.0 %cut.1 = (bf16[32,1536]{1,0:T(8,128)(2,1)S(1)}, bf16[32,1536]{1,0:T(8,128)(2,1)S(1)}) custom-call(bf16[32,3072]{1,0:T(8,128)(2,1)} %q_ref.1, bf16[32,3072]{1,0:T(8,128)(2,1)} %g_ref.1), custom_call_target="tpu_custom_call" | custom-call | flops 1000000 | bytes 1048576 | tf_op jit(solution)/shard_map/cut/pallas_call | solution.py:440
  1.6 3.1 %collective-permute-start.1 = (bf16[32,1536]{1,0:T(8,128)(2,1)S(1)}, bf16[32,1536]{1,0:T(8,128)(2,1)S(1)}, u32[]{:S(2)}, u32[]{:S(2)}) collective-permute-start(bf16[32,1536]{1,0:T(8,128)(2,1)S(1)} %get-tuple-element.40), channel_id=1, source_target_pairs={{0,16},{16,0},{1,17},{17,1},{2,18},{18,2},{3,19},{19,3},{4,20},{20... | collective-permute-start | bytes 294920 | tf_op jit(solution)/shard_map/ppermute | solution.py:450
  4.7 0.1 collective-permute-start
  4.7 2.9 %load.1 = (bf16[1024,1536]{1,0:T(8,128)(2,1)S(1)}, bf16[1024,1536]{1,0:T(8,128)(2,1)S(1)}, bf16[1536,1024]{1,0:T(8,128)(2,1)S(1)}, bf16[32,1536]{1,0:T(8,128)(2,...) custom-call(s32[1,1024]{1,0:T(1,128)} %bitcast.1, f32[5,24]{1,0:T(8,128)} %refs_1_.1, ...), custom_call_target="tpu_custom_call" | custom-call | flops 1000000000 | bytes 1048576 | tf_op jit(solution)/shard_map/load/pallas_call | solution.py:488
  8.4 0.0 collective-permute-done.1.refs_1_
  8.4 1.9 %attend.1 = (bf16[6,128,1024]{2,1,0:T(8,128)(2,1)S(1)}, f32[12,64,128]{2,1,0:T(8,128)S(1)}, f32[128,128]{1,0:T(8,128)S(1)}, bf16[6,128,256]{2,1,0:T(8,128)(2,1)S(1)}) custom-call(bf16[32,1536]{1,0:T(8,128)(2,1)S(1)} %get-tuple-element.39.refs_0_, bf16[32,1536]{1,0:T(8,128)(2,1)S(1)} %collective-permute-done.1.refs_1_, ...), custom_call_target="tpu_custom_call" | custom-call | flops 1000000000 | bytes 1048576 | tf_op jit(solution)/shard_map/attend/pallas_call | solution.py:472
  10.3 0.0 collective-permute-done.refs_1_
  10.3 2.8 %differ.1 = (f32[3,12,64,128]{3,2,1,0:T(8,128)S(1)}, bf16[3,12,32,128]{3,2,1,0:T(8,128)(2,1)S(1)}, f32[24,128]{1,0:T(8,128)S(1)}, bf16[6,128,1024]{2,1,0:T(8,128)(2,1)S(1)}, bf16[6,128,256]{2,1,0:T(8,128)(2,1)S(1)}) custom-call(bf16[32,1536]{1,0:T(8,128)(2,1)S(1)} %get-tuple-element.35.refs_0_, bf16[32,1536]{1,0:T(8,128)(2,1)S(1)} %collective-permute-done.refs_1_, ...), custom_call_target="tpu_custom_call" | custom-call | flops 1000000000 | bytes 1048576 | tf_op jit(solution)/shard_map/differ/pallas_call | solution.py:472
  13.0 0.1 collective-permute-start.2
  13.1 0.5 %collective-permute-start.3 = (f32[24,128]{1,0:T(8,128)S(1)}, f32[24,128]{1,0:T(8,128)S(1)}, u32[]{:S(2)}, u32[]{:S(2)}) collective-permute-start(f32[24,128]{1,0:T(8,128)S(1)} %get-tuple-element.48.stat_ref), channel_id=1, source_target_pairs={{0,1},{1,0},{2,3},{3,2},{4,5},{5,4},{6,7},{7,6},{8,9},{9,8},{10,11... | collective-permute-start | bytes 36872 | tf_op jit(solution)/shard_map/ppermute | solution.py:540
  13.6 1.1 %collective-permute-done.3.stat_came_ref = f32[24,128]{1,0:T(8,128)S(1)} collective-permute-done((f32[24,128]{1,0:T(8,128)S(1)}, f32[24,128]{1,0:T(8,128)S(1)}, u32[]{:S(2)}, u32[]{:S(2)}) %collective-permute-start.3) | collective-permute-done | bytes 12320 | tf_op jit(solution)/shard_map/ppermute | solution.py:540
  14.7 0.0 collective-permute-done.2.came_ref
  14.7 0.5 %merge0.1 = (f32[3,12,32,128]{3,2,1,0:T(8,128)S(1)}, bf16[3,12,16,128]{3,2,1,0:T(8,128)(2,1)S(1)}) custom-call(f32[3,12,64,128]{3,2,1,0:T(8,128)S(1)} %get-tuple-element.46.part_ref, bf16[3,12,32,128]{3,2,1,0:T(8,128)(2,1)S(1)} %collective-permute-done.2.came_ref, f32[24,128]{1,0:T(8,128)S(1)} %get-tuple-element.48.stat_ref, ...), custom_call_target="tpu_custom_call" | custom-call | flops 100000000 | bytes 1048576 | tf_op jit(solution)/shard_map/merge0/pallas_call | solution.py:557
  15.2 2.0 %collective-permute-start.4 = (bf16[3,12,16,128]{3,2,1,0:T(8,128)(2,1)S(1)}, bf16[3,12,16,128]{3,2,1,0:T(8,128)(2,1)S(1)}, u32[]{:S(2)}, u32[]{:S(2)}) collective-permute-start(bf16[3,12,16,128]{3,2,1,0:T(8,128)(2,1)S(1)} %get-tuple-element.50), channel_id=1, source_target_pairs={{0,2},{1,5},{2,0},{3,7},{4,6},{5,1},{6,4},{7,3},{8,10},{9,13},{10,... | collective-permute-start | bytes 442376 | tf_op jit(solution)/shard_map/ppermute | solution.py:541
  17.2 0.2 collective-permute-start.5
  17.4 3.6 %collective-permute-done.5.stat_came_ref = f32[24,128]{1,0:T(8,128)S(1)} collective-permute-done((f32[24,128]{1,0:T(8,128)S(1)}, f32[24,128]{1,0:T(8,128)S(1)}, u32[]{:S(2)}, u32[]{:S(2)}) %collective-permute-start.5) | collective-permute-done | bytes 12320 | tf_op jit(solution)/shard_map/ppermute | solution.py:540
  21.0 1.7 %collective-permute-start.7 = (f32[24,128]{1,0:T(8,128)S(1)}, f32[24,128]{1,0:T(8,128)S(1)}, u32[]{:S(2)}, u32[]{:S(2)}) collective-permute-start(f32[24,128]{1,0:T(8,128)S(1)} %statistics1.1.stat_ref), channel_id=1, source_target_pairs={{0,4},{1,3},{2,6},{3,1},{4,0},{5,7},{6,2},{7,5},{8,12},{9,11},{10,... | collective-permute-start | bytes 36872 | tf_op jit(solution)/shard_map/ppermute | solution.py:540
  22.7 2.1 %collective-permute-done.7.stat_came_ref = f32[24,128]{1,0:T(8,128)S(1)} collective-permute-done((f32[24,128]{1,0:T(8,128)S(1)}, f32[24,128]{1,0:T(8,128)S(1)}, u32[]{:S(2)}, u32[]{:S(2)}) %collective-permute-start.7) | collective-permute-done | bytes 12320 | tf_op jit(solution)/shard_map/ppermute | solution.py:540
  24.7 2.7 %collective-permute-start.9 = (f32[24,128]{1,0:T(8,128)S(1)}, f32[24,128]{1,0:T(8,128)S(1)}, u32[]{:S(2)}, u32[]{:S(2)}) collective-permute-start(f32[24,128]{1,0:T(8,128)S(1)} %statistics2.1.stat_ref), channel_id=1, source_target_pairs={{0,8},{1,9},{2,10},{3,11},{4,12},{5,13},{6,14},{7,15},{8,0},{9,1},... | collective-permute-start | bytes 36872 | tf_op jit(solution)/shard_map/ppermute | solution.py:540
  27.4 0.0 collective-permute-done.4.came_ref
  27.4 0.4 merge1.1
  27.8 1.6 %collective-permute-start.6 = (bf16[3,12,8,128]{3,2,1,0:T(8,128)(2,1)S(1)}, bf16[3,12,8,128]{3,2,1,0:T(8,128)(2,1)S(1)}, u32[]{:S(2)}, u32[]{:S(2)}) collective-permute-start(bf16[3,12,8,128]{3,2,1,0:T(8,128)(2,1)S(1)} %get-tuple-element.52), channel_id=1, source_target_pairs={{0,4},{1,3},{2,6},{3,1},{4,0},{5,7},{6,2},{7,5},{8,12},{9,11},{10,... | collective-permute-start | bytes 221192 | tf_op jit(solution)/shard_map/ppermute | solution.py:541
  29.4 0.9 %turn.1.turned_ref = bf16[6,1024,256]{2,1,0:T(8,128)(2,1)S(1)} custom-call(bf16[6,128,1024]{2,1,0:T(8,128)(2,1)S(1)} %get-tuple-element.43.refs_4_.eb_ref, bf16[6,128,1024]{2,1,0:T(8,128)(2,1)S(1)} %get-tuple-element.61.yb_ref), custom_call_target="tpu_custom_call" | custom-call | flops 1000000000 | bytes 1048576 | tf_op jit(solution)/shard_map/turn/pallas_call | solution.py:472
  30.3 0.0 collective-permute-done.9.stat_came_ref
  30.3 1.9 %collective-permute-done.6.came_ref = bf16[3,12,8,128]{3,2,1,0:T(8,128)(2,1)S(1)} collective-permute-done((bf16[3,12,8,128]{3,2,1,0:T(8,128)(2,1)S(1)}, bf16[3,12,8,128]{3,2,1,0:T(8,128)(2,1)S(1)}, u32[]{:S(2)}, u32[]{:S(2)}) %collective-permute-start.6) | collective-permute-done | bytes 73760 | tf_op jit(solution)/shard_map/ppermute | solution.py:541
  32.2 0.3 merge2.1
  32.5 0.4 collective-permute-start.8
  32.9 2.4 %backward0.1 = (bf16[1024,1536]{1,0:T(8,128)(2,1)}, bf16[1024,1536]{1,0:T(8,128)(2,1)}) custom-call(f32[24,128]{1,0:T(8,128)S(1)} %get-tuple-element.48.stat_ref, f32[24,128]{1,0:T(8,128)S(1)} %statistics3.1.stat_all_ref, bf16[6,128,256]{2,1,0:T(8,128)(2,1)S(1)} %get-tuple-element.59.qb_ref, bf16[6,128,256]{2,1,0:T(8,128)(2,1)S(1)} %get-tuple-element.60.gb_ref, ...), custom_call_target="tpu_custom_call" | custom-call | flops 4000000000 | bytes 1048576 | tf_op jit(solution)/shard_map/backward0/pallas_call | solution.py:573
  35.2 2.2 %collective-permute-done.8.came_ref = bf16[3,6,8,128]{3,2,1,0:T(8,128)(2,1)S(1)} collective-permute-done((bf16[3,6,8,128]{3,2,1,0:T(8,128)(2,1)S(1)}, bf16[3,6,8,128]{3,2,1,0:T(8,128)(2,1)S(1)}, u32[]{:S(2)}, u32[]{:S(2)}) %collective-permute-start.8) | collective-permute-done | bytes 36896 | tf_op jit(solution)/shard_map/ppermute | solution.py:541
  37.4 0.3 merge3.1
  37.7 1.6 %collective-permute-start.10 = (bf16[2,2,1536]{2,1,0:T(2,128)(2,1)S(1)}, bf16[2,2,1536]{2,1,0:T(2,128)(2,1)S(1)}, u32[]{:S(2)}, u32[]{:S(2)}) collective-permute-start(bf16[2,2,1536]{2,1,0:T(2,128)(2,1)S(1)} %get-tuple-element.56), channel_id=1, source_target_pairs={{0,16},{16,0},{1,17},{17,1},{2,18},{18,2},{3,19},{19,3},{4,20},{20... | collective-permute-start | bytes 36872 | tf_op jit(solution)/shard_map/ppermute | solution.py:570
  39.3 2.3 %backward1.1 = (bf16[1024,1536]{1,0:T(8,128)(2,1)}, bf16[1024,1536]{1,0:T(8,128)(2,1)}) custom-call(f32[24,128]{1,0:T(8,128)S(1)} %get-tuple-element.48.stat_ref, f32[24,128]{1,0:T(8,128)S(1)} %statistics3.1.stat_all_ref, bf16[6,128,256]{2,1,0:T(8,128)(2,1)S(1)} %get-tuple-element.59.qb_ref, ...), custom_call_target="tpu_custom_call", output_to_operand_aliasing={{0}: (5, {}), {1}: (6, {})} | custom-call | flops 4000000000 | bytes 1048576 | tf_op jit(solution)/shard_map/backward1/pallas_call | solution.py:573
  41.6 0.0 collective-permute-done.10.back_ref
  41.6 0.6 %gather.1 = (bf16[2,3072]{1,0:T(2,128)(2,1)}, bf16[2,3072]{1,0:T(2,128)(2,1)}) custom-call(bf16[2,2,1536]{2,1,0:T(2,128)(2,1)S(1)} %get-tuple-element.55.own_ref, bf16[2,2,1536]{2,1,0:T(2,128)(2,1)S(1)} %collective-permute-done.10.back_ref), custom_call_target="tpu_custom_call" | custom-call | flops 1000000000 | bytes 1048576 | tf_op jit(solution)/shard_map/gather/pallas_call | solution.py:472
  (5 shorter events, 0.1 us)
Async XLA Ops:
  1.6 6.8 %collective-permute-start.1 = (bf16[32,1536]{1,0:T(8,128)(2,1)S(1)}, bf16[32,1536]{1,0:T(8,128)(2,1)S(1)}, u32[]{:S(2)}, u32[]{:S(2)}) collective-permute-start(bf16[32,1536]{1,0:T(8,128)(2,1)S(1)} %get-tuple-element.40), channel_id=1, source_target_pairs={{0,16},{16,0},{1,17},{17,1},{2,18},{18,2},{3,19},{19,3},{4,20},{20... | collective-permute-start | bytes 294920 | tf_op jit(solution)/shard_map/ppermute | solution.py:450
  4.7 5.6 %collective-permute-start = (bf16[32,1536]{1,0:T(8,128)(2,1)S(1)}, bf16[32,1536]{1,0:T(8,128)(2,1)S(1)}, u32[]{:S(2)}, u32[]{:S(2)}) collective-permute-start(bf16[32,1536]{1,0:T(8,128)(2,1)S(1)} %get-tuple-element.36), channel_id=1, source_target_pairs={{0,16},{16,0},{1,17},{17,1},{2,18},{18,2},{3,19},{19,3},{4,20},{20... | collective-permute-start | bytes 294920 | tf_op jit(solution)/shard_map/ppermute | solution.py:451
  13.0 1.7 %collective-permute-start.2 = (bf16[3,12,32,128]{3,2,1,0:T(8,128)(2,1)S(1)}, bf16[3,12,32,128]{3,2,1,0:T(8,128)(2,1)S(1)}, u32[]{:S(2)}, u32[]{:S(2)}) collective-permute-start(bf16[3,12,32,128]{3,2,1,0:T(8,128)(2,1)S(1)} %get-tuple-element.47), channel_id=1, source_target_pairs={{0,1},{1,0},{2,3},{3,2},{4,5},{5,4},{6,7},{7,6},{8,9},{9,8},{10,11... | collective-permute-start | bytes 884744 | tf_op jit(solution)/shard_map/ppermute | solution.py:541
  13.1 1.6 %collective-permute-start.3 = (f32[24,128]{1,0:T(8,128)S(1)}, f32[24,128]{1,0:T(8,128)S(1)}, u32[]{:S(2)}, u32[]{:S(2)}) collective-permute-start(f32[24,128]{1,0:T(8,128)S(1)} %get-tuple-element.48.stat_ref), channel_id=1, source_target_pairs={{0,1},{1,0},{2,3},{3,2},{4,5},{5,4},{6,7},{7,6},{8,9},{9,8},{10,11... | collective-permute-start | bytes 36872 | tf_op jit(solution)/shard_map/ppermute | solution.py:540
  15.2 12.2 %collective-permute-start.4 = (bf16[3,12,16,128]{3,2,1,0:T(8,128)(2,1)S(1)}, bf16[3,12,16,128]{3,2,1,0:T(8,128)(2,1)S(1)}, u32[]{:S(2)}, u32[]{:S(2)}) collective-permute-start(bf16[3,12,16,128]{3,2,1,0:T(8,128)(2,1)S(1)} %get-tuple-element.50), channel_id=1, source_target_pairs={{0,2},{1,5},{2,0},{3,7},{4,6},{5,1},{6,4},{7,3},{8,10},{9,13},{10,... | collective-permute-start | bytes 442376 | tf_op jit(solution)/shard_map/ppermute | solution.py:541
  17.2 3.8 %collective-permute-start.5 = (f32[24,128]{1,0:T(8,128)S(1)}, f32[24,128]{1,0:T(8,128)S(1)}, u32[]{:S(2)}, u32[]{:S(2)}) collective-permute-start(f32[24,128]{1,0:T(8,128)S(1)} %statistics0.1.stat_ref), channel_id=1, source_target_pairs={{0,2},{1,5},{2,0},{3,7},{4,6},{5,1},{6,4},{7,3},{8,10},{9,13},{10,... | collective-permute-start | bytes 36872 | tf_op jit(solution)/shard_map/ppermute | solution.py:540
  21.0 3.8 %collective-permute-start.7 = (f32[24,128]{1,0:T(8,128)S(1)}, f32[24,128]{1,0:T(8,128)S(1)}, u32[]{:S(2)}, u32[]{:S(2)}) collective-permute-start(f32[24,128]{1,0:T(8,128)S(1)} %statistics1.1.stat_ref), channel_id=1, source_target_pairs={{0,4},{1,3},{2,6},{3,1},{4,0},{5,7},{6,2},{7,5},{8,12},{9,11},{10,... | collective-permute-start | bytes 36872 | tf_op jit(solution)/shard_map/ppermute | solution.py:540
  24.7 5.6 %collective-permute-start.9 = (f32[24,128]{1,0:T(8,128)S(1)}, f32[24,128]{1,0:T(8,128)S(1)}, u32[]{:S(2)}, u32[]{:S(2)}) collective-permute-start(f32[24,128]{1,0:T(8,128)S(1)} %statistics2.1.stat_ref), channel_id=1, source_target_pairs={{0,8},{1,9},{2,10},{3,11},{4,12},{5,13},{6,14},{7,15},{8,0},{9,1},... | collective-permute-start | bytes 36872 | tf_op jit(solution)/shard_map/ppermute | solution.py:540
  27.8 4.4 %collective-permute-start.6 = (bf16[3,12,8,128]{3,2,1,0:T(8,128)(2,1)S(1)}, bf16[3,12,8,128]{3,2,1,0:T(8,128)(2,1)S(1)}, u32[]{:S(2)}, u32[]{:S(2)}) collective-permute-start(bf16[3,12,8,128]{3,2,1,0:T(8,128)(2,1)S(1)} %get-tuple-element.52), channel_id=1, source_target_pairs={{0,4},{1,3},{2,6},{3,1},{4,0},{5,7},{6,2},{7,5},{8,12},{9,11},{10,... | collective-permute-start | bytes 221192 | tf_op jit(solution)/shard_map/ppermute | solution.py:541
  32.5 4.9 %collective-permute-start.8 = (bf16[3,6,8,128]{3,2,1,0:T(8,128)(2,1)S(1)}, bf16[3,6,8,128]{3,2,1,0:T(8,128)(2,1)S(1)}, u32[]{:S(2)}, u32[]{:S(2)}) collective-permute-start(bf16[3,6,8,128]{3,2,1,0:T(8,128)(2,1)S(1)} %get-tuple-element.54), channel_id=1, source_target_pairs={{0,8},{1,9},{2,10},{3,11},{4,12},{5,13},{6,14},{7,15},{8,0},{9,1},... | collective-permute-start | bytes 110600 | tf_op jit(solution)/shard_map/ppermute | solution.py:541
  37.7 3.9 %collective-permute-start.10 = (bf16[2,2,1536]{2,1,0:T(2,128)(2,1)S(1)}, bf16[2,2,1536]{2,1,0:T(2,128)(2,1)S(1)}, u32[]{:S(2)}, u32[]{:S(2)}) collective-permute-start(bf16[2,2,1536]{2,1,0:T(2,128)(2,1)S(1)} %get-tuple-element.56), channel_id=1, source_target_pairs={{0,16},{16,0},{1,17},{17,1},{2,18},{18,2},{3,19},{19,3},{4,20},{20... | collective-permute-start | bytes 36872 | tf_op jit(solution)/shard_map/ppermute | solution.py:570
